TPU v7x, 32 devices: a whole 2x2x4 slice. The times are simulated.
32 devices in a mesh: blk: 16 (over z, x, core), col: 2 (over y).
Axes of the slice: x: 2, y: 2, z: 4, core: 2. Of those that a mesh axis runs over, the one named last changes fastest.
Arguments:
- features: bfloat16 [4096, 128], P(('blk', 'col')), may hold values from -600 to 600
- tile_vals: bfloat16 [16, 128, 256, 256], P('blk', None, 'col'), may hold values from -8 to 8, as said below
- tile_cols: int32 [16, 128], P('blk'), may hold values from 0 to 15
- tile_count: int32 [16], P('blk'), may hold values from 32 to 128, as said below
- norm_gain: float32 [3, 128], replicated, may hold values from 0.25 to 1.75
Outputs:
- propagated: bfloat16 [4096, 128], P(('blk', 'col'))
Inputs may be any that keep to these rules, and one draw needn't show every extreme that they name: `tile_vals`: adjacency tiles are sparse: most entries are zero. `tile_count`: slots at or past a row block's count hold no tile; some row block has exactly 128 live slots in every draw. `tile_cols`: live slots of one row block may name the same column block more than once; entries of dead slots carry no meaning.
All inputs are finite; a program needn't handle non-finite values.
Results may differ from a plain program's by a relative error of at most 0.0052.
Values may be sent and summed in bfloat16 or wider, within the bound.
No kernel may reach another device: no remote copies, remote signals or barrier semaphores. Data moves between devices by JAX's collectives and lax.ppermute only.
A program may use at most 128 MiB of HBM per device.

v0:
```python
import jax
import jax.numpy as jnp
from jax import lax
from jax.sharding import PartitionSpec as P

epsilon = 1e-05


def shards(features, tile_vals, tile_cols, tile_count, norm_gain):
    tile_set = tile_vals[0]
    col_ids = tile_cols[0]
    slot_total = tile_set.shape[0]
    tile_rows = tile_set.shape[2]
    live_mask = jnp.arange(slot_total, dtype=jnp.int32) < tile_count[0]
    current = features
    for hop_index in range(norm_gain.shape[0]):
        whole = lax.all_gather(current, ("blk", "col"), axis=0, tiled=True)
        blocks = whole.reshape(-1, tile_rows, whole.shape[1])
        picked = jnp.where(live_mask[:, None, None], blocks[col_ids], jnp.zeros((), jnp.bfloat16))
        product = lax.dot_general(
            tile_set, picked, (((0, 2), (0, 1)), ((), ())), preferred_element_type=jnp.float32
        )
        summed = product + current.astype(jnp.float32)
        mean_sq = jnp.mean(summed * summed, axis=1, keepdims=True)
        scaled = summed * lax.rsqrt(mean_sq + epsilon) * norm_gain[hop_index][None, :]
        current = scaled.astype(jnp.bfloat16)
    return current


def solution(mesh):
    placed = (P(("blk", "col"), None), P("blk", None, "col", None), P("blk", None), P("blk"), P())
    return jax.shard_map(
        shards, mesh=mesh, in_specs=placed, out_specs=P(("blk", "col"), None), check_vma=False
    )
```

profile of v0, /device:TPU:0, one launch (start us, length us, event | category | flops | bytes accessed | tf_op | source)
XLA Modules:
  0.0 226.3 jit_solution(1349592682230761613)
XLA Ops:
  6.5 0.0 all-gather.4.cloned.1.call-start
  6.5 0.7 all-gather.4.cloned.1.call-update
  7.3 0.0 all-gather.6.cloned.1.call-start
  7.3 0.9 copy.9
  8.8 0.7 fusion.45
  9.5 0.8 slice_bitcast_fusion
  10.3 56.4 %all-gather.4.cloned.1.call-done = bf16[4096,128]{1,0:T(8,128)(2,1)} async-done(((bf16[128,128]{1,0:T(8,128)(2,1)}), bf16[4096,128]{1,0:T(8,128)(2,1)}) %all-gather.4.cloned.1.call-update) | async-done | bytes 1048592 | tf_op jit(solution)/shard_map/all_gather | solution.py:17
  66.7 7.8 %gather_fusion = bf16[128,256,128]{2,1,0:T(8,128)(2,1)} fusion(bf16[16,256,128]{2,1,0:T(8,128)(2,1)} %bitcast.60, s32[1024]{0:T(1024)S(1)} %pad_clamp_fusion), kind=kCustom, calls=%fused_computation | custom fusion | bytes 16777728 | tf_op jit(solution)/shard_map/gather | solution.py:19
  74.5 10.2 %multiply_reduce_fusion.2 = (f32[128]{0:T(128)S(1)}, f32[128,128]{0,1:T(8,128)S(1)}) fusion(bf16[128,128]{0,1:T(8,128)(2,1)S(1)} %copy.9, bf16[1,128,128,256]{3,2,1,0:T(8,128)(2,1)} %param.6, bf16[128,256,128]{2,1,0:T(8,128)(2,1)} %gather_fusion, pred[128]{0:T(512)(128)(4,1)S(1)} %iota_compare_fusion), kind=kOutput, calls=%fused_computation.29 | convolution fusion | flops 1078001536 | bytes 16876160 | tf_op jit(solution)/shard_map/dot_general | solution.py:20
  84.8 0.7 multiply_convert_fusion.2
  85.5 0.0 all-gather.6.cloned.1.call-update
  85.5 0.2 all-gather.8.cloned.1.call-start
  85.7 47.4 %all-gather.6.cloned.1.call-done = bf16[4096,128]{0,1:T(8,128)(2,1)} async-done(((bf16[128,128]{0,1:T(8,128)(2,1)}), bf16[4096,128]{0,1:T(8,128)(2,1)}) %all-gather.6.cloned.1.call-update) | async-done | bytes 1048592 | tf_op jit(solution)/shard_map/all_gather | solution.py:17
  133.1 1.6 copy.18
  134.7 0.0 copy-start
  134.7 6.6 %gather_fusion.1 = bf16[128,256,128]{2,1,0:T(8,128)(2,1)} fusion(bf16[16,256,128]{2,1,0:T(8,128)(2,1)S(1)} %bitcast.59, s32[1024]{0:T(1024)S(1)} %pad_clamp_fusion), kind=kCustom, calls=%fused_computation.1 | custom fusion | bytes 16777728 | tf_op jit(solution)/shard_map/gather | solution.py:19
  141.3 0.0 copy-done
  141.3 10.2 %multiply_reduce_fusion.1 = (f32[128]{0:T(128)S(1)}, f32[128,128]{0,1:T(8,128)S(1)}) fusion(bf16[128,128]{0,1:T(8,128)(2,1)S(1)} %copy-done, bf16[1,128,128,256]{3,2,1,0:T(8,128)(2,1)} %param.6, bf16[128,256,128]{2,1,0:T(8,128)(2,1)} %gather_fusion.1, pred[128]{0:T(512)(128)(4,1)S(1)} %iota_compare_fusion), kind=kOutput, calls=%fused_computation.27 | convolution fusion | flops 1078001536 | bytes 16876160 | tf_op jit(solution)/shard_map/dot_general | solution.py:20
  151.6 0.7 multiply_convert_fusion.1
  152.3 0.0 all-gather.8.cloned.1.call-update
  152.3 48.2 %all-gather.8.cloned.1.call-done = bf16[4096,128]{0,1:T(8,128)(2,1)} async-done(((bf16[128,128]{0,1:T(8,128)(2,1)}), bf16[4096,128]{0,1:T(8,128)(2,1)}) %all-gather.8.cloned.1.call-update) | async-done | bytes 1048592 | tf_op jit(solution)/shard_map/all_gather | solution.py:17
  200.5 1.6 copy.19
  202.1 0.0 copy-start.1
  202.1 6.6 %gather_fusion.2 = bf16[128,256,128]{2,1,0:T(8,128)(2,1)} fusion(bf16[16,256,128]{2,1,0:T(8,128)(2,1)S(1)} %bitcast.58, s32[1024]{0:T(1024)S(1)} %pad_clamp_fusion), kind=kCustom, calls=%fused_computation.2 | custom fusion | bytes 16777728 | tf_op jit(solution)/shard_map/gather | solution.py:19
  208.7 0.0 copy-done.1
  208.7 10.2 %multiply_reduce_fusion = (f32[128]{0:T(128)S(1)}, f32[128,128]{0,1:T(8,128)S(1)}) fusion(bf16[128,128]{0,1:T(8,128)(2,1)S(1)} %copy-done.1, bf16[1,128,128,256]{3,2,1,0:T(8,128)(2,1)} %param.6, bf16[128,256,128]{2,1,0:T(8,128)(2,1)} %gather_fusion.2, pred[128]{0:T(512)(128)(4,1)S(1)} %iota_compare_fusion), kind=kOutput, calls=%fused_computation.25 | convolution fusion | flops 1078001536 | bytes 16876160 | tf_op jit(solution)/shard_map/dot_general | solution.py:20
  218.9 0.1 multiply_convert_fusion
  219.0 0.7 copy.14
  (5 shorter events, 0.0 us)
Async XLA Ops:
  6.5 60.2 %all-gather.4.cloned.1.call-start = ((), (), s32[]{:S(2)}) async-start(), calls=%async_computation | async-start | bytes 1081344 | tf_op jit(solution)/shard_map/all_gather | solution.py:17
  7.3 125.8 %all-gather.6.cloned.1.call-start = ((), (), s32[]{:S(2)}) async-start(), calls=%async_computation.1 | async-start | bytes 1081344 | tf_op jit(solution)/shard_map/all_gather | solution.py:17
  85.5 115.0 %all-gather.8.cloned.1.call-start = ((), (), s32[]{:S(2)}) async-start(), calls=%async_computation.2 | async-start | bytes 1081344 | tf_op jit(solution)/shard_map/all_gather | solution.py:17
  134.7 6.6 %copy-start = (bf16[128,128]{0,1:T(8,128)(2,1)S(1)}, bf16[128,128]{0,1:T(8,128)(2,1)}, u32[]{:S(2)}) copy-start(bf16[128,128]{0,1:T(8,128)(2,1)} %multiply_convert_fusion.2) | copy-start | bytes 98308
  202.1 6.6 %copy-start.1 = (bf16[128,128]{0,1:T(8,128)(2,1)S(1)}, bf16[128,128]{0,1:T(8,128)(2,1)}, u32[]{:S(2)}) copy-start(bf16[128,128]{0,1:T(8,128)(2,1)} %multiply_convert_fusion.1) | copy-start | bytes 98308
Sparse Core Ops, SparseCore 0:
  10.2 56.4 all-gather.3
  85.6 47.4 all-gather.5
  152.4 48.0 all-gather.7
where the time goes:
time: 227 us; the launch traced here: 226 us
  waiting for transfers between devices  153 us (67%)
  matrix products  30.7 us (14%)
  local copies, waits for them, and re-layouts  26.5 us (12%)
  between operations  13.8 us (6%)
    all_gather x3, waiting for transfers between devices, shards(): whole = lax.all_gather(current, ('blk', 'col'), axis=0, tiled=True)  152 us
    dot_general x3, matrix products, shards(): lax.dot_general(tile_set, picked, (((0, 2), (0, 1)), ((), ())), preferred...  30.7 us
    gather x3, local copies, waits for them, and re-layouts, shards(): blocks[col_ids]  20.9 us
  transfers between devices with their start and end apart: 3, of which 3 were waited for; matrix products, arithmetic and copies ran while one was open for 1% of the time, Pallas kernels for 0%

commit v1 on v0

v1 whole, which is shorter than its diff:
```python
import functools

import jax
import jax.numpy as jnp
from jax import lax
from jax.experimental import pallas as pl
from jax.experimental.pallas import tpu as pltpu
from jax.sharding import PartitionSpec as P

epsilon = 1e-05
AXES = ("blk", "col")
CHUNK = 8


def moved(index, spots):
    result = 0
    for b, spot in enumerate(spots):
        result = result | (((index >> b) & 1) << spot)
    return result


def presum_kernel(cols_ref, count_ref, tiles_hbm, out_ref, buf, acc_a, acc_b, sems, *, devices, spots):
    slots = tiles_hbm.shape[0]
    half = out_ref.shape[2]
    chunks = slots // CHUNK
    count = count_ref[0]
    me = moved(lax.axis_index("blk") * devices[1] + lax.axis_index("col"), spots)

    def copy(c):
        window = pl.ds(c * CHUNK, CHUNK)
        return pltpu.make_async_copy(tiles_hbm.at[window], buf.at[window], sems.at[c])

    for c in range(chunks):
        @pl.when(c * CHUNK < count)
        def _():
            copy(c).start()

    def clear(i, carry):
        acc_a[i] = jnp.zeros(acc_a.shape[1:], jnp.float32)
        acc_b[i] = jnp.zeros(acc_b.shape[1:], jnp.float32)
        return carry

    lax.fori_loop(0, acc_a.shape[0], clear, 0)

    def add(acc, slot):
        @pl.when(slot < count)
        def _():
            left = me ^ moved(cols_ref[0, slot] * 2, spots)
            right = left ^ moved(1, spots)
            acc[left] = acc[left] + buf[slot, :, :half].astype(jnp.float32)
            acc[right] = acc[right] + buf[slot, :, half:].astype(jnp.float32)

    def chunk_body(c, carry):
        @pl.when(c * CHUNK < count)
        def _():
            copy(c).wait()
            for t in range(0, CHUNK, 2):
                add(acc_a, c * CHUNK + t)
                add(acc_b, c * CHUNK + t + 1)
        return carry

    lax.fori_loop(0, chunks, chunk_body, 0)

    def finish(i, carry):
        out_ref[i] = (acc_a[i] + acc_b[i]).astype(jnp.bfloat16)
        return carry

    lax.fori_loop(0, acc_a.shape[0], finish, 0)


def presum(tiles, cols, count, devices, spots):
    slots, rows, width = tiles.shape
    total = devices[0] * devices[1]
    half = width // 2
    return pl.pallas_call(
        functools.partial(presum_kernel, devices=devices, spots=spots),
        out_shape=jax.ShapeDtypeStruct((total, rows, half), jnp.bfloat16),
        in_specs=[
            pl.BlockSpec(memory_space=pltpu.SMEM),
            pl.BlockSpec(memory_space=pltpu.SMEM),
            pl.BlockSpec(memory_space=pl.ANY),
        ],
        out_specs=pl.BlockSpec(memory_space=pltpu.VMEM),
        scratch_shapes=[
            pltpu.VMEM((slots, rows, width), jnp.bfloat16),
            pltpu.VMEM((total, rows, half), jnp.float32),
            pltpu.VMEM((total, rows, half), jnp.float32),
            pltpu.SemaphoreType.DMA((slots // CHUNK,)),
        ],
        cost_estimate=pl.CostEstimate(
            flops=slots * rows * width * 8, bytes_accessed=slots * rows * width * 2, transcendentals=0
        ),
        name="presum",
    )(cols, count, tiles)


def product(adj_ref, first, parts):
    total = None
    spot = first
    for part in parts:
        blocks, rows, width = part.shape
        adj = jnp.concatenate([adj_ref[spot + j] for j in range(blocks)], axis=1)
        term = jnp.dot(adj, part[...].reshape(blocks * rows, width), preferred_element_type=jnp.float32)
        total = term if total is None else total + term
        spot += blocks
    return total


def near_kernel(adj_ref, *refs):
    refs[-1][...] = product(adj_ref, 0, refs[:-1])


def far_kernel(adj_ref, far_ref, partial_ref, own_ref, gain_ref, out_ref, *, first, hop):
    summed = product(adj_ref, first, [far_ref]) + partial_ref[...] + own_ref[...].astype(jnp.float32)
    mean_sq = jnp.mean(summed * summed, axis=1, keepdims=True)
    scaled = summed * lax.rsqrt(mean_sq + epsilon) * gain_ref[hop : hop + 1, :]
    out_ref[...] = scaled.astype(jnp.bfloat16)


def near(adj, parts):
    rows = adj.shape[1]
    width = parts[0].shape[2]
    depth = sum(part.shape[0] for part in parts) * rows
    return pl.pallas_call(
        near_kernel,
        out_shape=jax.ShapeDtypeStruct((rows, width), jnp.float32),
        cost_estimate=pl.CostEstimate(flops=2 * rows * depth * width, bytes_accessed=depth * width * 4, transcendentals=0),
        name="near",
    )(adj, *parts)


def far(adj, part, partial, own, gain, first, hop):
    return pl.pallas_call(
        functools.partial(far_kernel, first=first, hop=hop),
        out_shape=jax.ShapeDtypeStruct(own.shape, jnp.bfloat16),
        name="far",
    )(adj, part, partial, own, gain)


def exchange(value, mask, total):
    return lax.ppermute(value, AXES, [(i, i ^ mask) for i in range(total)])


def stages(devices):
    bits = (devices[0] * devices[1]).bit_length() - 1
    core_bit = devices[1].bit_length() - 1
    line = [b for b in range(bits) if b != core_bit][::-1]
    groups = [line[i : i + 2] for i in range(0, len(line), 2)]
    line = line + [core_bit]
    return groups, core_bit, [line.index(b) for b in range(bits)]


def solution(mesh):
    devices = (mesh.shape["blk"], mesh.shape["col"])
    total = devices[0] * devices[1]
    groups, core_bit, spots = stages(devices)

    def shards(features, tile_vals, tile_cols, tile_count, norm_gain):
        adj = presum(tile_vals[0], tile_cols, tile_count, devices, spots)
        current = features
        for hop in range(norm_gain.shape[0]):
            held = current[None]
            for group in groups:
                masks = [0]
                for b in group:
                    masks = masks + [m | (1 << b) for m in masks]
                parts = [held if m == 0 else exchange(held, m, total) for m in masks]
                held = jnp.concatenate(parts, axis=0)
            other = exchange(held, 1 << core_bit, total)
            partial = near(adj, [held])
            current = far(adj, other, partial, current, norm_gain, total // 2, hop)
        return current

    placed = (P(AXES, None), P("blk", None, "col", None), P("blk", None), P("blk"), P())
    return jax.shard_map(shards, mesh=mesh, in_specs=placed, out_specs=P(AXES, None), check_vma=False)
```

time: 227 us -> 81.3 us (0.36)
  waiting for transfers between devices: 153 us -> 25.5 us
  matrix products: 30.7 us -> 0 us
  starting transfers between devices: 0.26 us -> 25.3 us
  Pallas kernels: 0 us -> 20.2 us
  local copies, waits for them, and re-layouts: 26.5 us -> 6.59 us
  between operations: 13.8 us -> 0.82 us
    all_gather x3 -> x0, waiting for transfers between devices: 152 us -> none  [shards(): whole = lax.all_gather(current, ('blk', 'col'), axis=0, tiled=True)]
    dot_general x3 -> x0, matrix products: 30.7 us -> none  [shards(): lax.dot_general(tile_set, picked, (((0, 2), (0, 1)), ((), ())), preferred...]
    ppermute x0 -> x21, waiting for transfers between devices: none -> 25.5 us  [exchange(): return lax.ppermute(value, AXES, [(i, i ^ mask) for i in range(total)])]
    ppermute x0 -> x21, starting transfers between devices: none -> 25.3 us  [exchange(): return lax.ppermute(value, AXES, [(i, i ^ mask) for i in range(total)])]
    gather x3 -> x0, local copies, waits for them, and re-layouts: 20.9 us -> none  [shards(): blocks[col_ids]]
    pallas_call x0 -> x7, Pallas kernels: none -> 20.2 us  [the longest x3 7.19 us: far(): pl.pallas_call(functools.partial(far_kernel, first=first, hop=hop), out_s...]
    unnamed x5 -> x30, local copies, waits for them, and re-layouts: 0.87 us -> 6.53 us
    reshape x2 -> x0, local copies, waits for them, and re-layouts: 3.22 us -> none  [shards(): blocks = whole.reshape(-1, tile_rows, whole.shape[1])]
  transfers between devices with their start and end apart: 3 -> 21, of which waited for: 3 -> 15; matrix products, arithmetic and copies ran while one was open for 1% -> 3% of each run, Pallas kernels for 0% -> 16%
where the time goes in v1:
time: 81.3 us; the launch traced here: 80.8 us
  waiting for transfers between devices  25.5 us (31%)
  starting transfers between devices  25.3 us (31%)
  Pallas kernels  20.2 us (25%)
  local copies, waits for them, and re-layouts  6.59 us (8%)
  other arithmetic  2.33 us (3%)
  between operations  0.82 us (1%)
    ppermute x21, waiting for transfers between devices, exchange(): return lax.ppermute(value, AXES, [(i, i ^ mask) for i in range(total)])  25.5 us
    ppermute x21, starting transfers between devices, exchange(): return lax.ppermute(value, AXES, [(i, i ^ mask) for i in range(total)])  25.3 us
    pallas_call x3, Pallas kernels, far(): pl.pallas_call(functools.partial(far_kernel, first=first, hop=hop), out_s...  7.19 us
    pallas_call x3, Pallas kernels, near(): pl.pallas_call(near_kernel, out_shape=jax.ShapeDtypeStruct((rows, width),...  6.84 us
    unnamed x30, local copies, waits for them, and re-layouts  6.53 us
    pallas_call x1, Pallas kernels, presum(): pl.pallas_call(functools.partial(presum_kernel, devices=devices, spots=sp...  6.2 us
    concatenate x3, other arithmetic, shards(): held = jnp.concatenate(parts, axis=0)  2.33 us
  transfers between devices with their start and end apart: 21, of which 15 were waited for; matrix products, arithmetic and copies ran while one was open for 3% of the time, Pallas kernels for 16%

profile of v1, /device:TPU:0, one launch (start us, length us, event | category | flops | bytes accessed | tf_op | source)
XLA Modules:
  0.0 80.8 jit_solution(7249485271263384435)
XLA Ops:
  0.0 4.1 %collective-permute-start = (bf16[1,128,128]{2,1,0:T(8,128)(2,1)}, bf16[1,128,128]{2,1,0:T(8,128)(2,1)S(1)}, u32[]{:S(2)}, u32[]{:S(2)}) collective-permute-start(bf16[1,128,128]{2,1,0:T(8,128)(2,1)} %bitcast.16), channel_id=1, source_target_pairs={{0,16},{1,17},{2,18},{3,19},{4,20},{5,21},{6,22},{7,23},{8,24},{9,... | collective-permute-start | bytes 98312 | tf_op jit(solution)/shard_map/ppermute | solution.py:141
  4.1 1.6 %collective-permute-start.1 = (bf16[1,128,128]{2,1,0:T(8,128)(2,1)}, bf16[1,128,128]{2,1,0:T(8,128)(2,1)S(1)}, u32[]{:S(2)}, u32[]{:S(2)}) collective-permute-start(bf16[1,128,128]{2,1,0:T(8,128)(2,1)} %bitcast.17), channel_id=1, source_target_pairs={{0,8},{1,9},{2,10},{3,11},{4,12},{5,13},{6,14},{7,15},{8,0},{9,1},... | collective-permute-start | bytes 98312 | tf_op jit(solution)/shard_map/ppermute | solution.py:141
  5.6 0.8 %constant_dynamic-update-slice_fusion.6 = bf16[16,128,128]{2,1,0:T(8,128)(2,1)S(1)} fusion(bf16[128,128]{1,0:T(8,128)(2,1)} %own_ref.1), kind=kLoop, calls=%fused_computation.9 | loop fusion | bytes 65536
  6.6 1.6 %collective-permute-done.1 = bf16[1,128,128]{2,1,0:T(8,128)(2,1)S(1)} collective-permute-done((bf16[1,128,128]{2,1,0:T(8,128)(2,1)}, bf16[1,128,128]{2,1,0:T(8,128)(2,1)S(1)}, u32[]{:S(2)}, u32[]{:S(2)}) %collective-permute-start.1) | collective-permute-done | bytes 32800 | tf_op jit(solution)/shard_map/ppermute | solution.py:141
  8.2 3.4 %collective-permute-done.2 = bf16[1,128,128]{2,1,0:T(8,128)(2,1)S(1)} collective-permute-done((bf16[1,128,128]{2,1,0:T(8,128)(2,1)}, bf16[1,128,128]{2,1,0:T(8,128)(2,1)S(1)}, u32[]{:S(2)}, u32[]{:S(2)}) %collective-permute-start.2) | collective-permute-done | bytes 32800 | tf_op jit(solution)/shard_map/ppermute | solution.py:141
  12.3 1.6 %collective-permute-start.3 = (bf16[4,128,128]{2,1,0:T(8,128)(2,1)S(1)}, bf16[4,128,128]{2,1,0:T(8,128)(2,1)S(1)}, u32[]{:S(2)}, u32[]{:S(2)}) collective-permute-start(bf16[4,128,128]{2,1,0:T(8,128)(2,1)S(1)} %pad_maximum_fusion), channel_id=1, source_target_pairs={{0,4},{1,5},{2,6},{3,7},{4,0},{5,1},{6,2},{7,3},{8,12},{9,13},{10,... | collective-permute-start | bytes 393224 | tf_op jit(solution)/shard_map/ppermute | solution.py:141
  13.9 1.5 %collective-permute-start.4 = (bf16[4,128,128]{2,1,0:T(8,128)(2,1)S(1)}, bf16[4,128,128]{2,1,0:T(8,128)(2,1)S(1)}, u32[]{:S(2)}, u32[]{:S(2)}) collective-permute-start(bf16[4,128,128]{2,1,0:T(8,128)(2,1)S(1)} %pad_maximum_fusion), channel_id=1, source_target_pairs={{0,1},{1,0},{2,3},{3,2},{4,5},{5,4},{6,7},{7,6},{8,9},{9,8},{10,11... | collective-permute-start | bytes 393224 | tf_op jit(solution)/shard_map/ppermute | solution.py:141
  15.9 2.5 %collective-permute-done.3 = bf16[4,128,128]{2,1,0:T(8,128)(2,1)S(1)} collective-permute-done((bf16[4,128,128]{2,1,0:T(8,128)(2,1)S(1)}, bf16[4,128,128]{2,1,0:T(8,128)(2,1)S(1)}, u32[]{:S(2)}, u32[]{:S(2)}) %collective-permute-start.3) | collective-permute-done | bytes 131104 | tf_op jit(solution)/shard_map/ppermute | solution.py:141
  18.5 1.2 %collective-permute-done.4 = bf16[4,128,128]{2,1,0:T(8,128)(2,1)S(1)} collective-permute-done((bf16[4,128,128]{2,1,0:T(8,128)(2,1)S(1)}, bf16[4,128,128]{2,1,0:T(8,128)(2,1)S(1)}, u32[]{:S(2)}, u32[]{:S(2)}) %collective-permute-start.4) | collective-permute-done | bytes 131104 | tf_op jit(solution)/shard_map/ppermute | solution.py:141
  19.7 1.6 %collective-permute-done.5 = bf16[4,128,128]{2,1,0:T(8,128)(2,1)S(1)} collective-permute-done((bf16[4,128,128]{2,1,0:T(8,128)(2,1)S(1)}, bf16[4,128,128]{2,1,0:T(8,128)(2,1)S(1)}, u32[]{:S(2)}, u32[]{:S(2)}) %collective-permute-start.5) | collective-permute-done | bytes 131104 | tf_op jit(solution)/shard_map/ppermute | solution.py:141
  22.1 6.2 %presum.1.adj_ref = bf16[32,128,128]{2,1,0:T(8,128)(2,1)} custom-call(s32[1,128]{1,0:T(1,128)} %cols_ref.1, s32[1]{0:T(128)S(6)} %copy.24.count_ref, bf16[128,128,256]{2,1,0:T(8,128)(2,1)} %bitcast.7), custom_call_target="tpu_custom_call" | custom-call | flops 33554432 | bytes 8388608 | tf_op jit(solution)/shard_map/presum/pallas_call | solution.py:75
  28.3 2.3 %near.3.partial_ref = f32[128,128]{1,0:T(8,128)} custom-call(bf16[32,128,128]{2,1,0:T(8,128)(2,1)} %presum.1.adj_ref, bf16[16,128,128]{2,1,0:T(8,128)(2,1)} %copy-done), custom_call_target="tpu_custom_call" | custom-call | flops 67108864 | bytes 1048576 | tf_op jit(solution)/shard_map/near/pallas_call | solution.py:124
  30.6 0.8 %copy-done.3 = bf16[16,128,128]{2,1,0:T(8,128)(2,1)} copy-done((bf16[16,128,128]{2,1,0:T(8,128)(2,1)}, bf16[16,128,128]{2,1,0:T(8,128)(2,1)S(1)}, u32[]{:S(2)}) %copy-start.3) | copy-done | bytes 524312
  31.4 2.4 %far.3.own_ref = bf16[128,128]{1,0:T(8,128)(2,1)} custom-call(bf16[32,128,128]{2,1,0:T(8,128)(2,1)} %presum.1.adj_ref, bf16[16,128,128]{2,1,0:T(8,128)(2,1)} %copy-done.3, f32[128,128]{1,0:T(8,128)} %near.3.partial_ref, bf16[128,128]{1,0:T(8,128)(2,1)} %own_ref.1, f32[3,128]{1,0:T(4,128)} %gain_ref.5), custom_call_target="tpu_custom_call" | custom-call | tf_op jit(solution)/shard_map/far/pallas_call | solution.py:133
  33.8 4.4 %collective-permute-start.9 = (bf16[1,128,128]{2,1,0:T(8,128)(2,1)}, bf16[1,128,128]{2,1,0:T(8,128)(2,1)S(1)}, u32[]{:S(2)}, u32[]{:S(2)}) collective-permute-start(bf16[1,128,128]{2,1,0:T(8,128)(2,1)} %bitcast.14), channel_id=1, source_target_pairs={{0,24},{1,25},{2,26},{3,27},{4,28},{5,29},{6,30},{7,31},{8,16},{9,... | collective-permute-start | bytes 98312 | tf_op jit(solution)/shard_map/ppermute | solution.py:141
  39.0 1.6 %collective-permute-done.9 = bf16[1,128,128]{2,1,0:T(8,128)(2,1)S(1)} collective-permute-done((bf16[1,128,128]{2,1,0:T(8,128)(2,1)}, bf16[1,128,128]{2,1,0:T(8,128)(2,1)S(1)}, u32[]{:S(2)}, u32[]{:S(2)}) %collective-permute-start.9) | collective-permute-done | bytes 32800 | tf_op jit(solution)/shard_map/ppermute | solution.py:141
  42.7 2.2 %collective-permute-start.12 = (bf16[4,128,128]{2,1,0:T(8,128)(2,1)S(1)}, bf16[4,128,128]{2,1,0:T(8,128)(2,1)S(1)}, u32[]{:S(2)}, u32[]{:S(2)}) collective-permute-start(bf16[4,128,128]{2,1,0:T(8,128)(2,1)S(1)} %pad_maximum_fusion.1), channel_id=1, source_target_pairs={{0,5},{1,4},{2,7},{3,6},{4,1},{5,0},{6,3},{7,2},{8,13},{9,12},{10,... | collective-permute-start | bytes 393224 | tf_op jit(solution)/shard_map/ppermute | solution.py:141
  45.0 1.4 %collective-permute-done.10 = bf16[4,128,128]{2,1,0:T(8,128)(2,1)S(1)} collective-permute-done((bf16[4,128,128]{2,1,0:T(8,128)(2,1)S(1)}, bf16[4,128,128]{2,1,0:T(8,128)(2,1)S(1)}, u32[]{:S(2)}, u32[]{:S(2)}) %collective-permute-start.10) | collective-permute-done | bytes 131104 | tf_op jit(solution)/shard_map/ppermute | solution.py:141
  47.0 1.6 %collective-permute-done.12 = bf16[4,128,128]{2,1,0:T(8,128)(2,1)S(1)} collective-permute-done((bf16[4,128,128]{2,1,0:T(8,128)(2,1)S(1)}, bf16[4,128,128]{2,1,0:T(8,128)(2,1)S(1)}, u32[]{:S(2)}, u32[]{:S(2)}) %collective-permute-start.12) | collective-permute-done | bytes 131104 | tf_op jit(solution)/shard_map/ppermute | solution.py:141
  49.4 2.3 %near.4.partial_ref = f32[128,128]{1,0:T(8,128)} custom-call(bf16[32,128,128]{2,1,0:T(8,128)(2,1)} %presum.1.adj_ref, bf16[16,128,128]{2,1,0:T(8,128)(2,1)} %copy-done.1), custom_call_target="tpu_custom_call" | custom-call | flops 67108864 | bytes 1048576 | tf_op jit(solution)/shard_map/near/pallas_call | solution.py:124
  51.7 0.8 %copy-done.5 = bf16[16,128,128]{2,1,0:T(8,128)(2,1)} copy-done((bf16[16,128,128]{2,1,0:T(8,128)(2,1)}, bf16[16,128,128]{2,1,0:T(8,128)(2,1)S(1)}, u32[]{:S(2)}) %copy-start.5) | copy-done | bytes 524312
  52.6 2.4 %far.4.own_ref = bf16[128,128]{1,0:T(8,128)(2,1)} custom-call(bf16[32,128,128]{2,1,0:T(8,128)(2,1)} %presum.1.adj_ref, bf16[16,128,128]{2,1,0:T(8,128)(2,1)} %copy-done.5, f32[128,128]{1,0:T(8,128)} %near.4.partial_ref, bf16[128,128]{1,0:T(8,128)(2,1)} %far.3.own_ref, f32[3,128]{1,0:T(4,128)} %gain_ref.5), custom_call_target="tpu_custom_call" | custom-call | tf_op jit(solution)/shard_map/far/pallas_call | solution.py:133
  54.9 3.7 %collective-permute-start.15 = (bf16[1,128,128]{2,1,0:T(8,128)(2,1)}, bf16[1,128,128]{2,1,0:T(8,128)(2,1)S(1)}, u32[]{:S(2)}, u32[]{:S(2)}) collective-permute-start(bf16[1,128,128]{2,1,0:T(8,128)(2,1)} %bitcast.9), channel_id=1, source_target_pairs={{0,8},{1,9},{2,10},{3,11},{4,12},{5,13},{6,14},{7,15},{8,0},{9,1},... | collective-permute-start | bytes 98312 | tf_op jit(solution)/shard_map/ppermute | solution.py:141
  60.8 3.8 %collective-permute-done.16 = bf16[1,128,128]{2,1,0:T(8,128)(2,1)S(1)} collective-permute-done((bf16[1,128,128]{2,1,0:T(8,128)(2,1)}, bf16[1,128,128]{2,1,0:T(8,128)(2,1)S(1)}, u32[]{:S(2)}, u32[]{:S(2)}) %collective-permute-start.16) | collective-permute-done | bytes 32800 | tf_op jit(solution)/shard_map/ppermute | solution.py:141
  65.3 2.0 %collective-permute-start.17 = (bf16[4,128,128]{2,1,0:T(8,128)(2,1)S(1)}, bf16[4,128,128]{2,1,0:T(8,128)(2,1)S(1)}, u32[]{:S(2)}, u32[]{:S(2)}) collective-permute-start(bf16[4,128,128]{2,1,0:T(8,128)(2,1)S(1)} %pad_maximum_fusion.2), channel_id=1, source_target_pairs={{0,4},{1,5},{2,6},{3,7},{4,0},{5,1},{6,2},{7,3},{8,12},{9,13},{10,... | collective-permute-start | bytes 393224 | tf_op jit(solution)/shard_map/ppermute | solution.py:141
  67.3 1.2 %collective-permute-start.18 = (bf16[4,128,128]{2,1,0:T(8,128)(2,1)S(1)}, bf16[4,128,128]{2,1,0:T(8,128)(2,1)S(1)}, u32[]{:S(2)}, u32[]{:S(2)}) collective-permute-start(bf16[4,128,128]{2,1,0:T(8,128)(2,1)S(1)} %pad_maximum_fusion.2), channel_id=1, source_target_pairs={{0,1},{1,0},{2,3},{3,2},{4,5},{5,4},{6,7},{7,6},{8,9},{9,8},{10,11... | collective-permute-start | bytes 393224 | tf_op jit(solution)/shard_map/ppermute | solution.py:141
  68.9 2.8 %collective-permute-done.17 = bf16[4,128,128]{2,1,0:T(8,128)(2,1)S(1)} collective-permute-done((bf16[4,128,128]{2,1,0:T(8,128)(2,1)S(1)}, bf16[4,128,128]{2,1,0:T(8,128)(2,1)S(1)}, u32[]{:S(2)}, u32[]{:S(2)}) %collective-permute-start.17) | collective-permute-done | bytes 131104 | tf_op jit(solution)/shard_map/ppermute | solution.py:141
  71.7 1.3 %collective-permute-done.18 = bf16[4,128,128]{2,1,0:T(8,128)(2,1)S(1)} collective-permute-done((bf16[4,128,128]{2,1,0:T(8,128)(2,1)S(1)}, bf16[4,128,128]{2,1,0:T(8,128)(2,1)S(1)}, u32[]{:S(2)}, u32[]{:S(2)}) %collective-permute-start.18) | collective-permute-done | bytes 131104 | tf_op jit(solution)/shard_map/ppermute | solution.py:141
  73.0 1.4 %collective-permute-done.19 = bf16[4,128,128]{2,1,0:T(8,128)(2,1)S(1)} collective-permute-done((bf16[4,128,128]{2,1,0:T(8,128)(2,1)S(1)}, bf16[4,128,128]{2,1,0:T(8,128)(2,1)S(1)}, u32[]{:S(2)}, u32[]{:S(2)}) %collective-permute-start.19) | collective-permute-done | bytes 131104 | tf_op jit(solution)/shard_map/ppermute | solution.py:141
  75.3 2.3 %near.5.partial_ref = f32[128,128]{1,0:T(8,128)} custom-call(bf16[32,128,128]{2,1,0:T(8,128)(2,1)} %presum.1.adj_ref, bf16[16,128,128]{2,1,0:T(8,128)(2,1)} %copy-done.2), custom_call_target="tpu_custom_call" | custom-call | flops 67108864 | bytes 1048576 | tf_op jit(solution)/shard_map/near/pallas_call | solution.py:124
  77.5 0.8 %copy-done.4 = bf16[16,128,128]{2,1,0:T(8,128)(2,1)} copy-done((bf16[16,128,128]{2,1,0:T(8,128)(2,1)}, bf16[16,128,128]{2,1,0:T(8,128)(2,1)S(1)}, u32[]{:S(2)}) %copy-start.4) | copy-done | bytes 524312
  78.4 2.4 %far.5 = bf16[128,128]{1,0:T(8,128)(2,1)} custom-call(bf16[32,128,128]{2,1,0:T(8,128)(2,1)} %presum.1.adj_ref, bf16[16,128,128]{2,1,0:T(8,128)(2,1)} %copy-done.4, f32[128,128]{1,0:T(8,128)} %near.5.partial_ref, bf16[128,128]{1,0:T(8,128)(2,1)} %far.4.own_ref, f32[3,128]{1,0:T(4,128)} %gain_ref.5), custom_call_target="tpu_custom_call" | custom-call | tf_op jit(solution)/shard_map/far/pallas_call | solution.py:133
  (53 shorter events, 10.0 us)
Async XLA Ops:
  0.0 6.6 %collective-permute-start = (bf16[1,128,128]{2,1,0:T(8,128)(2,1)}, bf16[1,128,128]{2,1,0:T(8,128)(2,1)S(1)}, u32[]{:S(2)}, u32[]{:S(2)}) collective-permute-start(bf16[1,128,128]{2,1,0:T(8,128)(2,1)} %bitcast.16), channel_id=1, source_target_pairs={{0,16},{1,17},{2,18},{3,19},{4,20},{5,21},{6,22},{7,23},{8,24},{9,... | collective-permute-start | bytes 98312 | tf_op jit(solution)/shard_map/ppermute | solution.py:141
  4.1 4.1 %collective-permute-start.1 = (bf16[1,128,128]{2,1,0:T(8,128)(2,1)}, bf16[1,128,128]{2,1,0:T(8,128)(2,1)S(1)}, u32[]{:S(2)}, u32[]{:S(2)}) collective-permute-start(bf16[1,128,128]{2,1,0:T(8,128)(2,1)} %bitcast.17), channel_id=1, source_target_pairs={{0,8},{1,9},{2,10},{3,11},{4,12},{5,13},{6,14},{7,15},{8,0},{9,1},... | collective-permute-start | bytes 98312 | tf_op jit(solution)/shard_map/ppermute | solution.py:141
  5.6 5.9 %collective-permute-start.2 = (bf16[1,128,128]{2,1,0:T(8,128)(2,1)}, bf16[1,128,128]{2,1,0:T(8,128)(2,1)S(1)}, u32[]{:S(2)}, u32[]{:S(2)}) collective-permute-start(bf16[1,128,128]{2,1,0:T(8,128)(2,1)} %bitcast.18), channel_id=1, source_target_pairs={{0,24},{1,25},{2,26},{3,27},{4,28},{5,29},{6,30},{7,31},{8,16},{9,... | collective-permute-start | bytes 98312 | tf_op jit(solution)/shard_map/ppermute | solution.py:141
  12.3 6.1 %collective-permute-start.3 = (bf16[4,128,128]{2,1,0:T(8,128)(2,1)S(1)}, bf16[4,128,128]{2,1,0:T(8,128)(2,1)S(1)}, u32[]{:S(2)}, u32[]{:S(2)}) collective-permute-start(bf16[4,128,128]{2,1,0:T(8,128)(2,1)S(1)} %pad_maximum_fusion), channel_id=1, source_target_pairs={{0,4},{1,5},{2,6},{3,7},{4,0},{5,1},{6,2},{7,3},{8,12},{9,13},{10,... | collective-permute-start | bytes 393224 | tf_op jit(solution)/shard_map/ppermute | solution.py:141
  13.9 5.8 %collective-permute-start.4 = (bf16[4,128,128]{2,1,0:T(8,128)(2,1)S(1)}, bf16[4,128,128]{2,1,0:T(8,128)(2,1)S(1)}, u32[]{:S(2)}, u32[]{:S(2)}) collective-permute-start(bf16[4,128,128]{2,1,0:T(8,128)(2,1)S(1)} %pad_maximum_fusion), channel_id=1, source_target_pairs={{0,1},{1,0},{2,3},{3,2},{4,5},{5,4},{6,7},{7,6},{8,9},{9,8},{10,11... | collective-permute-start | bytes 393224 | tf_op jit(solution)/shard_map/ppermute | solution.py:141
  15.4 5.9 %collective-permute-start.5 = (bf16[4,128,128]{2,1,0:T(8,128)(2,1)S(1)}, bf16[4,128,128]{2,1,0:T(8,128)(2,1)S(1)}, u32[]{:S(2)}, u32[]{:S(2)}) collective-permute-start(bf16[4,128,128]{2,1,0:T(8,128)(2,1)S(1)} %pad_maximum_fusion), channel_id=1, source_target_pairs={{0,5},{1,4},{2,7},{3,6},{4,1},{5,0},{6,3},{7,2},{8,13},{9,12},{10,... | collective-permute-start | bytes 393224 | tf_op jit(solution)/shard_map/ppermute | solution.py:141
  21.3 7.0 %copy-start = (bf16[16,128,128]{2,1,0:T(8,128)(2,1)}, bf16[16,128,128]{2,1,0:T(8,128)(2,1)S(1)}, u32[]{:S(2)}) copy-start(bf16[16,128,128]{2,1,0:T(8,128)(2,1)S(1)} %constant_dynamic-update-slice_fusion.refs_0_) | copy-start | bytes 1572868
  21.3 9.3 %collective-permute-start.6 = (bf16[16,128,128]{2,1,0:T(8,128)(2,1)S(1)}, bf16[16,128,128]{2,1,0:T(8,128)(2,1)S(1)}, u32[]{:S(2)}, u32[]{:S(2)}) collective-permute-start(bf16[16,128,128]{2,1,0:T(8,128)(2,1)S(1)} %constant_dynamic-update-slice_fusion.refs_0_), channel_id=1, source_target_pairs={{0,2},{1,3},{2,0},{3,1},{4,6},{5,7},{6,4},{7,5},{8,10},{9,11},{10,... | collective-permute-start | bytes 1572872 | tf_op jit(solution)/shard_map/ppermute | solution.py:141
  30.6 0.8 %copy-start.3 = (bf16[16,128,128]{2,1,0:T(8,128)(2,1)}, bf16[16,128,128]{2,1,0:T(8,128)(2,1)S(1)}, u32[]{:S(2)}) copy-start(bf16[16,128,128]{2,1,0:T(8,128)(2,1)S(1)} %collective-permute-done.6.far_ref) | copy-start | bytes 1572868
  33.8 5.2 %collective-permute-start.7 = (bf16[1,128,128]{2,1,0:T(8,128)(2,1)}, bf16[1,128,128]{2,1,0:T(8,128)(2,1)S(1)}, u32[]{:S(2)}, u32[]{:S(2)}) collective-permute-start(bf16[1,128,128]{2,1,0:T(8,128)(2,1)} %bitcast.12), channel_id=1, source_target_pairs={{0,16},{1,17},{2,18},{3,19},{4,20},{5,21},{6,22},{7,23},{8,24},{9,... | collective-permute-start | bytes 98312 | tf_op jit(solution)/shard_map/ppermute | solution.py:141
  33.8 5.2 %collective-permute-start.8 = (bf16[1,128,128]{2,1,0:T(8,128)(2,1)}, bf16[1,128,128]{2,1,0:T(8,128)(2,1)S(1)}, u32[]{:S(2)}, u32[]{:S(2)}) collective-permute-start(bf16[1,128,128]{2,1,0:T(8,128)(2,1)} %bitcast.13), channel_id=1, source_target_pairs={{0,8},{1,9},{2,10},{3,11},{4,12},{5,13},{6,14},{7,15},{8,0},{9,1},... | collective-permute-start | bytes 98312 | tf_op jit(solution)/shard_map/ppermute | solution.py:141
  33.8 6.8 %collective-permute-start.9 = (bf16[1,128,128]{2,1,0:T(8,128)(2,1)}, bf16[1,128,128]{2,1,0:T(8,128)(2,1)S(1)}, u32[]{:S(2)}, u32[]{:S(2)}) collective-permute-start(bf16[1,128,128]{2,1,0:T(8,128)(2,1)} %bitcast.14), channel_id=1, source_target_pairs={{0,24},{1,25},{2,26},{3,27},{4,28},{5,29},{6,30},{7,31},{8,16},{9,... | collective-permute-start | bytes 98312 | tf_op jit(solution)/shard_map/ppermute | solution.py:141
  41.4 5.0 %collective-permute-start.10 = (bf16[4,128,128]{2,1,0:T(8,128)(2,1)S(1)}, bf16[4,128,128]{2,1,0:T(8,128)(2,1)S(1)}, u32[]{:S(2)}, u32[]{:S(2)}) collective-permute-start(bf16[4,128,128]{2,1,0:T(8,128)(2,1)S(1)} %pad_maximum_fusion.1), channel_id=1, source_target_pairs={{0,4},{1,5},{2,6},{3,7},{4,0},{5,1},{6,2},{7,3},{8,12},{9,13},{10,... | collective-permute-start | bytes 393224 | tf_op jit(solution)/shard_map/ppermute | solution.py:141
  42.0 5.0 %collective-permute-start.11 = (bf16[4,128,128]{2,1,0:T(8,128)(2,1)S(1)}, bf16[4,128,128]{2,1,0:T(8,128)(2,1)S(1)}, u32[]{:S(2)}, u32[]{:S(2)}) collective-permute-start(bf16[4,128,128]{2,1,0:T(8,128)(2,1)S(1)} %pad_maximum_fusion.1), channel_id=1, source_target_pairs={{0,1},{1,0},{2,3},{3,2},{4,5},{5,4},{6,7},{7,6},{8,9},{9,8},{10,11... | collective-permute-start | bytes 393224 | tf_op jit(solution)/shard_map/ppermute | solution.py:141
  42.7 5.9 %collective-permute-start.12 = (bf16[4,128,128]{2,1,0:T(8,128)(2,1)S(1)}, bf16[4,128,128]{2,1,0:T(8,128)(2,1)S(1)}, u32[]{:S(2)}, u32[]{:S(2)}) collective-permute-start(bf16[4,128,128]{2,1,0:T(8,128)(2,1)S(1)} %pad_maximum_fusion.1), channel_id=1, source_target_pairs={{0,5},{1,4},{2,7},{3,6},{4,1},{5,0},{6,3},{7,2},{8,13},{9,12},{10,... | collective-permute-start | bytes 393224 | tf_op jit(solution)/shard_map/ppermute | solution.py:141
  48.6 0.8 %copy-start.1 = (bf16[16,128,128]{2,1,0:T(8,128)(2,1)}, bf16[16,128,128]{2,1,0:T(8,128)(2,1)S(1)}, u32[]{:S(2)}) copy-start(bf16[16,128,128]{2,1,0:T(8,128)(2,1)S(1)} %constant_dynamic-update-slice_fusion.7.refs_0_) | copy-start | bytes 1572868
  48.6 3.1 %collective-permute-start.13 = (bf16[16,128,128]{2,1,0:T(8,128)(2,1)S(1)}, bf16[16,128,128]{2,1,0:T(8,128)(2,1)S(1)}, u32[]{:S(2)}, u32[]{:S(2)}) collective-permute-start(bf16[16,128,128]{2,1,0:T(8,128)(2,1)S(1)} %constant_dynamic-update-slice_fusion.7.refs_0_), channel_id=1, source_target_pairs={{0,2},{1,3},{2,0},{3,1},{4,6},{5,7},{6,4},{7,5},{8,10},{9,11},{10,... | collective-permute-start | bytes 1572872 | tf_op jit(solution)/shard_map/ppermute | solution.py:141
  51.7 0.8 %copy-start.5 = (bf16[16,128,128]{2,1,0:T(8,128)(2,1)}, bf16[16,128,128]{2,1,0:T(8,128)(2,1)S(1)}, u32[]{:S(2)}) copy-start(bf16[16,128,128]{2,1,0:T(8,128)(2,1)S(1)} %collective-permute-done.13.far_ref) | copy-start | bytes 1572868
  54.9 5.2 %collective-permute-start.14 = (bf16[1,128,128]{2,1,0:T(8,128)(2,1)}, bf16[1,128,128]{2,1,0:T(8,128)(2,1)S(1)}, u32[]{:S(2)}, u32[]{:S(2)}) collective-permute-start(bf16[1,128,128]{2,1,0:T(8,128)(2,1)} %bitcast.8), channel_id=1, source_target_pairs={{0,16},{1,17},{2,18},{3,19},{4,20},{5,21},{6,22},{7,23},{8,24},{9,... | collective-permute-start | bytes 98312 | tf_op jit(solution)/shard_map/ppermute | solution.py:141
  54.9 5.8 %collective-permute-start.15 = (bf16[1,128,128]{2,1,0:T(8,128)(2,1)}, bf16[1,128,128]{2,1,0:T(8,128)(2,1)S(1)}, u32[]{:S(2)}, u32[]{:S(2)}) collective-permute-start(bf16[1,128,128]{2,1,0:T(8,128)(2,1)} %bitcast.9), channel_id=1, source_target_pairs={{0,8},{1,9},{2,10},{3,11},{4,12},{5,13},{6,14},{7,15},{8,0},{9,1},... | collective-permute-start | bytes 98312 | tf_op jit(solution)/shard_map/ppermute | solution.py:141
  58.6 5.9 %collective-permute-start.16 = (bf16[1,128,128]{2,1,0:T(8,128)(2,1)}, bf16[1,128,128]{2,1,0:T(8,128)(2,1)S(1)}, u32[]{:S(2)}, u32[]{:S(2)}) collective-permute-start(bf16[1,128,128]{2,1,0:T(8,128)(2,1)} %bitcast.10), channel_id=1, source_target_pairs={{0,24},{1,25},{2,26},{3,27},{4,28},{5,29},{6,30},{7,31},{8,16},{9,... | collective-permute-start | bytes 98312 | tf_op jit(solution)/shard_map/ppermute | solution.py:141
  65.3 6.4 %collective-permute-start.17 = (bf16[4,128,128]{2,1,0:T(8,128)(2,1)S(1)}, bf16[4,128,128]{2,1,0:T(8,128)(2,1)S(1)}, u32[]{:S(2)}, u32[]{:S(2)}) collective-permute-start(bf16[4,128,128]{2,1,0:T(8,128)(2,1)S(1)} %pad_maximum_fusion.2), channel_id=1, source_target_pairs={{0,4},{1,5},{2,6},{3,7},{4,0},{5,1},{6,2},{7,3},{8,12},{9,13},{10,... | collective-permute-start | bytes 393224 | tf_op jit(solution)/shard_map/ppermute | solution.py:141
  67.3 5.7 %collective-permute-start.18 = (bf16[4,128,128]{2,1,0:T(8,128)(2,1)S(1)}, bf16[4,128,128]{2,1,0:T(8,128)(2,1)S(1)}, u32[]{:S(2)}, u32[]{:S(2)}) collective-permute-start(bf16[4,128,128]{2,1,0:T(8,128)(2,1)S(1)} %pad_maximum_fusion.2), channel_id=1, source_target_pairs={{0,1},{1,0},{2,3},{3,2},{4,5},{5,4},{6,7},{7,6},{8,9},{9,8},{10,11... | collective-permute-start | bytes 393224 | tf_op jit(solution)/shard_map/ppermute | solution.py:141
  68.5 5.9 %collective-permute-start.19 = (bf16[4,128,128]{2,1,0:T(8,128)(2,1)S(1)}, bf16[4,128,128]{2,1,0:T(8,128)(2,1)S(1)}, u32[]{:S(2)}, u32[]{:S(2)}) collective-permute-start(bf16[4,128,128]{2,1,0:T(8,128)(2,1)S(1)} %pad_maximum_fusion.2), channel_id=1, source_target_pairs={{0,5},{1,4},{2,7},{3,6},{4,1},{5,0},{6,3},{7,2},{8,13},{9,12},{10,... | collective-permute-start | bytes 393224 | tf_op jit(solution)/shard_map/ppermute | solution.py:141
  74.4 0.8 %copy-start.2 = (bf16[16,128,128]{2,1,0:T(8,128)(2,1)}, bf16[16,128,128]{2,1,0:T(8,128)(2,1)S(1)}, u32[]{:S(2)}) copy-start(bf16[16,128,128]{2,1,0:T(8,128)(2,1)S(1)} %constant_dynamic-update-slice_fusion.14.refs_0_) | copy-start | bytes 1572868
  74.4 3.1 %collective-permute-start.20 = (bf16[16,128,128]{2,1,0:T(8,128)(2,1)S(1)}, bf16[16,128,128]{2,1,0:T(8,128)(2,1)S(1)}, u32[]{:S(2)}, u32[]{:S(2)}) collective-permute-start(bf16[16,128,128]{2,1,0:T(8,128)(2,1)S(1)} %constant_dynamic-update-slice_fusion.14.refs_0_), channel_id=1, source_target_pairs={{0,2},{1,3},{2,0},{3,1},{4,6},{5,7},{6,4},{7,5},{8,10},{9,11},{10,... | collective-permute-start | bytes 1572872 | tf_op jit(solution)/shard_map/ppermute | solution.py:141
  77.5 0.8 %copy-start.4 = (bf16[16,128,128]{2,1,0:T(8,128)(2,1)}, bf16[16,128,128]{2,1,0:T(8,128)(2,1)S(1)}, u32[]{:S(2)}) copy-start(bf16[16,128,128]{2,1,0:T(8,128)(2,1)S(1)} %collective-permute-done.20.far_ref) | copy-start | bytes 1572868

commit v2 on v1

v2 whole, which is shorter than its diff:
```python
import functools

import jax
import jax.numpy as jnp
from jax import lax
from jax.experimental import pallas as pl
from jax.experimental.pallas import tpu as pltpu
from jax.sharding import PartitionSpec as P

epsilon = 1e-05
AXES = ("blk", "col")
CHUNK = 8


def moved(index, spots):
    result = 0
    for b, spot in enumerate(spots):
        result = result ^ (((index >> b) & 1) * spot)
    return result


def presum_kernel(count_ref, cols_hbm, tiles_hbm, out_ref, cols_ref, buf, *rest, devices, spots):
    accs, sems = rest[:-1], rest[-1]
    slots = tiles_hbm.shape[0]
    rows, half = accs[0].shape[1:]
    total = out_ref.shape[0]
    chunks = slots // CHUNK
    me = moved(lax.axis_index("blk") * devices[1] + lax.axis_index("col"), spots)
    count = count_ref[0]
    cols_copy = pltpu.make_async_copy(cols_hbm, cols_ref, sems.at[chunks])

    def copy(c):
        window = pl.ds(c * CHUNK, CHUNK)
        return pltpu.make_async_copy(tiles_hbm.at[window], buf.at[window], sems.at[c])

    cols_copy.start()

    for c in range(chunks):
        @pl.when(c * CHUNK < count)
        def _():
            copy(c).start()

    def clear(i, carry):
        for acc in accs:
            acc[i] = jnp.zeros((rows, half), jnp.float32)
        return carry

    lax.fori_loop(0, total, clear, 0)
    cols_copy.wait()

    def chunk_body(c, carry):
        @pl.when(c * CHUNK < count)
        def _():
            copy(c).wait()
            for t in range(CHUNK):
                acc = accs[t % len(accs)]
                slot = c * CHUNK + t
                left = me ^ moved(cols_ref[0, slot] * 2, spots)
                right = left ^ spots[0]
                left = jnp.where(slot < count, left, total)
                right = jnp.where(slot < count, right, total + 1)
                acc[left] = acc[left] + buf[slot, :, :half].astype(jnp.float32)
                acc[right] = acc[right] + buf[slot, :, half:].astype(jnp.float32)
        return carry

    lax.fori_loop(0, chunks, chunk_body, 0)

    def finish(i, carry):
        summed = sum(acc[i] for acc in accs)
        high = summed.astype(jnp.bfloat16)
        out_ref[i, :rows] = high
        out_ref[i, rows:] = (summed - high.astype(jnp.float32)).astype(jnp.bfloat16)
        return carry

    lax.fori_loop(0, total, finish, 0)


def limit(scratch):
    return pltpu.CompilerParams(vmem_limit_bytes=scratch + 4 * 2**20)


def fast(value):
    return pltpu.with_memory_space_constraint(value, pltpu.VMEM)


def slow(value):
    return pltpu.with_memory_space_constraint(value, pltpu.HBM)


def presum(tiles, cols, count, devices, spots):
    slots, rows, width = tiles.shape
    total = devices[0] * devices[1]
    half = width // 2
    accs = [pltpu.VMEM((total + 2, rows, half), jnp.float32)] * (2 if total <= 64 else 1)
    scratch = slots * rows * width * 2 + len(accs) * (total + 2) * rows * half * 4
    return pl.pallas_call(
        functools.partial(presum_kernel, devices=devices, spots=spots),
        out_shape=pltpu.VMEM((total, 2 * rows, half), jnp.bfloat16),
        in_specs=[
            pl.BlockSpec(memory_space=pltpu.SMEM),
            pl.BlockSpec(memory_space=pltpu.HBM),
            pl.BlockSpec(memory_space=pltpu.HBM),
        ],
        out_specs=pl.BlockSpec(memory_space=pltpu.VMEM),
        scratch_shapes=[
            pltpu.SMEM((1, slots), jnp.int32),
            pltpu.VMEM((slots, rows, width), jnp.bfloat16),
            *accs,
            pltpu.SemaphoreType.DMA((slots // CHUNK + 1,)),
        ],
        cost_estimate=pl.CostEstimate(
            flops=slots * rows * width * 8, bytes_accessed=slots * rows * width * 2, transcendentals=0
        ),
        compiler_params=limit(scratch),
        name="presum",
    )(count, slow(cols), slow(tiles))


def near_kernel(value_ref, out_ref):
    out_ref[...] = value_ref[...]


def into_fast(value):
    return pl.pallas_call(
        near_kernel, out_shape=pltpu.VMEM(value.shape, value.dtype), compiler_params=limit(0), name="into_fast"
    )(slow(value))


def product(adj_ref, spots, parts):
    total = None
    for spot, part in zip(spots, parts):
        blocks, rows, width = part.shape
        adj = jnp.concatenate([adj_ref[spot + j] for j in range(blocks)], axis=1)
        term = jnp.dot(adj, part[...].reshape(blocks * rows, width), preferred_element_type=jnp.float32)
        total = term if total is None else total + term
    rows = total.shape[0] // 2
    return total[:rows] + total[rows:]


def partial_kernel(adj_ref, *refs, spots):
    refs[-1][...] = product(adj_ref, spots, refs[:-1])


def last_kernel(adj_ref, part_ref, partial_ref, own_ref, gain_ref, out_ref, *, spot, hop):
    summed = product(adj_ref, [spot], [part_ref]) + partial_ref[...] + own_ref[...].astype(jnp.float32)
    mean_sq = jnp.mean(summed * summed, axis=1, keepdims=True)
    scaled = summed * lax.rsqrt(mean_sq + epsilon) * gain_ref[hop : hop + 1, :]
    out_ref[...] = scaled.astype(jnp.bfloat16)


def partial_sum(adj, spots, parts):
    rows = adj.shape[1] // 2
    width = parts[0].shape[2]
    depth = sum(part.shape[0] for part in parts) * rows
    return pl.pallas_call(
        functools.partial(partial_kernel, spots=spots),
        out_shape=pltpu.VMEM((rows, width), jnp.float32),
        compiler_params=limit(0),
        cost_estimate=pl.CostEstimate(flops=4 * rows * depth * width, bytes_accessed=depth * width * 4, transcendentals=0),
        name="partial",
    )(fast(adj), *[fast(part) for part in parts])


def last(adj, part, partial, own, gain, spot, hop, final):
    return pl.pallas_call(
        functools.partial(last_kernel, spot=spot, hop=hop),
        out_shape=jax.ShapeDtypeStruct(own.shape, own.dtype) if final else pltpu.VMEM(own.shape, own.dtype),
        compiler_params=limit(0),
        name="last",
    )(fast(adj), fast(part), fast(partial), fast(own), fast(gain))


def exchange(value, mask, total):
    return lax.ppermute(value, AXES, [(i, i ^ mask) for i in range(total)])


def masks_of(group):
    if len(group) == 1:
        return [1 << group[0]]
    high, low = 1 << group[0], 1 << group[1]
    return [high | low, high, low]


def stages(devices):
    bits = (devices[0] * devices[1]).bit_length() - 1
    core_bit = devices[1].bit_length() - 1
    line = [b for b in range(bits) if b != core_bit][::-1]
    groups = [line[i : i + 2] for i in range(0, len(line), 2)]
    spots = [0] * bits
    size = 1
    for group in groups:
        for place, mask in enumerate(masks_of(group)):
            if mask & (mask - 1) == 0:
                spots[mask.bit_length() - 1] = size * (place + 1)
        size <<= len(group)
    spots[core_bit] = size
    return groups, core_bit, spots


def solution(mesh):
    devices = (mesh.shape["blk"], mesh.shape["col"])
    total = devices[0] * devices[1]
    groups, core_bit, spots = stages(devices)

    def shards(features, tile_vals, tile_cols, tile_count, norm_gain):
        adj = presum(tile_vals[0], tile_cols, tile_count, devices, spots)
        current = features
        for hop in range(norm_gain.shape[0]):
            held = current[None]
            if hop == 0:
                current = into_fast(current)
            for group in groups:
                received = [exchange(held, mask, total) for mask in masks_of(group)]
                parts = [current[None] if group is groups[0] else held, *received]
                if group is not groups[-1]:
                    held = jnp.concatenate(parts, axis=0)
            if hop == 0:
                *received, adj = lax.optimization_barrier((*parts[1:], adj))
                parts = [parts[0], *received]
            others = [exchange(part, 1 << core_bit, total) for part in parts]
            size = parts[0].shape[0]
            near = [j * size for j in range(len(parts))]
            far = [total // 2 + spot for spot in near]
            partial = partial_sum(adj, near + far[:-1], parts + others[:-1])
            current = last(adj, others[-1], partial, current, norm_gain, far[-1], hop, hop + 1 == norm_gain.shape[0])
        return current

    placed = (P(AXES, None), P("blk", None, "col", None), P("blk", None), P("blk"), P())
    return jax.shard_map(shards, mesh=mesh, in_specs=placed, out_specs=P(AXES, None), check_vma=False)
```

time: 81.3 us -> 56.9 us (0.70)
  Pallas kernels: 20.2 us -> 6.58 us
  local copies, waits for them, and re-layouts: 6.59 us -> 0.01 us
  waiting for transfers between devices: 25.5 us -> 23.2 us
  other arithmetic: 2.33 us -> 0.06 us
    pallas_call x6 -> x7, Pallas kernels: 14 us -> 4.21 us  [the longest x3 1.89 us: partial_sum(): pl.pallas_call(functools.partial(partial_kernel, spots=spots), out_shape=...]
    unnamed x30 -> x2, local copies, waits for them, and re-layouts: 6.53 us -> 0.01 us
    pallas_call x1, Pallas kernels: 6.2 us -> 2.37 us  [presum(): pl.pallas_call(functools.partial(presum_kernel, devices=devices, spots=sp...]
    ppermute x21 -> x30, waiting for transfers between devices: 25.5 us -> 23.2 us  [exchange(): return lax.ppermute(value, AXES, [(i, i ^ mask) for i in range(total)])]
    concatenate x3, other arithmetic: 2.33 us -> 0.06 us  [shards(): held = jnp.concatenate(parts, axis=0)]
    ppermute x21 -> x30, starting transfers between devices: 25.3 us -> 26 us  [exchange(): return lax.ppermute(value, AXES, [(i, i ^ mask) for i in range(total)])]
  transfers between devices with their start and end apart: 21 -> 30, of which waited for: 15 -> 19; matrix products, arithmetic and copies ran while one was open for 3% -> 0% of each run, Pallas kernels for 16% -> 9%
where the time goes in v2:
time: 56.9 us; the launch traced here: 56.6 us
  starting transfers between devices  26 us (46%)
  waiting for transfers between devices  23.2 us (41%)
  Pallas kernels  6.58 us (12%)
  between operations  0.77 us (1%)
    ppermute x30, starting transfers between devices, exchange(): return lax.ppermute(value, AXES, [(i, i ^ mask) for i in range(total)])  26 us
    ppermute x30, waiting for transfers between devices, exchange(): return lax.ppermute(value, AXES, [(i, i ^ mask) for i in range(total)])  23.2 us
    pallas_call x1, Pallas kernels, presum(): pl.pallas_call(functools.partial(presum_kernel, devices=devices, spots=sp...  2.37 us
    pallas_call x3, Pallas kernels, partial_sum(): pl.pallas_call(functools.partial(partial_kernel, spots=spots), out_shape=...  1.89 us
    pallas_call x3, Pallas kernels, last(): pl.pallas_call(functools.partial(last_kernel, spot=spot, hop=hop), out_sh...  1.52 us
  transfers between devices with their start and end apart: 30, of which 19 were waited for; matrix products, arithmetic and copies ran while one was open for 0% of the time, Pallas kernels for 9%

profile of v2, /device:TPU:0, one launch (start us, length us, event | category | flops | bytes accessed | tf_op | source)
XLA Modules:
  0.0 56.6 jit_solution(17466344020694038221)
XLA Ops:
  0.0 5.1 %collective-permute-start = (bf16[1,128,128]{2,1,0:T(8,128)(2,1)}, bf16[1,128,128]{2,1,0:T(8,128)(2,1)S(1)}, u32[]{:S(2)}, u32[]{:S(2)}) collective-permute-start(bf16[1,128,128]{2,1,0:T(8,128)(2,1)} %bitcast.15), channel_id=1, source_target_pairs={{0,24},{1,25},{2,26},{3,27},{4,28},{5,29},{6,30},{7,31},{8,16},{9,... | collective-permute-start | bytes 98312 | tf_op jit(solution)/shard_map/ppermute | solution.py:174
  5.1 0.6 %collective-permute-start.2 = (bf16[1,128,128]{2,1,0:T(8,128)(2,1)}, bf16[1,128,128]{2,1,0:T(8,128)(2,1)S(1)}, u32[]{:S(2)}, u32[]{:S(2)}) collective-permute-start(bf16[1,128,128]{2,1,0:T(8,128)(2,1)} %bitcast.17), channel_id=1, source_target_pairs={{0,8},{1,9},{2,10},{3,11},{4,12},{5,13},{6,14},{7,15},{8,0},{9,1},... | collective-permute-start | bytes 98312 | tf_op jit(solution)/shard_map/ppermute | solution.py:174
  5.7 0.8 %into_fast.1.own_ref = bf16[128,128]{1,0:T(8,128)(2,1)S(1)} custom-call(bf16[128,128]{1,0:T(8,128)(2,1)} %value_ref.1), custom_call_target="tpu_custom_call" | custom-call | tf_op jit(solution)/shard_map/into_fast/pallas_call | solution.py:124
  6.5 0.7 %collective-permute-done = bf16[1,128,128]{2,1,0:T(8,128)(2,1)S(1)} collective-permute-done((bf16[1,128,128]{2,1,0:T(8,128)(2,1)}, bf16[1,128,128]{2,1,0:T(8,128)(2,1)S(1)}, u32[]{:S(2)}, u32[]{:S(2)}) %collective-permute-start) | collective-permute-done | bytes 32800 | tf_op jit(solution)/shard_map/ppermute | solution.py:174
  7.2 2.9 %collective-permute-done.1 = bf16[1,128,128]{2,1,0:T(8,128)(2,1)S(1)} collective-permute-done((bf16[1,128,128]{2,1,0:T(8,128)(2,1)}, bf16[1,128,128]{2,1,0:T(8,128)(2,1)S(1)}, u32[]{:S(2)}, u32[]{:S(2)}) %collective-permute-start.1) | collective-permute-done | bytes 32800 | tf_op jit(solution)/shard_map/ppermute | solution.py:174
  10.1 2.5 %collective-permute-start.3 = (bf16[4,128,128]{2,1,0:T(8,128)(2,1)S(1)}, bf16[4,128,128]{2,1,0:T(8,128)(2,1)S(1)}, u32[]{:S(2)}, u32[]{:S(2)}) collective-permute-start(bf16[4,128,128]{2,1,0:T(8,128)(2,1)S(1)} %pad_maximum_fusion.refs_0_), channel_id=1, source_target_pairs={{0,5},{1,4},{2,7},{3,6},{4,1},{5,0},{6,3},{7,2},{8,13},{9,12},{10,... | collective-permute-start | bytes 393224 | tf_op jit(solution)/shard_map/ppermute | solution.py:174
  14.3 2.4 %presum.1.adj_ref = bf16[32,256,128]{2,1,0:T(8,128)(2,1)S(1)} custom-call(s32[1]{0:T(128)S(6)} %copy.6.count_ref, s32[1,128]{1,0:T(1,128)} %cols_hbm.1, bf16[128,128,256]{2,1,0:T(8,128)(2,1)} %bitcast.14), custom_call_target="tpu_custom_call" | custom-call | flops 33554432 | bytes 8388608 | tf_op jit(solution)/shard_map/presum/pallas_call | solution.py:96
  16.8 1.0 %collective-permute-done.4.refs_2_ = bf16[4,128,128]{2,1,0:T(8,128)(2,1)S(1)} collective-permute-done((bf16[4,128,128]{2,1,0:T(8,128)(2,1)S(1)}, bf16[4,128,128]{2,1,0:T(8,128)(2,1)S(1)}, u32[]{:S(2)}, u32[]{:S(2)}) %collective-permute-start.4) | collective-permute-done | bytes 131104 | tf_op jit(solution)/shard_map/ppermute | solution.py:174
  18.7 0.8 %collective-permute-done.8.refs_5_ = bf16[4,128,128]{2,1,0:T(8,128)(2,1)S(1)} collective-permute-done((bf16[4,128,128]{2,1,0:T(8,128)(2,1)S(1)}, bf16[4,128,128]{2,1,0:T(8,128)(2,1)S(1)}, u32[]{:S(2)}, u32[]{:S(2)}) %collective-permute-start.8) | collective-permute-done | bytes 131104 | tf_op jit(solution)/shard_map/ppermute | solution.py:174
  19.7 0.6 %partial.3.partial_ref = f32[128,128]{1,0:T(8,128)S(1)} custom-call(bf16[32,256,128]{2,1,0:T(8,128)(2,1)S(1)} %presum.1.adj_ref, bf16[4,128,128]{2,1,0:T(8,128)(2,1)S(1)} %pad_maximum_fusion.refs_0_, bf16[4,128,128]{2,1,0:T(8,128)(2,1)S(1)} %collective-permute-done.3.refs_1_, bf16[4,128,128]{2,1,0:T(8,128)(2,1)S(1)} %collective-permute-done.4.refs_2_, ...), custom_call_target="tpu_custom_call" | custom-call | flops 234881024 | bytes 1835008 | tf_op jit(solution)/shard_map/partial/pallas_call | solution.py:155
  20.6 1.6 %collective-permute-start.10 = (bf16[1,128,128]{2,1,0:T(8,128)(2,1)S(1)}, bf16[1,128,128]{2,1,0:T(8,128)(2,1)S(1)}, u32[]{:S(2)}, u32[]{:S(2)}) collective-permute-start(bf16[1,128,128]{2,1,0:T(8,128)(2,1)S(1)} %bitcast.9), channel_id=1, source_target_pairs={{0,24},{1,25},{2,26},{3,27},{4,28},{5,29},{6,30},{7,31},{8,16},{9,... | collective-permute-start | bytes 98312 | tf_op jit(solution)/shard_map/ppermute | solution.py:174
  22.2 0.6 %collective-permute-start.11 = (bf16[1,128,128]{2,1,0:T(8,128)(2,1)S(1)}, bf16[1,128,128]{2,1,0:T(8,128)(2,1)S(1)}, u32[]{:S(2)}, u32[]{:S(2)}) collective-permute-start(bf16[1,128,128]{2,1,0:T(8,128)(2,1)S(1)} %bitcast.10), channel_id=1, source_target_pairs={{0,16},{1,17},{2,18},{3,19},{4,20},{5,21},{6,22},{7,23},{8,24},{9,... | collective-permute-start | bytes 98312 | tf_op jit(solution)/shard_map/ppermute | solution.py:174
  22.8 2.3 %collective-permute-start.12 = (bf16[1,128,128]{2,1,0:T(8,128)(2,1)S(1)}, bf16[1,128,128]{2,1,0:T(8,128)(2,1)S(1)}, u32[]{:S(2)}, u32[]{:S(2)}) collective-permute-start(bf16[1,128,128]{2,1,0:T(8,128)(2,1)S(1)} %bitcast.11), channel_id=1, source_target_pairs={{0,8},{1,9},{2,10},{3,11},{4,12},{5,13},{6,14},{7,15},{8,0},{9,1},... | collective-permute-start | bytes 98312 | tf_op jit(solution)/shard_map/ppermute | solution.py:174
  25.1 1.5 %collective-permute-done.10 = bf16[1,128,128]{2,1,0:T(8,128)(2,1)S(1)} collective-permute-done((bf16[1,128,128]{2,1,0:T(8,128)(2,1)S(1)}, bf16[1,128,128]{2,1,0:T(8,128)(2,1)S(1)}, u32[]{:S(2)}, u32[]{:S(2)}) %collective-permute-start.10) | collective-permute-done | bytes 32800 | tf_op jit(solution)/shard_map/ppermute | solution.py:174
  26.6 0.6 collective-permute-done.11
  27.6 2.8 %collective-permute-start.15 = (bf16[4,128,128]{2,1,0:T(8,128)(2,1)S(1)}, bf16[4,128,128]{2,1,0:T(8,128)(2,1)S(1)}, u32[]{:S(2)}, u32[]{:S(2)}) collective-permute-start(bf16[4,128,128]{2,1,0:T(8,128)(2,1)S(1)} %pad_maximum_fusion.1.refs_0_), channel_id=1, source_target_pairs={{0,5},{1,4},{2,7},{3,6},{4,1},{5,0},{6,3},{7,2},{8,13},{9,12},{10,... | collective-permute-start | bytes 393224 | tf_op jit(solution)/shard_map/ppermute | solution.py:174
  30.4 0.7 %collective-permute-start.13 = (bf16[4,128,128]{2,1,0:T(8,128)(2,1)S(1)}, bf16[4,128,128]{2,1,0:T(8,128)(2,1)S(1)}, u32[]{:S(2)}, u32[]{:S(2)}) collective-permute-start(bf16[4,128,128]{2,1,0:T(8,128)(2,1)S(1)} %pad_maximum_fusion.1.refs_0_), channel_id=1, source_target_pairs={{0,1},{1,0},{2,3},{3,2},{4,5},{5,4},{6,7},{7,6},{8,9},{9,8},{10,11... | collective-permute-start | bytes 393224 | tf_op jit(solution)/shard_map/ppermute | solution.py:174
  31.1 3.8 %collective-permute-done.15.refs_1_ = bf16[4,128,128]{2,1,0:T(8,128)(2,1)S(1)} collective-permute-done((bf16[4,128,128]{2,1,0:T(8,128)(2,1)S(1)}, bf16[4,128,128]{2,1,0:T(8,128)(2,1)S(1)}, u32[]{:S(2)}, u32[]{:S(2)}) %collective-permute-start.15) | collective-permute-done | bytes 131104 | tf_op jit(solution)/shard_map/ppermute | solution.py:174
  34.9 1.4 %collective-permute-done.16.refs_2_ = bf16[4,128,128]{2,1,0:T(8,128)(2,1)S(1)} collective-permute-done((bf16[4,128,128]{2,1,0:T(8,128)(2,1)S(1)}, bf16[4,128,128]{2,1,0:T(8,128)(2,1)S(1)}, u32[]{:S(2)}, u32[]{:S(2)}) %collective-permute-start.16) | collective-permute-done | bytes 131104 | tf_op jit(solution)/shard_map/ppermute | solution.py:174
  36.8 0.8 %collective-permute-done.19.refs_6_ = bf16[4,128,128]{2,1,0:T(8,128)(2,1)S(1)} collective-permute-done((bf16[4,128,128]{2,1,0:T(8,128)(2,1)S(1)}, bf16[4,128,128]{2,1,0:T(8,128)(2,1)S(1)}, u32[]{:S(2)}, u32[]{:S(2)}) %collective-permute-start.19) | collective-permute-done | bytes 131104 | tf_op jit(solution)/shard_map/ppermute | solution.py:174
  37.6 0.6 %partial.4.partial_ref = f32[128,128]{1,0:T(8,128)S(1)} custom-call(bf16[32,256,128]{2,1,0:T(8,128)(2,1)S(1)} %presum.1.adj_ref, bf16[4,128,128]{2,1,0:T(8,128)(2,1)S(1)} %pad_maximum_fusion.1.refs_0_, bf16[4,128,128]{2,1,0:T(8,128)(2,1)S(1)} %collective-permute-done.15.refs_1_, bf16[4,128,128]{2,1,0:T(8,128)(2,1)S(1)} %collective-permute-done.16.refs_2_, ...), custom_call_target="tpu_custom_call" | custom-call | flops 234881024 | bytes 1835008 | tf_op jit(solution)/shard_map/partial/pallas_call | solution.py:155
  38.6 2.2 %collective-permute-start.20 = (bf16[1,128,128]{2,1,0:T(8,128)(2,1)S(1)}, bf16[1,128,128]{2,1,0:T(8,128)(2,1)S(1)}, u32[]{:S(2)}, u32[]{:S(2)}) collective-permute-start(bf16[1,128,128]{2,1,0:T(8,128)(2,1)S(1)} %bitcast.5), channel_id=1, source_target_pairs={{0,24},{1,25},{2,26},{3,27},{4,28},{5,29},{6,30},{7,31},{8,16},{9,... | collective-permute-start | bytes 98312 | tf_op jit(solution)/shard_map/ppermute | solution.py:174
  40.8 2.2 %collective-permute-start.22 = (bf16[1,128,128]{2,1,0:T(8,128)(2,1)S(1)}, bf16[1,128,128]{2,1,0:T(8,128)(2,1)S(1)}, u32[]{:S(2)}, u32[]{:S(2)}) collective-permute-start(bf16[1,128,128]{2,1,0:T(8,128)(2,1)S(1)} %bitcast.7), channel_id=1, source_target_pairs={{0,8},{1,9},{2,10},{3,11},{4,12},{5,13},{6,14},{7,15},{8,0},{9,1},... | collective-permute-start | bytes 98312 | tf_op jit(solution)/shard_map/ppermute | solution.py:174
  43.0 1.3 %collective-permute-done.20 = bf16[1,128,128]{2,1,0:T(8,128)(2,1)S(1)} collective-permute-done((bf16[1,128,128]{2,1,0:T(8,128)(2,1)S(1)}, bf16[1,128,128]{2,1,0:T(8,128)(2,1)S(1)}, u32[]{:S(2)}, u32[]{:S(2)}) %collective-permute-start.20) | collective-permute-done | bytes 32800 | tf_op jit(solution)/shard_map/ppermute | solution.py:174
  44.4 1.2 %collective-permute-done.21 = bf16[1,128,128]{2,1,0:T(8,128)(2,1)S(1)} collective-permute-done((bf16[1,128,128]{2,1,0:T(8,128)(2,1)S(1)}, bf16[1,128,128]{2,1,0:T(8,128)(2,1)S(1)}, u32[]{:S(2)}, u32[]{:S(2)}) %collective-permute-start.21) | collective-permute-done | bytes 32800 | tf_op jit(solution)/shard_map/ppermute | solution.py:174
  45.6 2.3 %collective-permute-start.25 = (bf16[4,128,128]{2,1,0:T(8,128)(2,1)S(1)}, bf16[4,128,128]{2,1,0:T(8,128)(2,1)S(1)}, u32[]{:S(2)}, u32[]{:S(2)}) collective-permute-start(bf16[4,128,128]{2,1,0:T(8,128)(2,1)S(1)} %pad_maximum_fusion.2.refs_0_), channel_id=1, source_target_pairs={{0,5},{1,4},{2,7},{3,6},{4,1},{5,0},{6,3},{7,2},{8,13},{9,12},{10,... | collective-permute-start | bytes 393224 | tf_op jit(solution)/shard_map/ppermute | solution.py:174
  48.0 1.1 %collective-permute-start.23 = (bf16[4,128,128]{2,1,0:T(8,128)(2,1)S(1)}, bf16[4,128,128]{2,1,0:T(8,128)(2,1)S(1)}, u32[]{:S(2)}, u32[]{:S(2)}) collective-permute-start(bf16[4,128,128]{2,1,0:T(8,128)(2,1)S(1)} %pad_maximum_fusion.2.refs_0_), channel_id=1, source_target_pairs={{0,1},{1,0},{2,3},{3,2},{4,5},{5,4},{6,7},{7,6},{8,9},{9,8},{10,11... | collective-permute-start | bytes 393224 | tf_op jit(solution)/shard_map/ppermute | solution.py:174
  49.2 3.6 %collective-permute-done.25.refs_1_ = bf16[4,128,128]{2,1,0:T(8,128)(2,1)S(1)} collective-permute-done((bf16[4,128,128]{2,1,0:T(8,128)(2,1)S(1)}, bf16[4,128,128]{2,1,0:T(8,128)(2,1)S(1)}, u32[]{:S(2)}, u32[]{:S(2)}) %collective-permute-start.25) | collective-permute-done | bytes 131104 | tf_op jit(solution)/shard_map/ppermute | solution.py:174
  52.8 0.9 %collective-permute-done.26.refs_2_ = bf16[4,128,128]{2,1,0:T(8,128)(2,1)S(1)} collective-permute-done((bf16[4,128,128]{2,1,0:T(8,128)(2,1)S(1)}, bf16[4,128,128]{2,1,0:T(8,128)(2,1)S(1)}, u32[]{:S(2)}, u32[]{:S(2)}) %collective-permute-start.26) | collective-permute-done | bytes 131104 | tf_op jit(solution)/shard_map/ppermute | solution.py:174
  54.2 0.8 %collective-permute-done.29.refs_6_ = bf16[4,128,128]{2,1,0:T(8,128)(2,1)S(1)} collective-permute-done((bf16[4,128,128]{2,1,0:T(8,128)(2,1)S(1)}, bf16[4,128,128]{2,1,0:T(8,128)(2,1)S(1)}, u32[]{:S(2)}, u32[]{:S(2)}) %collective-permute-start.29) | collective-permute-done | bytes 131104 | tf_op jit(solution)/shard_map/ppermute | solution.py:174
  55.0 0.6 %partial.5.partial_ref = f32[128,128]{1,0:T(8,128)S(1)} custom-call(bf16[32,256,128]{2,1,0:T(8,128)(2,1)S(1)} %presum.1.adj_ref, bf16[4,128,128]{2,1,0:T(8,128)(2,1)S(1)} %pad_maximum_fusion.2.refs_0_, bf16[4,128,128]{2,1,0:T(8,128)(2,1)S(1)} %collective-permute-done.25.refs_1_, bf16[4,128,128]{2,1,0:T(8,128)(2,1)S(1)} %collective-permute-done.26.refs_2_, ...), custom_call_target="tpu_custom_call" | custom-call | flops 234881024 | bytes 1835008 | tf_op jit(solution)/shard_map/partial/pallas_call | solution.py:155
  55.7 0.9 %last.5 = bf16[128,128]{1,0:T(8,128)(2,1)} custom-call(bf16[32,256,128]{2,1,0:T(8,128)(2,1)S(1)} %presum.1.adj_ref, bf16[4,128,128]{2,1,0:T(8,128)(2,1)S(1)} %collective-permute-done.24.part_ref, f32[128,128]{1,0:T(8,128)S(1)} %partial.5.partial_ref, bf16[128,128]{1,0:T(8,128)(2,1)S(1)} %last.4.own_ref, f32[3,128]{1,0:T(4,128)S(1)} %copy-done), custom_call_target="tpu_custom_call" | custom-call | tf_op jit(solution)/shard_map/last/pallas_call | solution.py:165
  (41 shorter events, 4.5 us)
Async XLA Ops:
  0.0 20.3 %copy-start = (f32[3,128]{1,0:T(4,128)S(1)}, f32[3,128]{1,0:T(4,128)}, u32[]{:S(2)}) copy-start(f32[3,128]{1,0:T(4,128)} %gain_ref.5) | copy-start | bytes 4612
  0.0 7.2 %collective-permute-start = (bf16[1,128,128]{2,1,0:T(8,128)(2,1)}, bf16[1,128,128]{2,1,0:T(8,128)(2,1)S(1)}, u32[]{:S(2)}, u32[]{:S(2)}) collective-permute-start(bf16[1,128,128]{2,1,0:T(8,128)(2,1)} %bitcast.15), channel_id=1, source_target_pairs={{0,24},{1,25},{2,26},{3,27},{4,28},{5,29},{6,30},{7,31},{8,16},{9,... | collective-permute-start | bytes 98312 | tf_op jit(solution)/shard_map/ppermute | solution.py:174
  5.1 5.0 %collective-permute-start.1 = (bf16[1,128,128]{2,1,0:T(8,128)(2,1)}, bf16[1,128,128]{2,1,0:T(8,128)(2,1)S(1)}, u32[]{:S(2)}, u32[]{:S(2)}) collective-permute-start(bf16[1,128,128]{2,1,0:T(8,128)(2,1)} %bitcast.16), channel_id=1, source_target_pairs={{0,16},{1,17},{2,18},{3,19},{4,20},{5,21},{6,22},{7,23},{8,24},{9,... | collective-permute-start | bytes 98312 | tf_op jit(solution)/shard_map/ppermute | solution.py:174
  5.1 5.0 %collective-permute-start.2 = (bf16[1,128,128]{2,1,0:T(8,128)(2,1)}, bf16[1,128,128]{2,1,0:T(8,128)(2,1)S(1)}, u32[]{:S(2)}, u32[]{:S(2)}) collective-permute-start(bf16[1,128,128]{2,1,0:T(8,128)(2,1)} %bitcast.17), channel_id=1, source_target_pairs={{0,8},{1,9},{2,10},{3,11},{4,12},{5,13},{6,14},{7,15},{8,0},{9,1},... | collective-permute-start | bytes 98312 | tf_op jit(solution)/shard_map/ppermute | solution.py:174
  10.1 6.7 %collective-permute-start.3 = (bf16[4,128,128]{2,1,0:T(8,128)(2,1)S(1)}, bf16[4,128,128]{2,1,0:T(8,128)(2,1)S(1)}, u32[]{:S(2)}, u32[]{:S(2)}) collective-permute-start(bf16[4,128,128]{2,1,0:T(8,128)(2,1)S(1)} %pad_maximum_fusion.refs_0_), channel_id=1, source_target_pairs={{0,5},{1,4},{2,7},{3,6},{4,1},{5,0},{6,3},{7,2},{8,13},{9,12},{10,... | collective-permute-start | bytes 393224 | tf_op jit(solution)/shard_map/ppermute | solution.py:174
  12.6 5.1 %collective-permute-start.4 = (bf16[4,128,128]{2,1,0:T(8,128)(2,1)S(1)}, bf16[4,128,128]{2,1,0:T(8,128)(2,1)S(1)}, u32[]{:S(2)}, u32[]{:S(2)}) collective-permute-start(bf16[4,128,128]{2,1,0:T(8,128)(2,1)S(1)} %pad_maximum_fusion.refs_0_), channel_id=1, source_target_pairs={{0,4},{1,5},{2,6},{3,7},{4,0},{5,1},{6,2},{7,3},{8,12},{9,13},{10,... | collective-permute-start | bytes 393224 | tf_op jit(solution)/shard_map/ppermute | solution.py:174
  13.2 5.0 %collective-permute-start.5 = (bf16[4,128,128]{2,1,0:T(8,128)(2,1)S(1)}, bf16[4,128,128]{2,1,0:T(8,128)(2,1)S(1)}, u32[]{:S(2)}, u32[]{:S(2)}) collective-permute-start(bf16[4,128,128]{2,1,0:T(8,128)(2,1)S(1)} %pad_maximum_fusion.refs_0_), channel_id=1, source_target_pairs={{0,1},{1,0},{2,3},{3,2},{4,5},{5,4},{6,7},{7,6},{8,9},{9,8},{10,11... | collective-permute-start | bytes 393224 | tf_op jit(solution)/shard_map/ppermute | solution.py:174
  16.7 1.9 %collective-permute-start.7 = (bf16[4,128,128]{2,1,0:T(8,128)(2,1)S(1)}, bf16[4,128,128]{2,1,0:T(8,128)(2,1)S(1)}, u32[]{:S(2)}, u32[]{:S(2)}) collective-permute-start(bf16[4,128,128]{2,1,0:T(8,128)(2,1)S(1)} %pad_maximum_fusion.refs_0_), channel_id=1, source_target_pairs={{0,2},{1,3},{2,0},{3,1},{4,6},{5,7},{6,4},{7,5},{8,10},{9,11},{10,... | collective-permute-start | bytes 393224 | tf_op jit(solution)/shard_map/ppermute | solution.py:174
  18.1 1.3 %collective-permute-start.8 = (bf16[4,128,128]{2,1,0:T(8,128)(2,1)S(1)}, bf16[4,128,128]{2,1,0:T(8,128)(2,1)S(1)}, u32[]{:S(2)}, u32[]{:S(2)}) collective-permute-start(bf16[4,128,128]{2,1,0:T(8,128)(2,1)S(1)} %collective-permute-done.3.refs_1_), channel_id=1, source_target_pairs={{0,2},{1,3},{2,0},{3,1},{4,6},{5,7},{6,4},{7,5},{8,10},{9,11},{10,... | collective-permute-start | bytes 393224 | tf_op jit(solution)/shard_map/ppermute | solution.py:174
  18.2 1.5 %collective-permute-start.9 = (bf16[4,128,128]{2,1,0:T(8,128)(2,1)S(1)}, bf16[4,128,128]{2,1,0:T(8,128)(2,1)S(1)}, u32[]{:S(2)}, u32[]{:S(2)}) collective-permute-start(bf16[4,128,128]{2,1,0:T(8,128)(2,1)S(1)} %collective-permute-done.4.refs_2_), channel_id=1, source_target_pairs={{0,2},{1,3},{2,0},{3,1},{4,6},{5,7},{6,4},{7,5},{8,10},{9,11},{10,... | collective-permute-start | bytes 393224 | tf_op jit(solution)/shard_map/ppermute | solution.py:174
  18.7 1.7 %collective-permute-start.6 = (bf16[4,128,128]{2,1,0:T(8,128)(2,1)S(1)}, bf16[4,128,128]{2,1,0:T(8,128)(2,1)S(1)}, u32[]{:S(2)}, u32[]{:S(2)}) collective-permute-start(bf16[4,128,128]{2,1,0:T(8,128)(2,1)S(1)} %collective-permute-done.5.refs_3_), channel_id=1, source_target_pairs={{0,2},{1,3},{2,0},{3,1},{4,6},{5,7},{6,4},{7,5},{8,10},{9,11},{10,... | collective-permute-start | bytes 393224 | tf_op jit(solution)/shard_map/ppermute | solution.py:174
  20.6 6.0 %collective-permute-start.10 = (bf16[1,128,128]{2,1,0:T(8,128)(2,1)S(1)}, bf16[1,128,128]{2,1,0:T(8,128)(2,1)S(1)}, u32[]{:S(2)}, u32[]{:S(2)}) collective-permute-start(bf16[1,128,128]{2,1,0:T(8,128)(2,1)S(1)} %bitcast.9), channel_id=1, source_target_pairs={{0,24},{1,25},{2,26},{3,27},{4,28},{5,29},{6,30},{7,31},{8,16},{9,... | collective-permute-start | bytes 98312 | tf_op jit(solution)/shard_map/ppermute | solution.py:174
  22.2 4.9 %collective-permute-start.11 = (bf16[1,128,128]{2,1,0:T(8,128)(2,1)S(1)}, bf16[1,128,128]{2,1,0:T(8,128)(2,1)S(1)}, u32[]{:S(2)}, u32[]{:S(2)}) collective-permute-start(bf16[1,128,128]{2,1,0:T(8,128)(2,1)S(1)} %bitcast.10), channel_id=1, source_target_pairs={{0,16},{1,17},{2,18},{3,19},{4,20},{5,21},{6,22},{7,23},{8,24},{9,... | collective-permute-start | bytes 98312 | tf_op jit(solution)/shard_map/ppermute | solution.py:174
  22.8 4.7 %collective-permute-start.12 = (bf16[1,128,128]{2,1,0:T(8,128)(2,1)S(1)}, bf16[1,128,128]{2,1,0:T(8,128)(2,1)S(1)}, u32[]{:S(2)}, u32[]{:S(2)}) collective-permute-start(bf16[1,128,128]{2,1,0:T(8,128)(2,1)S(1)} %bitcast.11), channel_id=1, source_target_pairs={{0,8},{1,9},{2,10},{3,11},{4,12},{5,13},{6,14},{7,15},{8,0},{9,1},... | collective-permute-start | bytes 98312 | tf_op jit(solution)/shard_map/ppermute | solution.py:174
  27.6 7.3 %collective-permute-start.15 = (bf16[4,128,128]{2,1,0:T(8,128)(2,1)S(1)}, bf16[4,128,128]{2,1,0:T(8,128)(2,1)S(1)}, u32[]{:S(2)}, u32[]{:S(2)}) collective-permute-start(bf16[4,128,128]{2,1,0:T(8,128)(2,1)S(1)} %pad_maximum_fusion.1.refs_0_), channel_id=1, source_target_pairs={{0,5},{1,4},{2,7},{3,6},{4,1},{5,0},{6,3},{7,2},{8,13},{9,12},{10,... | collective-permute-start | bytes 393224 | tf_op jit(solution)/shard_map/ppermute | solution.py:174
  30.3 6.0 %collective-permute-start.16 = (bf16[4,128,128]{2,1,0:T(8,128)(2,1)S(1)}, bf16[4,128,128]{2,1,0:T(8,128)(2,1)S(1)}, u32[]{:S(2)}, u32[]{:S(2)}) collective-permute-start(bf16[4,128,128]{2,1,0:T(8,128)(2,1)S(1)} %pad_maximum_fusion.1.refs_0_), channel_id=1, source_target_pairs={{0,4},{1,5},{2,6},{3,7},{4,0},{5,1},{6,2},{7,3},{8,12},{9,13},{10,... | collective-permute-start | bytes 393224 | tf_op jit(solution)/shard_map/ppermute | solution.py:174
  30.4 6.2 %collective-permute-start.13 = (bf16[4,128,128]{2,1,0:T(8,128)(2,1)S(1)}, bf16[4,128,128]{2,1,0:T(8,128)(2,1)S(1)}, u32[]{:S(2)}, u32[]{:S(2)}) collective-permute-start(bf16[4,128,128]{2,1,0:T(8,128)(2,1)S(1)} %pad_maximum_fusion.1.refs_0_), channel_id=1, source_target_pairs={{0,1},{1,0},{2,3},{3,2},{4,5},{5,4},{6,7},{7,6},{8,9},{9,8},{10,11... | collective-permute-start | bytes 393224 | tf_op jit(solution)/shard_map/ppermute | solution.py:174
  31.1 5.7 %collective-permute-start.17 = (bf16[4,128,128]{2,1,0:T(8,128)(2,1)S(1)}, bf16[4,128,128]{2,1,0:T(8,128)(2,1)S(1)}, u32[]{:S(2)}, u32[]{:S(2)}) collective-permute-start(bf16[4,128,128]{2,1,0:T(8,128)(2,1)S(1)} %pad_maximum_fusion.1.refs_0_), channel_id=1, source_target_pairs={{0,2},{1,3},{2,0},{3,1},{4,6},{5,7},{6,4},{7,5},{8,10},{9,11},{10,... | collective-permute-start | bytes 393224 | tf_op jit(solution)/shard_map/ppermute | solution.py:174
  34.9 1.9 %collective-permute-start.18 = (bf16[4,128,128]{2,1,0:T(8,128)(2,1)S(1)}, bf16[4,128,128]{2,1,0:T(8,128)(2,1)S(1)}, u32[]{:S(2)}, u32[]{:S(2)}) collective-permute-start(bf16[4,128,128]{2,1,0:T(8,128)(2,1)S(1)} %collective-permute-done.15.refs_1_), channel_id=1, source_target_pairs={{0,2},{1,3},{2,0},{3,1},{4,6},{5,7},{6,4},{7,5},{8,10},{9,11},{10,... | collective-permute-start | bytes 393224 | tf_op jit(solution)/shard_map/ppermute | solution.py:174
  36.3 1.3 %collective-permute-start.19 = (bf16[4,128,128]{2,1,0:T(8,128)(2,1)S(1)}, bf16[4,128,128]{2,1,0:T(8,128)(2,1)S(1)}, u32[]{:S(2)}, u32[]{:S(2)}) collective-permute-start(bf16[4,128,128]{2,1,0:T(8,128)(2,1)S(1)} %collective-permute-done.16.refs_2_), channel_id=1, source_target_pairs={{0,2},{1,3},{2,0},{3,1},{4,6},{5,7},{6,4},{7,5},{8,10},{9,11},{10,... | collective-permute-start | bytes 393224 | tf_op jit(solution)/shard_map/ppermute | solution.py:174
  36.7 1.6 %collective-permute-start.14 = (bf16[4,128,128]{2,1,0:T(8,128)(2,1)S(1)}, bf16[4,128,128]{2,1,0:T(8,128)(2,1)S(1)}, u32[]{:S(2)}, u32[]{:S(2)}) collective-permute-start(bf16[4,128,128]{2,1,0:T(8,128)(2,1)S(1)} %collective-permute-done.13.refs_3_), channel_id=1, source_target_pairs={{0,2},{1,3},{2,0},{3,1},{4,6},{5,7},{6,4},{7,5},{8,10},{9,11},{10,... | collective-permute-start | bytes 393224 | tf_op jit(solution)/shard_map/ppermute | solution.py:174
  38.6 5.8 %collective-permute-start.20 = (bf16[1,128,128]{2,1,0:T(8,128)(2,1)S(1)}, bf16[1,128,128]{2,1,0:T(8,128)(2,1)S(1)}, u32[]{:S(2)}, u32[]{:S(2)}) collective-permute-start(bf16[1,128,128]{2,1,0:T(8,128)(2,1)S(1)} %bitcast.5), channel_id=1, source_target_pairs={{0,24},{1,25},{2,26},{3,27},{4,28},{5,29},{6,30},{7,31},{8,16},{9,... | collective-permute-start | bytes 98312 | tf_op jit(solution)/shard_map/ppermute | solution.py:174
  40.8 4.8 %collective-permute-start.21 = (bf16[1,128,128]{2,1,0:T(8,128)(2,1)S(1)}, bf16[1,128,128]{2,1,0:T(8,128)(2,1)S(1)}, u32[]{:S(2)}, u32[]{:S(2)}) collective-permute-start(bf16[1,128,128]{2,1,0:T(8,128)(2,1)S(1)} %bitcast.6), channel_id=1, source_target_pairs={{0,16},{1,17},{2,18},{3,19},{4,20},{5,21},{6,22},{7,23},{8,24},{9,... | collective-permute-start | bytes 98312 | tf_op jit(solution)/shard_map/ppermute | solution.py:174
  40.8 4.8 %collective-permute-start.22 = (bf16[1,128,128]{2,1,0:T(8,128)(2,1)S(1)}, bf16[1,128,128]{2,1,0:T(8,128)(2,1)S(1)}, u32[]{:S(2)}, u32[]{:S(2)}) collective-permute-start(bf16[1,128,128]{2,1,0:T(8,128)(2,1)S(1)} %bitcast.7), channel_id=1, source_target_pairs={{0,8},{1,9},{2,10},{3,11},{4,12},{5,13},{6,14},{7,15},{8,0},{9,1},... | collective-permute-start | bytes 98312 | tf_op jit(solution)/shard_map/ppermute | solution.py:174
  45.6 7.2 %collective-permute-start.25 = (bf16[4,128,128]{2,1,0:T(8,128)(2,1)S(1)}, bf16[4,128,128]{2,1,0:T(8,128)(2,1)S(1)}, u32[]{:S(2)}, u32[]{:S(2)}) collective-permute-start(bf16[4,128,128]{2,1,0:T(8,128)(2,1)S(1)} %pad_maximum_fusion.2.refs_0_), channel_id=1, source_target_pairs={{0,5},{1,4},{2,7},{3,6},{4,1},{5,0},{6,3},{7,2},{8,13},{9,12},{10,... | collective-permute-start | bytes 393224 | tf_op jit(solution)/shard_map/ppermute | solution.py:174
  47.9 5.8 %collective-permute-start.26 = (bf16[4,128,128]{2,1,0:T(8,128)(2,1)S(1)}, bf16[4,128,128]{2,1,0:T(8,128)(2,1)S(1)}, u32[]{:S(2)}, u32[]{:S(2)}) collective-permute-start(bf16[4,128,128]{2,1,0:T(8,128)(2,1)S(1)} %pad_maximum_fusion.2.refs_0_), channel_id=1, source_target_pairs={{0,4},{1,5},{2,6},{3,7},{4,0},{5,1},{6,2},{7,3},{8,12},{9,13},{10,... | collective-permute-start | bytes 393224 | tf_op jit(solution)/shard_map/ppermute | solution.py:174
  48.0 6.1 %collective-permute-start.23 = (bf16[4,128,128]{2,1,0:T(8,128)(2,1)S(1)}, bf16[4,128,128]{2,1,0:T(8,128)(2,1)S(1)}, u32[]{:S(2)}, u32[]{:S(2)}) collective-permute-start(bf16[4,128,128]{2,1,0:T(8,128)(2,1)S(1)} %pad_maximum_fusion.2.refs_0_), channel_id=1, source_target_pairs={{0,1},{1,0},{2,3},{3,2},{4,5},{5,4},{6,7},{7,6},{8,9},{9,8},{10,11... | collective-permute-start | bytes 393224 | tf_op jit(solution)/shard_map/ppermute | solution.py:174
  49.2 5.0 %collective-permute-start.27 = (bf16[4,128,128]{2,1,0:T(8,128)(2,1)S(1)}, bf16[4,128,128]{2,1,0:T(8,128)(2,1)S(1)}, u32[]{:S(2)}, u32[]{:S(2)}) collective-permute-start(bf16[4,128,128]{2,1,0:T(8,128)(2,1)S(1)} %pad_maximum_fusion.2.refs_0_), channel_id=1, source_target_pairs={{0,2},{1,3},{2,0},{3,1},{4,6},{5,7},{6,4},{7,5},{8,10},{9,11},{10,... | collective-permute-start | bytes 393224 | tf_op jit(solution)/shard_map/ppermute | solution.py:174
  52.8 1.4 %collective-permute-start.28 = (bf16[4,128,128]{2,1,0:T(8,128)(2,1)S(1)}, bf16[4,128,128]{2,1,0:T(8,128)(2,1)S(1)}, u32[]{:S(2)}, u32[]{:S(2)}) collective-permute-start(bf16[4,128,128]{2,1,0:T(8,128)(2,1)S(1)} %collective-permute-done.25.refs_1_), channel_id=1, source_target_pairs={{0,2},{1,3},{2,0},{3,1},{4,6},{5,7},{6,4},{7,5},{8,10},{9,11},{10,... | collective-permute-start | bytes 393224 | tf_op jit(solution)/shard_map/ppermute | solution.py:174
  53.7 1.3 %collective-permute-start.29 = (bf16[4,128,128]{2,1,0:T(8,128)(2,1)S(1)}, bf16[4,128,128]{2,1,0:T(8,128)(2,1)S(1)}, u32[]{:S(2)}, u32[]{:S(2)}) collective-permute-start(bf16[4,128,128]{2,1,0:T(8,128)(2,1)S(1)} %collective-permute-done.26.refs_2_), channel_id=1, source_target_pairs={{0,2},{1,3},{2,0},{3,1},{4,6},{5,7},{6,4},{7,5},{8,10},{9,11},{10,... | collective-permute-start | bytes 393224 | tf_op jit(solution)/shard_map/ppermute | solution.py:174
  54.2 1.5 %collective-permute-start.24 = (bf16[4,128,128]{2,1,0:T(8,128)(2,1)S(1)}, bf16[4,128,128]{2,1,0:T(8,128)(2,1)S(1)}, u32[]{:S(2)}, u32[]{:S(2)}) collective-permute-start(bf16[4,128,128]{2,1,0:T(8,128)(2,1)S(1)} %collective-permute-done.23.refs_3_), channel_id=1, source_target_pairs={{0,2},{1,3},{2,0},{3,1},{4,6},{5,7},{6,4},{7,5},{8,10},{9,11},{10,... | collective-permute-start | bytes 393224 | tf_op jit(solution)/shard_map/ppermute | solution.py:174

commit v3 on v2

v3 whole, which is shorter than its diff:
```python
import functools

import jax
import jax.numpy as jnp
from jax import lax
from jax.experimental import pallas as pl
from jax.experimental.pallas import tpu as pltpu
from jax.sharding import PartitionSpec as P

epsilon = 1e-05
AXES = ("blk", "col")
CHUNK = 8


def moved(index, spots):
    result = 0
    for b, spot in enumerate(spots):
        result = result ^ (((index >> b) & 1) * spot)
    return result


def add_tiles(count, cols_hbm, tiles_hbm, cols_ref, buf, accs, sems, window, meanwhile, devices, spots):
    first, stop = window
    half = accs[0].shape[2]
    total = devices[0] * devices[1]
    chunks = (stop - first) // CHUNK
    me = moved(lax.axis_index("blk") * devices[1] + lax.axis_index("col"), spots)
    cols_copy = pltpu.make_async_copy(cols_hbm, cols_ref, sems.at[chunks])

    def copy(c):
        return pltpu.make_async_copy(
            tiles_hbm.at[pl.ds(first + c * CHUNK, CHUNK)], buf.at[pl.ds(c * CHUNK, CHUNK)], sems.at[c]
        )

    cols_copy.start()
    for c in range(chunks):
        @pl.when(first + c * CHUNK < count)
        def _():
            copy(c).start()

    meanwhile()
    cols_copy.wait()

    def chunk_body(c, carry):
        @pl.when(first + c * CHUNK < count)
        def _():
            copy(c).wait()
            for t in range(CHUNK):
                acc = accs[t % len(accs)]
                place = c * CHUNK + t
                slot = first + place
                left = me ^ moved(cols_ref[0, slot] * 2, spots)
                right = left ^ spots[0]
                left = jnp.where(slot < count, left, total)
                right = jnp.where(slot < count, right, total + 1)
                acc[left] = acc[left] + buf[place, :, :half].astype(jnp.float32)
                acc[right] = acc[right] + buf[place, :, half:].astype(jnp.float32)
        return carry

    lax.fori_loop(0, chunks, chunk_body, 0)


def begin_kernel(count_ref, cols_hbm, tiles_hbm, own_hbm, *rest, ways, **fixed):
    own_ref, accs = rest[0], rest[1 : 1 + ways]
    cols_ref, buf, sems = rest[1 + ways :]
    own_copy = pltpu.make_async_copy(own_hbm, own_ref, sems.at[sems.shape[0] - 1])
    own_copy.start()

    def clear():
        def body(i, carry):
            for acc in accs:
                acc[i] = jnp.zeros(acc.shape[1:], jnp.float32)
            return carry

        lax.fori_loop(0, accs[0].shape[0], body, 0)

    add_tiles(count_ref[0], cols_hbm, tiles_hbm, cols_ref, buf, accs, sems, meanwhile=clear, **fixed)
    own_copy.wait()


def finish_kernel(count_ref, cols_hbm, tiles_hbm, *rest, ways, **fixed):
    out_ref, accs = rest[ways], rest[ways + 1 : 2 * ways + 1]
    cols_ref, buf, sems = rest[2 * ways + 1 :]
    rows = accs[0].shape[1]
    add_tiles(count_ref[0], cols_hbm, tiles_hbm, cols_ref, buf, accs, sems, meanwhile=lambda: None, **fixed)

    def body(i, carry):
        summed = sum(acc[i] for acc in accs)
        high = summed.astype(jnp.bfloat16)
        out_ref[i, :rows] = high
        out_ref[i, rows:] = (summed - high.astype(jnp.float32)).astype(jnp.bfloat16)
        return carry

    lax.fori_loop(0, out_ref.shape[0], body, 0)


def limit(scratch):
    return pltpu.CompilerParams(vmem_limit_bytes=scratch + 4 * 2**20)


def fast(value):
    return pltpu.with_memory_space_constraint(value, pltpu.VMEM)


def slow(value):
    return pltpu.with_memory_space_constraint(value, pltpu.HBM)


def split(slots):
    return slots * 2 // (8 * CHUNK) * CHUNK


def scratch_of(tiles, length):
    slots, rows, width = tiles.shape
    return [
        pltpu.SMEM((1, slots), jnp.int32),
        pltpu.VMEM((length, rows, width), jnp.bfloat16),
        pltpu.SemaphoreType.DMA((length // CHUNK + 2,)),
    ]


def cost_of(tiles, length):
    _, rows, width = tiles.shape
    size = length * rows * width
    return pl.CostEstimate(flops=size * 8, bytes_accessed=size * 2, transcendentals=0)


def begin(tiles, cols, count, own, devices, spots):
    slots, rows, width = tiles.shape
    total = devices[0] * devices[1]
    ways = 2 if total <= 64 else 1
    length = split(slots)
    memory = [pltpu.SMEM, pltpu.HBM, pltpu.HBM, pltpu.HBM]
    own, *accs = pl.pallas_call(
        functools.partial(begin_kernel, ways=ways, window=(0, length), devices=devices, spots=spots),
        out_shape=[pltpu.VMEM(own.shape, own.dtype)] + [pltpu.VMEM((total + 2, rows, width // 2), jnp.float32)] * ways,
        in_specs=[pl.BlockSpec(memory_space=space) for space in memory],
        out_specs=[pl.BlockSpec(memory_space=pltpu.VMEM)] * (1 + ways),
        scratch_shapes=scratch_of(tiles, length),
        cost_estimate=cost_of(tiles, length),
        compiler_params=limit(length * rows * width * 2),
        name="begin",
    )(count, slow(cols), slow(tiles), slow(own))
    return own, accs


def finish(tiles, cols, count, accs, devices, spots):
    slots, rows, width = tiles.shape
    total = devices[0] * devices[1]
    ways = len(accs)
    length = slots - split(slots)
    memory = [pltpu.SMEM, pltpu.HBM, pltpu.HBM] + [pltpu.VMEM] * ways
    return pl.pallas_call(
        functools.partial(finish_kernel, ways=ways, window=(split(slots), slots), devices=devices, spots=spots),
        out_shape=[pltpu.VMEM((total, 2 * rows, width // 2), jnp.bfloat16)] + [pltpu.VMEM(acc.shape, acc.dtype) for acc in accs],
        in_specs=[pl.BlockSpec(memory_space=space) for space in memory],
        out_specs=[pl.BlockSpec(memory_space=pltpu.VMEM)] * (1 + ways),
        input_output_aliases={3 + j: 1 + j for j in range(ways)},
        scratch_shapes=scratch_of(tiles, length),
        cost_estimate=cost_of(tiles, length),
        compiler_params=limit(length * rows * width * 2),
        name="finish",
    )(count, slow(cols), slow(tiles), *[fast(acc) for acc in accs])[0]


def product(adj_ref, spots, parts):
    total = None
    for spot, part in zip(spots, parts):
        blocks, rows, width = part.shape
        adj = jnp.concatenate([adj_ref[spot + j] for j in range(blocks)], axis=1)
        term = jnp.dot(adj, part[...].reshape(blocks * rows, width), preferred_element_type=jnp.float32)
        total = term if total is None else total + term
    rows = total.shape[0] // 2
    return total[:rows] + total[rows:]


def partial_kernel(adj_ref, *refs, spots):
    refs[-1][...] = product(adj_ref, spots, refs[:-1])


def last_kernel(adj_ref, partial_ref, own_ref, gain_ref, *refs, spots, hop):
    parts, out_ref = refs[:-1], refs[-1]
    summed = product(adj_ref, spots, parts) + partial_ref[...] + own_ref[...].astype(jnp.float32)
    mean_sq = jnp.mean(summed * summed, axis=1, keepdims=True)
    scaled = summed * lax.rsqrt(mean_sq + epsilon) * gain_ref[hop : hop + 1, :]
    out_ref[...] = scaled.astype(jnp.bfloat16)


def partial_sum(adj, spots, parts):
    rows = adj.shape[1] // 2
    width = parts[0].shape[2]
    depth = sum(part.shape[0] for part in parts) * rows
    return pl.pallas_call(
        functools.partial(partial_kernel, spots=spots),
        out_shape=pltpu.VMEM((rows, width), jnp.float32),
        compiler_params=limit(0),
        cost_estimate=pl.CostEstimate(flops=4 * rows * depth * width, bytes_accessed=depth * width * 4, transcendentals=0),
        name="partial",
    )(fast(adj), *[fast(part) for part in parts])


def last(adj, parts, partial, own, gain, spots, hop, final):
    return pl.pallas_call(
        functools.partial(last_kernel, spots=spots, hop=hop),
        out_shape=jax.ShapeDtypeStruct(own.shape, own.dtype) if final else pltpu.VMEM(own.shape, own.dtype),
        compiler_params=limit(0),
        name="last",
    )(fast(adj), fast(partial), fast(own), fast(gain), *[fast(part) for part in parts])


def exchange(value, mask, total):
    return lax.ppermute(value, AXES, [(i, i ^ mask) for i in range(total)])


def masks_of(group, closing):
    if len(group) == 1:
        return [1 << group[0]]
    high, low = 1 << group[0], 1 << group[1]
    return [high | low, high, low] if closing else [high, high | low, low]


def stages(devices):
    bits = (devices[0] * devices[1]).bit_length() - 1
    core_bit = devices[1].bit_length() - 1
    line = [b for b in range(bits) if b != core_bit][::-1]
    groups = [line[i : i + 2] for i in range(0, len(line), 2)]
    spots = [0] * bits
    size = 1
    for group in groups:
        for place, mask in enumerate(masks_of(group, group is groups[-1])):
            if mask & (mask - 1) == 0:
                spots[mask.bit_length() - 1] = size * (place + 1)
        size <<= len(group)
    spots[core_bit] = size
    return groups, core_bit, spots


def solution(mesh):
    devices = (mesh.shape["blk"], mesh.shape["col"])
    total = devices[0] * devices[1]
    groups, core_bit, spots = stages(devices)

    def shards(features, tile_vals, tile_cols, tile_count, norm_gain):
        current = features
        for hop in range(norm_gain.shape[0]):
            held = current[None]
            if hop == 0:
                current, accs = begin(tile_vals[0], tile_cols, tile_count, features, devices, spots)
            for group in groups:
                received = [exchange(held, mask, total) for mask in masks_of(group, group is groups[-1])]
                if hop == 0 and group is groups[0]:
                    received, accs = lax.optimization_barrier((received, accs))
                    adj = finish(tile_vals[0], tile_cols, tile_count, accs, devices, spots)
                parts = [current[None] if group is groups[0] else held, *received]
                if group is not groups[-1]:
                    held = jnp.concatenate(parts, axis=0)
            if hop == 0:
                *received, adj = lax.optimization_barrier((*parts[1:], adj))
                parts = [parts[0], *received]
            others = [exchange(part, 1 << core_bit, total) for part in parts]
            size = parts[0].shape[0]
            near = [j * size for j in range(len(parts))]
            far = [total // 2 + spot for spot in near]
            partial = partial_sum(adj, near + far[:-3], parts + others[:-3])
            final = hop + 1 == norm_gain.shape[0]
            current = last(adj, others[-3:], partial, current, norm_gain, far[-3:], hop, final)
        return current

    placed = (P(AXES, None), P("blk", None, "col", None), P("blk", None), P("blk"), P())
    return jax.shard_map(shards, mesh=mesh, in_specs=placed, out_specs=P(AXES, None), check_vma=False)
```

time: 56.9 us -> 54.6 us (0.960)
  starting transfers between devices: 26 us -> 24.4 us
  waiting for transfers between devices: 23.2 us -> 21.7 us
  Pallas kernels: 6.58 us -> 7.55 us
    ppermute x30, starting transfers between devices: 26 us -> 24.4 us  [exchange(): return lax.ppermute(value, AXES, [(i, i ^ mask) for i in range(total)])]
    ppermute x30, waiting for transfers between devices: 23.2 us -> 21.7 us  [exchange(): return lax.ppermute(value, AXES, [(i, i ^ mask) for i in range(total)])]
    pallas_call x5, Pallas kernels: 4.69 us -> 6.06 us  [the longest x1 2.42 us: finish(): pl.pallas_call(functools.partial(finish_kernel, ways=ways, window=(split(...]
  transfers between devices with their start and end apart: 30 -> 30, of which waited for: 19 -> 21; matrix products, arithmetic and copies ran while one was open for 0% -> 0% of each run, Pallas kernels for 9% -> 10%
where the time goes in v3:
time: 54.6 us; the launch traced here: 54.5 us
  starting transfers between devices  24.4 us (45%)
  waiting for transfers between devices  21.7 us (40%)
  Pallas kernels  7.55 us (14%)
  between operations  0.77 us (1%)
    ppermute x30, starting transfers between devices, exchange(): return lax.ppermute(value, AXES, [(i, i ^ mask) for i in range(total)])  24.4 us
    ppermute x30, waiting for transfers between devices, exchange(): return lax.ppermute(value, AXES, [(i, i ^ mask) for i in range(total)])  21.7 us
    pallas_call x1, Pallas kernels, finish(): pl.pallas_call(functools.partial(finish_kernel, ways=ways, window=(split(...  2.42 us
    pallas_call x3, Pallas kernels, last(): pl.pallas_call(functools.partial(last_kernel, spots=spots, hop=hop), out_...  1.95 us
    pallas_call x1, Pallas kernels, begin(): pl.pallas_call(functools.partial(begin_kernel, ways=ways, window=(0, leng...  1.69 us
    pallas_call x3, Pallas kernels, partial_sum(): pl.pallas_call(functools.partial(partial_kernel, spots=spots), out_shape=...  1.49 us
  transfers between devices with their start and end apart: 30, of which 21 were waited for; matrix products, arithmetic and copies ran while one was open for 0% of the time, Pallas kernels for 10%

profile of v3, /device:TPU:0, one launch (start us, length us, event | category | flops | bytes accessed | tf_op | source)
XLA Modules:
  0.0 54.5 jit_solution(5173920476668335544)
XLA Ops:
  0.0 4.1 %collective-permute-start = (bf16[1,128,128]{2,1,0:T(8,128)(2,1)}, bf16[1,128,128]{2,1,0:T(8,128)(2,1)S(1)}, u32[]{:S(2)}, u32[]{:S(2)}) collective-permute-start(bf16[1,128,128]{2,1,0:T(8,128)(2,1)} %bitcast.16), channel_id=1, source_target_pairs={{0,16},{1,17},{2,18},{3,19},{4,20},{5,21},{6,22},{7,23},{8,24},{9,... | collective-permute-start | bytes 98312 | tf_op jit(solution)/shard_map/ppermute | solution.py:212
  4.1 1.3 %collective-permute-start.1 = (bf16[1,128,128]{2,1,0:T(8,128)(2,1)}, bf16[1,128,128]{2,1,0:T(8,128)(2,1)S(1)}, u32[]{:S(2)}, u32[]{:S(2)}) collective-permute-start(bf16[1,128,128]{2,1,0:T(8,128)(2,1)} %bitcast.17), channel_id=1, source_target_pairs={{0,24},{1,25},{2,26},{3,27},{4,28},{5,29},{6,30},{7,31},{8,16},{9,... | collective-permute-start | bytes 98312 | tf_op jit(solution)/shard_map/ppermute | solution.py:212
  6.3 1.7 %begin.1 = (bf16[128,128]{1,0:T(8,128)(2,1)S(1)}, f32[34,128,128]{2,1,0:T(8,128)S(1)}, f32[34,128,128]{2,1,0:T(8,128)S(1)}) custom-call(s32[1]{0:T(128)S(6)} %copy.10.count_ref, s32[1,128]{1,0:T(1,128)} %cols_hbm.3, bf16[128,128,256]{2,1,0:T(8,128)(2,1)} %bitcast.14, bf16[128,128]{1,0:T(8,128)(2,1)} %own_hbm.1), custom_call_target="tpu_custom_call" | custom-call | flops 8388608 | bytes 2097152 | tf_op jit(solution)/shard_map/begin/pallas_call | solution.py:134
  8.0 2.0 %collective-permute-done.1 = bf16[1,128,128]{2,1,0:T(8,128)(2,1)S(1)} collective-permute-done((bf16[1,128,128]{2,1,0:T(8,128)(2,1)}, bf16[1,128,128]{2,1,0:T(8,128)(2,1)S(1)}, u32[]{:S(2)}, u32[]{:S(2)}) %collective-permute-start.1) | collective-permute-done | bytes 32800 | tf_op jit(solution)/shard_map/ppermute | solution.py:212
  10.0 2.5 %collective-permute-start.3 = (bf16[4,128,128]{2,1,0:T(8,128)(2,1)S(1)}, bf16[4,128,128]{2,1,0:T(8,128)(2,1)S(1)}, u32[]{:S(2)}, u32[]{:S(2)}) collective-permute-start(bf16[4,128,128]{2,1,0:T(8,128)(2,1)S(1)} %pad_maximum_fusion.refs_0_), channel_id=1, source_target_pairs={{0,5},{1,4},{2,7},{3,6},{4,1},{5,0},{6,3},{7,2},{8,13},{9,12},{10,... | collective-permute-start | bytes 393224 | tf_op jit(solution)/shard_map/ppermute | solution.py:212
  12.5 0.5 collective-permute-start.4
  13.1 0.5 collective-permute-start.5
  13.6 2.4 %finish.1 = (bf16[32,256,128]{2,1,0:T(8,128)(2,1)S(1)}, f32[34,128,128]{2,1,0:T(8,128)S(1)}, f32[34,128,128]{2,1,0:T(8,128)S(1)}) custom-call(s32[1]{0:T(128)S(6)} %copy.10.count_ref, s32[1,128]{1,0:T(1,128)} %cols_hbm.3, bf16[128,128,256]{2,1,0:T(8,128)(2,1)} %bitcast.15, ...), custom_call_target="tpu_custom_call", output_to_operand_aliasing={{1}: (3, {}), {2}: (4, {})} | custom-call | flops 25165824 | bytes 6291456 | tf_op jit(solution)/shard_map/finish/pallas_call | solution.py:153
  16.3 1.4 %collective-permute-done.4.refs_2_ = bf16[4,128,128]{2,1,0:T(8,128)(2,1)S(1)} collective-permute-done((bf16[4,128,128]{2,1,0:T(8,128)(2,1)S(1)}, bf16[4,128,128]{2,1,0:T(8,128)(2,1)S(1)}, u32[]{:S(2)}, u32[]{:S(2)}) %collective-permute-start.4) | collective-permute-done | bytes 131104 | tf_op jit(solution)/shard_map/ppermute | solution.py:212
  18.0 0.5 collective-permute-start.8
  20.3 1.3 %collective-permute-start.10 = (bf16[1,128,128]{2,1,0:T(8,128)(2,1)S(1)}, bf16[1,128,128]{2,1,0:T(8,128)(2,1)S(1)}, u32[]{:S(2)}, u32[]{:S(2)}) collective-permute-start(bf16[1,128,128]{2,1,0:T(8,128)(2,1)S(1)} %bitcast.9), channel_id=1, source_target_pairs={{0,16},{1,17},{2,18},{3,19},{4,20},{5,21},{6,22},{7,23},{8,24},{9,... | collective-permute-start | bytes 98312 | tf_op jit(solution)/shard_map/ppermute | solution.py:212
  21.6 1.2 %collective-permute-start.11 = (bf16[1,128,128]{2,1,0:T(8,128)(2,1)S(1)}, bf16[1,128,128]{2,1,0:T(8,128)(2,1)S(1)}, u32[]{:S(2)}, u32[]{:S(2)}) collective-permute-start(bf16[1,128,128]{2,1,0:T(8,128)(2,1)S(1)} %bitcast.10), channel_id=1, source_target_pairs={{0,24},{1,25},{2,26},{3,27},{4,28},{5,29},{6,30},{7,31},{8,16},{9,... | collective-permute-start | bytes 98312 | tf_op jit(solution)/shard_map/ppermute | solution.py:212
  22.9 1.0 %collective-permute-start.12 = (bf16[1,128,128]{2,1,0:T(8,128)(2,1)S(1)}, bf16[1,128,128]{2,1,0:T(8,128)(2,1)S(1)}, u32[]{:S(2)}, u32[]{:S(2)}) collective-permute-start(bf16[1,128,128]{2,1,0:T(8,128)(2,1)S(1)} %bitcast.11), channel_id=1, source_target_pairs={{0,8},{1,9},{2,10},{3,11},{4,12},{5,13},{6,14},{7,15},{8,0},{9,1},... | collective-permute-start | bytes 98312 | tf_op jit(solution)/shard_map/ppermute | solution.py:212
  23.9 1.4 %collective-permute-done.10 = bf16[1,128,128]{2,1,0:T(8,128)(2,1)S(1)} collective-permute-done((bf16[1,128,128]{2,1,0:T(8,128)(2,1)S(1)}, bf16[1,128,128]{2,1,0:T(8,128)(2,1)S(1)}, u32[]{:S(2)}, u32[]{:S(2)}) %collective-permute-start.10) | collective-permute-done | bytes 32800 | tf_op jit(solution)/shard_map/ppermute | solution.py:212
  25.4 2.0 %collective-permute-done.11 = bf16[1,128,128]{2,1,0:T(8,128)(2,1)S(1)} collective-permute-done((bf16[1,128,128]{2,1,0:T(8,128)(2,1)S(1)}, bf16[1,128,128]{2,1,0:T(8,128)(2,1)S(1)}, u32[]{:S(2)}, u32[]{:S(2)}) %collective-permute-start.11) | collective-permute-done | bytes 32800 | tf_op jit(solution)/shard_map/ppermute | solution.py:212
  27.4 2.3 %collective-permute-start.13 = (bf16[4,128,128]{2,1,0:T(8,128)(2,1)S(1)}, bf16[4,128,128]{2,1,0:T(8,128)(2,1)S(1)}, u32[]{:S(2)}, u32[]{:S(2)}) collective-permute-start(bf16[4,128,128]{2,1,0:T(8,128)(2,1)S(1)} %pad_maximum_fusion.1.refs_0_), channel_id=1, source_target_pairs={{0,5},{1,4},{2,7},{3,6},{4,1},{5,0},{6,3},{7,2},{8,13},{9,12},{10,... | collective-permute-start | bytes 393224 | tf_op jit(solution)/shard_map/ppermute | solution.py:212
  29.7 0.5 collective-permute-start.14
  30.2 0.7 %collective-permute-start.15 = (bf16[4,128,128]{2,1,0:T(8,128)(2,1)S(1)}, bf16[4,128,128]{2,1,0:T(8,128)(2,1)S(1)}, u32[]{:S(2)}, u32[]{:S(2)}) collective-permute-start(bf16[4,128,128]{2,1,0:T(8,128)(2,1)S(1)} %pad_maximum_fusion.1.refs_0_), channel_id=1, source_target_pairs={{0,1},{1,0},{2,3},{3,2},{4,5},{5,4},{6,7},{7,6},{8,9},{9,8},{10,11... | collective-permute-start | bytes 393224 | tf_op jit(solution)/shard_map/ppermute | solution.py:212
  30.9 3.0 %collective-permute-done.13.refs_1_ = bf16[4,128,128]{2,1,0:T(8,128)(2,1)S(1)} collective-permute-done((bf16[4,128,128]{2,1,0:T(8,128)(2,1)S(1)}, bf16[4,128,128]{2,1,0:T(8,128)(2,1)S(1)}, u32[]{:S(2)}, u32[]{:S(2)}) %collective-permute-start.13) | collective-permute-done | bytes 131104 | tf_op jit(solution)/shard_map/ppermute | solution.py:212
  33.9 1.2 %collective-permute-done.14.refs_2_ = bf16[4,128,128]{2,1,0:T(8,128)(2,1)S(1)} collective-permute-done((bf16[4,128,128]{2,1,0:T(8,128)(2,1)S(1)}, bf16[4,128,128]{2,1,0:T(8,128)(2,1)S(1)}, u32[]{:S(2)}, u32[]{:S(2)}) %collective-permute-start.14) | collective-permute-done | bytes 131104 | tf_op jit(solution)/shard_map/ppermute | solution.py:212
  37.1 1.2 %collective-permute-start.20 = (bf16[1,128,128]{2,1,0:T(8,128)(2,1)S(1)}, bf16[1,128,128]{2,1,0:T(8,128)(2,1)S(1)}, u32[]{:S(2)}, u32[]{:S(2)}) collective-permute-start(bf16[1,128,128]{2,1,0:T(8,128)(2,1)S(1)} %bitcast.5), channel_id=1, source_target_pairs={{0,16},{1,17},{2,18},{3,19},{4,20},{5,21},{6,22},{7,23},{8,24},{9,... | collective-permute-start | bytes 98312 | tf_op jit(solution)/shard_map/ppermute | solution.py:212
  38.3 1.6 %collective-permute-start.21 = (bf16[1,128,128]{2,1,0:T(8,128)(2,1)S(1)}, bf16[1,128,128]{2,1,0:T(8,128)(2,1)S(1)}, u32[]{:S(2)}, u32[]{:S(2)}) collective-permute-start(bf16[1,128,128]{2,1,0:T(8,128)(2,1)S(1)} %bitcast.6), channel_id=1, source_target_pairs={{0,24},{1,25},{2,26},{3,27},{4,28},{5,29},{6,30},{7,31},{8,16},{9,... | collective-permute-start | bytes 98312 | tf_op jit(solution)/shard_map/ppermute | solution.py:212
  39.9 0.8 %collective-permute-start.22 = (bf16[1,128,128]{2,1,0:T(8,128)(2,1)S(1)}, bf16[1,128,128]{2,1,0:T(8,128)(2,1)S(1)}, u32[]{:S(2)}, u32[]{:S(2)}) collective-permute-start(bf16[1,128,128]{2,1,0:T(8,128)(2,1)S(1)} %bitcast.7), channel_id=1, source_target_pairs={{0,8},{1,9},{2,10},{3,11},{4,12},{5,13},{6,14},{7,15},{8,0},{9,1},... | collective-permute-start | bytes 98312 | tf_op jit(solution)/shard_map/ppermute | solution.py:212
  40.7 1.5 %collective-permute-done.20 = bf16[1,128,128]{2,1,0:T(8,128)(2,1)S(1)} collective-permute-done((bf16[1,128,128]{2,1,0:T(8,128)(2,1)S(1)}, bf16[1,128,128]{2,1,0:T(8,128)(2,1)S(1)}, u32[]{:S(2)}, u32[]{:S(2)}) %collective-permute-start.20) | collective-permute-done | bytes 32800 | tf_op jit(solution)/shard_map/ppermute | solution.py:212
  42.2 1.9 %collective-permute-done.21 = bf16[1,128,128]{2,1,0:T(8,128)(2,1)S(1)} collective-permute-done((bf16[1,128,128]{2,1,0:T(8,128)(2,1)S(1)}, bf16[1,128,128]{2,1,0:T(8,128)(2,1)S(1)}, u32[]{:S(2)}, u32[]{:S(2)}) %collective-permute-start.21) | collective-permute-done | bytes 32800 | tf_op jit(solution)/shard_map/ppermute | solution.py:212
  44.2 2.1 %collective-permute-start.23 = (bf16[4,128,128]{2,1,0:T(8,128)(2,1)S(1)}, bf16[4,128,128]{2,1,0:T(8,128)(2,1)S(1)}, u32[]{:S(2)}, u32[]{:S(2)}) collective-permute-start(bf16[4,128,128]{2,1,0:T(8,128)(2,1)S(1)} %pad_maximum_fusion.2.refs_0_), channel_id=1, source_target_pairs={{0,5},{1,4},{2,7},{3,6},{4,1},{5,0},{6,3},{7,2},{8,13},{9,12},{10,... | collective-permute-start | bytes 393224 | tf_op jit(solution)/shard_map/ppermute | solution.py:212
  46.3 0.5 collective-permute-start.24
  46.8 0.9 %collective-permute-start.25 = (bf16[4,128,128]{2,1,0:T(8,128)(2,1)S(1)}, bf16[4,128,128]{2,1,0:T(8,128)(2,1)S(1)}, u32[]{:S(2)}, u32[]{:S(2)}) collective-permute-start(bf16[4,128,128]{2,1,0:T(8,128)(2,1)S(1)} %pad_maximum_fusion.2.refs_0_), channel_id=1, source_target_pairs={{0,1},{1,0},{2,3},{3,2},{4,5},{5,4},{6,7},{7,6},{8,9},{9,8},{10,11... | collective-permute-start | bytes 393224 | tf_op jit(solution)/shard_map/ppermute | solution.py:212
  47.7 3.0 %collective-permute-done.23.refs_1_ = bf16[4,128,128]{2,1,0:T(8,128)(2,1)S(1)} collective-permute-done((bf16[4,128,128]{2,1,0:T(8,128)(2,1)S(1)}, bf16[4,128,128]{2,1,0:T(8,128)(2,1)S(1)}, u32[]{:S(2)}, u32[]{:S(2)}) %collective-permute-start.23) | collective-permute-done | bytes 131104 | tf_op jit(solution)/shard_map/ppermute | solution.py:212
  50.7 1.0 %collective-permute-done.24.refs_2_ = bf16[4,128,128]{2,1,0:T(8,128)(2,1)S(1)} collective-permute-done((bf16[4,128,128]{2,1,0:T(8,128)(2,1)S(1)}, bf16[4,128,128]{2,1,0:T(8,128)(2,1)S(1)}, u32[]{:S(2)}, u32[]{:S(2)}) %collective-permute-start.24) | collective-permute-done | bytes 131104 | tf_op jit(solution)/shard_map/ppermute | solution.py:212
  52.2 0.5 partial.5.partial_ref
  53.4 1.1 %last.5 = bf16[128,128]{1,0:T(8,128)(2,1)} custom-call(bf16[32,256,128]{2,1,0:T(8,128)(2,1)S(1)} %get-tuple-element.27.adj_ref, f32[128,128]{1,0:T(8,128)S(1)} %partial.5.partial_ref, bf16[128,128]{1,0:T(8,128)(2,1)S(1)} %last.4.own_ref, f32[3,128]{1,0:T(4,128)S(1)} %copy-done, bf16[4,128,128]{2,1,0:T(8,128)(2,1)S(1)} %collective-permute-done.27.refs_0_, ...), custom_call_target="tpu_custom_call" | custom-call | tf_op jit(solution)/shard_map/last/pallas_call | solution.py:203
  (41 shorter events, 5.9 us)
Async XLA Ops:
  0.0 8.0 %collective-permute-start = (bf16[1,128,128]{2,1,0:T(8,128)(2,1)}, bf16[1,128,128]{2,1,0:T(8,128)(2,1)S(1)}, u32[]{:S(2)}, u32[]{:S(2)}) collective-permute-start(bf16[1,128,128]{2,1,0:T(8,128)(2,1)} %bitcast.16), channel_id=1, source_target_pairs={{0,16},{1,17},{2,18},{3,19},{4,20},{5,21},{6,22},{7,23},{8,24},{9,... | collective-permute-start | bytes 98312 | tf_op jit(solution)/shard_map/ppermute | solution.py:212
  4.1 5.9 %collective-permute-start.1 = (bf16[1,128,128]{2,1,0:T(8,128)(2,1)}, bf16[1,128,128]{2,1,0:T(8,128)(2,1)S(1)}, u32[]{:S(2)}, u32[]{:S(2)}) collective-permute-start(bf16[1,128,128]{2,1,0:T(8,128)(2,1)} %bitcast.17), channel_id=1, source_target_pairs={{0,24},{1,25},{2,26},{3,27},{4,28},{5,29},{6,30},{7,31},{8,16},{9,... | collective-permute-start | bytes 98312 | tf_op jit(solution)/shard_map/ppermute | solution.py:212
  5.4 4.6 %collective-permute-start.2 = (bf16[1,128,128]{2,1,0:T(8,128)(2,1)}, bf16[1,128,128]{2,1,0:T(8,128)(2,1)S(1)}, u32[]{:S(2)}, u32[]{:S(2)}) collective-permute-start(bf16[1,128,128]{2,1,0:T(8,128)(2,1)} %bitcast.18), channel_id=1, source_target_pairs={{0,8},{1,9},{2,10},{3,11},{4,12},{5,13},{6,14},{7,15},{8,0},{9,1},... | collective-permute-start | bytes 98312 | tf_op jit(solution)/shard_map/ppermute | solution.py:212
  10.0 6.3 %collective-permute-start.3 = (bf16[4,128,128]{2,1,0:T(8,128)(2,1)S(1)}, bf16[4,128,128]{2,1,0:T(8,128)(2,1)S(1)}, u32[]{:S(2)}, u32[]{:S(2)}) collective-permute-start(bf16[4,128,128]{2,1,0:T(8,128)(2,1)S(1)} %pad_maximum_fusion.refs_0_), channel_id=1, source_target_pairs={{0,5},{1,4},{2,7},{3,6},{4,1},{5,0},{6,3},{7,2},{8,13},{9,12},{10,... | collective-permute-start | bytes 393224 | tf_op jit(solution)/shard_map/ppermute | solution.py:212
  12.5 5.1 %collective-permute-start.4 = (bf16[4,128,128]{2,1,0:T(8,128)(2,1)S(1)}, bf16[4,128,128]{2,1,0:T(8,128)(2,1)S(1)}, u32[]{:S(2)}, u32[]{:S(2)}) collective-permute-start(bf16[4,128,128]{2,1,0:T(8,128)(2,1)S(1)} %pad_maximum_fusion.refs_0_), channel_id=1, source_target_pairs={{0,4},{1,5},{2,6},{3,7},{4,0},{5,1},{6,2},{7,3},{8,12},{9,13},{10,... | collective-permute-start | bytes 393224 | tf_op jit(solution)/shard_map/ppermute | solution.py:212
  13.1 5.0 %collective-permute-start.5 = (bf16[4,128,128]{2,1,0:T(8,128)(2,1)S(1)}, bf16[4,128,128]{2,1,0:T(8,128)(2,1)S(1)}, u32[]{:S(2)}, u32[]{:S(2)}) collective-permute-start(bf16[4,128,128]{2,1,0:T(8,128)(2,1)S(1)} %pad_maximum_fusion.refs_0_), channel_id=1, source_target_pairs={{0,1},{1,0},{2,3},{3,2},{4,5},{5,4},{6,7},{7,6},{8,9},{9,8},{10,11... | collective-permute-start | bytes 393224 | tf_op jit(solution)/shard_map/ppermute | solution.py:212
  13.6 5.0 %collective-permute-start.6 = (bf16[4,128,128]{2,1,0:T(8,128)(2,1)S(1)}, bf16[4,128,128]{2,1,0:T(8,128)(2,1)S(1)}, u32[]{:S(2)}, u32[]{:S(2)}) collective-permute-start(bf16[4,128,128]{2,1,0:T(8,128)(2,1)S(1)} %pad_maximum_fusion.refs_0_), channel_id=1, source_target_pairs={{0,2},{1,3},{2,0},{3,1},{4,6},{5,7},{6,4},{7,5},{8,10},{9,11},{10,... | collective-permute-start | bytes 393224 | tf_op jit(solution)/shard_map/ppermute | solution.py:212
  16.0 3.9 %copy-start = (f32[3,128]{1,0:T(4,128)S(1)}, f32[3,128]{1,0:T(4,128)}, u32[]{:S(2)}) copy-start(f32[3,128]{1,0:T(4,128)} %gain_ref.5) | copy-start | bytes 4612
  18.0 1.3 %collective-permute-start.7 = (bf16[4,128,128]{2,1,0:T(8,128)(2,1)S(1)}, bf16[4,128,128]{2,1,0:T(8,128)(2,1)S(1)}, u32[]{:S(2)}, u32[]{:S(2)}) collective-permute-start(bf16[4,128,128]{2,1,0:T(8,128)(2,1)S(1)} %collective-permute-done.3.refs_1_), channel_id=1, source_target_pairs={{0,2},{1,3},{2,0},{3,1},{4,6},{5,7},{6,4},{7,5},{8,10},{9,11},{10,... | collective-permute-start | bytes 393224 | tf_op jit(solution)/shard_map/ppermute | solution.py:212
  18.0 1.5 %collective-permute-start.8 = (bf16[4,128,128]{2,1,0:T(8,128)(2,1)S(1)}, bf16[4,128,128]{2,1,0:T(8,128)(2,1)S(1)}, u32[]{:S(2)}, u32[]{:S(2)}) collective-permute-start(bf16[4,128,128]{2,1,0:T(8,128)(2,1)S(1)} %collective-permute-done.4.refs_2_), channel_id=1, source_target_pairs={{0,2},{1,3},{2,0},{3,1},{4,6},{5,7},{6,4},{7,5},{8,10},{9,11},{10,... | collective-permute-start | bytes 393224 | tf_op jit(solution)/shard_map/ppermute | solution.py:212
  18.5 1.3 %collective-permute-start.9 = (bf16[4,128,128]{2,1,0:T(8,128)(2,1)S(1)}, bf16[4,128,128]{2,1,0:T(8,128)(2,1)S(1)}, u32[]{:S(2)}, u32[]{:S(2)}) collective-permute-start(bf16[4,128,128]{2,1,0:T(8,128)(2,1)S(1)} %collective-permute-done.5.refs_3_), channel_id=1, source_target_pairs={{0,2},{1,3},{2,0},{3,1},{4,6},{5,7},{6,4},{7,5},{8,10},{9,11},{10,... | collective-permute-start | bytes 393224 | tf_op jit(solution)/shard_map/ppermute | solution.py:212
  20.3 5.0 %collective-permute-start.10 = (bf16[1,128,128]{2,1,0:T(8,128)(2,1)S(1)}, bf16[1,128,128]{2,1,0:T(8,128)(2,1)S(1)}, u32[]{:S(2)}, u32[]{:S(2)}) collective-permute-start(bf16[1,128,128]{2,1,0:T(8,128)(2,1)S(1)} %bitcast.9), channel_id=1, source_target_pairs={{0,16},{1,17},{2,18},{3,19},{4,20},{5,21},{6,22},{7,23},{8,24},{9,... | collective-permute-start | bytes 98312 | tf_op jit(solution)/shard_map/ppermute | solution.py:212
  21.6 5.7 %collective-permute-start.11 = (bf16[1,128,128]{2,1,0:T(8,128)(2,1)S(1)}, bf16[1,128,128]{2,1,0:T(8,128)(2,1)S(1)}, u32[]{:S(2)}, u32[]{:S(2)}) collective-permute-start(bf16[1,128,128]{2,1,0:T(8,128)(2,1)S(1)} %bitcast.10), channel_id=1, source_target_pairs={{0,24},{1,25},{2,26},{3,27},{4,28},{5,29},{6,30},{7,31},{8,16},{9,... | collective-permute-start | bytes 98312 | tf_op jit(solution)/shard_map/ppermute | solution.py:212
  22.9 4.5 %collective-permute-start.12 = (bf16[1,128,128]{2,1,0:T(8,128)(2,1)S(1)}, bf16[1,128,128]{2,1,0:T(8,128)(2,1)S(1)}, u32[]{:S(2)}, u32[]{:S(2)}) collective-permute-start(bf16[1,128,128]{2,1,0:T(8,128)(2,1)S(1)} %bitcast.11), channel_id=1, source_target_pairs={{0,8},{1,9},{2,10},{3,11},{4,12},{5,13},{6,14},{7,15},{8,0},{9,1},... | collective-permute-start | bytes 98312 | tf_op jit(solution)/shard_map/ppermute | solution.py:212
  27.4 6.6 %collective-permute-start.13 = (bf16[4,128,128]{2,1,0:T(8,128)(2,1)S(1)}, bf16[4,128,128]{2,1,0:T(8,128)(2,1)S(1)}, u32[]{:S(2)}, u32[]{:S(2)}) collective-permute-start(bf16[4,128,128]{2,1,0:T(8,128)(2,1)S(1)} %pad_maximum_fusion.1.refs_0_), channel_id=1, source_target_pairs={{0,5},{1,4},{2,7},{3,6},{4,1},{5,0},{6,3},{7,2},{8,13},{9,12},{10,... | collective-permute-start | bytes 393224 | tf_op jit(solution)/shard_map/ppermute | solution.py:212
  29.7 5.5 %collective-permute-start.14 = (bf16[4,128,128]{2,1,0:T(8,128)(2,1)S(1)}, bf16[4,128,128]{2,1,0:T(8,128)(2,1)S(1)}, u32[]{:S(2)}, u32[]{:S(2)}) collective-permute-start(bf16[4,128,128]{2,1,0:T(8,128)(2,1)S(1)} %pad_maximum_fusion.1.refs_0_), channel_id=1, source_target_pairs={{0,4},{1,5},{2,6},{3,7},{4,0},{5,1},{6,2},{7,3},{8,12},{9,13},{10,... | collective-permute-start | bytes 393224 | tf_op jit(solution)/shard_map/ppermute | solution.py:212
  30.2 5.1 %collective-permute-start.15 = (bf16[4,128,128]{2,1,0:T(8,128)(2,1)S(1)}, bf16[4,128,128]{2,1,0:T(8,128)(2,1)S(1)}, u32[]{:S(2)}, u32[]{:S(2)}) collective-permute-start(bf16[4,128,128]{2,1,0:T(8,128)(2,1)S(1)} %pad_maximum_fusion.1.refs_0_), channel_id=1, source_target_pairs={{0,1},{1,0},{2,3},{3,2},{4,5},{5,4},{6,7},{7,6},{8,9},{9,8},{10,11... | collective-permute-start | bytes 393224 | tf_op jit(solution)/shard_map/ppermute | solution.py:212
  30.9 4.7 %collective-permute-start.16 = (bf16[4,128,128]{2,1,0:T(8,128)(2,1)S(1)}, bf16[4,128,128]{2,1,0:T(8,128)(2,1)S(1)}, u32[]{:S(2)}, u32[]{:S(2)}) collective-permute-start(bf16[4,128,128]{2,1,0:T(8,128)(2,1)S(1)} %pad_maximum_fusion.1.refs_0_), channel_id=1, source_target_pairs={{0,2},{1,3},{2,0},{3,1},{4,6},{5,7},{6,4},{7,5},{8,10},{9,11},{10,... | collective-permute-start | bytes 393224 | tf_op jit(solution)/shard_map/ppermute | solution.py:212
  33.9 2.2 %collective-permute-start.17 = (bf16[4,128,128]{2,1,0:T(8,128)(2,1)S(1)}, bf16[4,128,128]{2,1,0:T(8,128)(2,1)S(1)}, u32[]{:S(2)}, u32[]{:S(2)}) collective-permute-start(bf16[4,128,128]{2,1,0:T(8,128)(2,1)S(1)} %collective-permute-done.13.refs_1_), channel_id=1, source_target_pairs={{0,2},{1,3},{2,0},{3,1},{4,6},{5,7},{6,4},{7,5},{8,10},{9,11},{10,... | collective-permute-start | bytes 393224 | tf_op jit(solution)/shard_map/ppermute | solution.py:212
  35.1 1.3 %collective-permute-start.18 = (bf16[4,128,128]{2,1,0:T(8,128)(2,1)S(1)}, bf16[4,128,128]{2,1,0:T(8,128)(2,1)S(1)}, u32[]{:S(2)}, u32[]{:S(2)}) collective-permute-start(bf16[4,128,128]{2,1,0:T(8,128)(2,1)S(1)} %collective-permute-done.14.refs_2_), channel_id=1, source_target_pairs={{0,2},{1,3},{2,0},{3,1},{4,6},{5,7},{6,4},{7,5},{8,10},{9,11},{10,... | collective-permute-start | bytes 393224 | tf_op jit(solution)/shard_map/ppermute | solution.py:212
  35.3 1.4 %collective-permute-start.19 = (bf16[4,128,128]{2,1,0:T(8,128)(2,1)S(1)}, bf16[4,128,128]{2,1,0:T(8,128)(2,1)S(1)}, u32[]{:S(2)}, u32[]{:S(2)}) collective-permute-start(bf16[4,128,128]{2,1,0:T(8,128)(2,1)S(1)} %collective-permute-done.15.refs_3_), channel_id=1, source_target_pairs={{0,2},{1,3},{2,0},{3,1},{4,6},{5,7},{6,4},{7,5},{8,10},{9,11},{10,... | collective-permute-start | bytes 393224 | tf_op jit(solution)/shard_map/ppermute | solution.py:212
  37.1 5.1 %collective-permute-start.20 = (bf16[1,128,128]{2,1,0:T(8,128)(2,1)S(1)}, bf16[1,128,128]{2,1,0:T(8,128)(2,1)S(1)}, u32[]{:S(2)}, u32[]{:S(2)}) collective-permute-start(bf16[1,128,128]{2,1,0:T(8,128)(2,1)S(1)} %bitcast.5), channel_id=1, source_target_pairs={{0,16},{1,17},{2,18},{3,19},{4,20},{5,21},{6,22},{7,23},{8,24},{9,... | collective-permute-start | bytes 98312 | tf_op jit(solution)/shard_map/ppermute | solution.py:212
  38.3 5.8 %collective-permute-start.21 = (bf16[1,128,128]{2,1,0:T(8,128)(2,1)S(1)}, bf16[1,128,128]{2,1,0:T(8,128)(2,1)S(1)}, u32[]{:S(2)}, u32[]{:S(2)}) collective-permute-start(bf16[1,128,128]{2,1,0:T(8,128)(2,1)S(1)} %bitcast.6), channel_id=1, source_target_pairs={{0,24},{1,25},{2,26},{3,27},{4,28},{5,29},{6,30},{7,31},{8,16},{9,... | collective-permute-start | bytes 98312 | tf_op jit(solution)/shard_map/ppermute | solution.py:212
  39.9 4.3 %collective-permute-start.22 = (bf16[1,128,128]{2,1,0:T(8,128)(2,1)S(1)}, bf16[1,128,128]{2,1,0:T(8,128)(2,1)S(1)}, u32[]{:S(2)}, u32[]{:S(2)}) collective-permute-start(bf16[1,128,128]{2,1,0:T(8,128)(2,1)S(1)} %bitcast.7), channel_id=1, source_target_pairs={{0,8},{1,9},{2,10},{3,11},{4,12},{5,13},{6,14},{7,15},{8,0},{9,1},... | collective-permute-start | bytes 98312 | tf_op jit(solution)/shard_map/ppermute | solution.py:212
  44.2 6.5 %collective-permute-start.23 = (bf16[4,128,128]{2,1,0:T(8,128)(2,1)S(1)}, bf16[4,128,128]{2,1,0:T(8,128)(2,1)S(1)}, u32[]{:S(2)}, u32[]{:S(2)}) collective-permute-start(bf16[4,128,128]{2,1,0:T(8,128)(2,1)S(1)} %pad_maximum_fusion.2.refs_0_), channel_id=1, source_target_pairs={{0,5},{1,4},{2,7},{3,6},{4,1},{5,0},{6,3},{7,2},{8,13},{9,12},{10,... | collective-permute-start | bytes 393224 | tf_op jit(solution)/shard_map/ppermute | solution.py:212
  46.3 5.4 %collective-permute-start.24 = (bf16[4,128,128]{2,1,0:T(8,128)(2,1)S(1)}, bf16[4,128,128]{2,1,0:T(8,128)(2,1)S(1)}, u32[]{:S(2)}, u32[]{:S(2)}) collective-permute-start(bf16[4,128,128]{2,1,0:T(8,128)(2,1)S(1)} %pad_maximum_fusion.2.refs_0_), channel_id=1, source_target_pairs={{0,4},{1,5},{2,6},{3,7},{4,0},{5,1},{6,2},{7,3},{8,12},{9,13},{10,... | collective-permute-start | bytes 393224 | tf_op jit(solution)/shard_map/ppermute | solution.py:212
  46.8 5.3 %collective-permute-start.25 = (bf16[4,128,128]{2,1,0:T(8,128)(2,1)S(1)}, bf16[4,128,128]{2,1,0:T(8,128)(2,1)S(1)}, u32[]{:S(2)}, u32[]{:S(2)}) collective-permute-start(bf16[4,128,128]{2,1,0:T(8,128)(2,1)S(1)} %pad_maximum_fusion.2.refs_0_), channel_id=1, source_target_pairs={{0,1},{1,0},{2,3},{3,2},{4,5},{5,4},{6,7},{7,6},{8,9},{9,8},{10,11... | collective-permute-start | bytes 393224 | tf_op jit(solution)/shard_map/ppermute | solution.py:212
  47.7 4.5 %collective-permute-start.26 = (bf16[4,128,128]{2,1,0:T(8,128)(2,1)S(1)}, bf16[4,128,128]{2,1,0:T(8,128)(2,1)S(1)}, u32[]{:S(2)}, u32[]{:S(2)}) collective-permute-start(bf16[4,128,128]{2,1,0:T(8,128)(2,1)S(1)} %pad_maximum_fusion.2.refs_0_), channel_id=1, source_target_pairs={{0,2},{1,3},{2,0},{3,1},{4,6},{5,7},{6,4},{7,5},{8,10},{9,11},{10,... | collective-permute-start | bytes 393224 | tf_op jit(solution)/shard_map/ppermute | solution.py:212
  50.7 2.0 %collective-permute-start.27 = (bf16[4,128,128]{2,1,0:T(8,128)(2,1)S(1)}, bf16[4,128,128]{2,1,0:T(8,128)(2,1)S(1)}, u32[]{:S(2)}, u32[]{:S(2)}) collective-permute-start(bf16[4,128,128]{2,1,0:T(8,128)(2,1)S(1)} %collective-permute-done.23.refs_1_), channel_id=1, source_target_pairs={{0,2},{1,3},{2,0},{3,1},{4,6},{5,7},{6,4},{7,5},{8,10},{9,11},{10,... | collective-permute-start | bytes 393224 | tf_op jit(solution)/shard_map/ppermute | solution.py:212
  51.7 1.3 %collective-permute-start.28 = (bf16[4,128,128]{2,1,0:T(8,128)(2,1)S(1)}, bf16[4,128,128]{2,1,0:T(8,128)(2,1)S(1)}, u32[]{:S(2)}, u32[]{:S(2)}) collective-permute-start(bf16[4,128,128]{2,1,0:T(8,128)(2,1)S(1)} %collective-permute-done.24.refs_2_), channel_id=1, source_target_pairs={{0,2},{1,3},{2,0},{3,1},{4,6},{5,7},{6,4},{7,5},{8,10},{9,11},{10,... | collective-permute-start | bytes 393224 | tf_op jit(solution)/shard_map/ppermute | solution.py:212
  52.1 1.3 %collective-permute-start.29 = (bf16[4,128,128]{2,1,0:T(8,128)(2,1)S(1)}, bf16[4,128,128]{2,1,0:T(8,128)(2,1)S(1)}, u32[]{:S(2)}, u32[]{:S(2)}) collective-permute-start(bf16[4,128,128]{2,1,0:T(8,128)(2,1)S(1)} %collective-permute-done.25.refs_3_), channel_id=1, source_target_pairs={{0,2},{1,3},{2,0},{3,1},{4,6},{5,7},{6,4},{7,5},{8,10},{9,11},{10,... | collective-permute-start | bytes 393224 | tf_op jit(solution)/shard_map/ppermute | solution.py:212

commit v4 on v3

--- a/solution.py
+++ b/solution.py
@@ -10,6 +10,8 @@
 epsilon = 1e-05
 AXES = ("blk", "col")
 CHUNK = 8
+ORDERS = (((1, 0, 2), (0, 1, 2)), ((0, 1, 2), (0, 1, 2)))
+SWAP = 1
 
 
 def moved(index, spots):
@@ -19,12 +21,19 @@
     return result
 
 
-def add_tiles(count, cols_hbm, tiles_hbm, cols_ref, buf, accs, sems, window, meanwhile, devices, spots):
+def landing(me, device, plan):
+    core_bit, both = plan
+    index = me ^ device
+    core = (device >> core_bit) & 1
+    return jnp.where(core == 1, moved(index, both[1]), moved(index, both[0]))
+
+
+def add_tiles(count, cols_hbm, tiles_hbm, cols_ref, buf, accs, sems, window, meanwhile, devices, plan):
     first, stop = window
     half = accs[0].shape[2]
     total = devices[0] * devices[1]
     chunks = (stop - first) // CHUNK
-    me = moved(lax.axis_index("blk") * devices[1] + lax.axis_index("col"), spots)
+    me = lax.axis_index("blk") * devices[1] + lax.axis_index("col")
     cols_copy = pltpu.make_async_copy(cols_hbm, cols_ref, sems.at[chunks])
 
     def copy(c):
@@ -49,8 +58,8 @@
                 acc = accs[t % len(accs)]
                 place = c * CHUNK + t
                 slot = first + place
-                left = me ^ moved(cols_ref[0, slot] * 2, spots)
-                right = left ^ spots[0]
+                left = landing(me, cols_ref[0, slot] * 2, plan)
+                right = landing(me, cols_ref[0, slot] * 2 + 1, plan)
                 left = jnp.where(slot < count, left, total)
                 right = jnp.where(slot < count, right, total + 1)
                 acc[left] = acc[left] + buf[place, :, :half].astype(jnp.float32)
@@ -125,14 +134,14 @@
     return pl.CostEstimate(flops=size * 8, bytes_accessed=size * 2, transcendentals=0)
 
 
-def begin(tiles, cols, count, own, devices, spots):
+def begin(tiles, cols, count, own, devices, plan):
     slots, rows, width = tiles.shape
     total = devices[0] * devices[1]
     ways = 2 if total <= 64 else 1
     length = split(slots)
     memory = [pltpu.SMEM, pltpu.HBM, pltpu.HBM, pltpu.HBM]
     own, *accs = pl.pallas_call(
-        functools.partial(begin_kernel, ways=ways, window=(0, length), devices=devices, spots=spots),
+        functools.partial(begin_kernel, ways=ways, window=(0, length), devices=devices, plan=plan),
         out_shape=[pltpu.VMEM(own.shape, own.dtype)] + [pltpu.VMEM((total + 2, rows, width // 2), jnp.float32)] * ways,
         in_specs=[pl.BlockSpec(memory_space=space) for space in memory],
         out_specs=[pl.BlockSpec(memory_space=pltpu.VMEM)] * (1 + ways),
@@ -144,14 +153,14 @@
     return own, accs
 
 
-def finish(tiles, cols, count, accs, devices, spots):
+def finish(tiles, cols, count, accs, devices, plan):
     slots, rows, width = tiles.shape
     total = devices[0] * devices[1]
     ways = len(accs)
     length = slots - split(slots)
     memory = [pltpu.SMEM, pltpu.HBM, pltpu.HBM] + [pltpu.VMEM] * ways
     return pl.pallas_call(
-        functools.partial(finish_kernel, ways=ways, window=(split(slots), slots), devices=devices, spots=spots),
+        functools.partial(finish_kernel, ways=ways, window=(split(slots), slots), devices=devices, plan=plan),
         out_shape=[pltpu.VMEM((total, 2 * rows, width // 2), jnp.bfloat16)] + [pltpu.VMEM(acc.shape, acc.dtype) for acc in accs],
         in_specs=[pl.BlockSpec(memory_space=space) for space in memory],
         out_specs=[pl.BlockSpec(memory_space=pltpu.VMEM)] * (1 + ways),
@@ -208,15 +217,16 @@
     )(fast(adj), fast(partial), fast(own), fast(gain), *[fast(part) for part in parts])
 
 
-def exchange(value, mask, total):
-    return lax.ppermute(value, AXES, [(i, i ^ mask) for i in range(total)])
-
-
-def masks_of(group, closing):
+def exchange(value, masks, core_bit, total):
+    return lax.ppermute(value, AXES, [(i, i ^ masks[(i >> core_bit) & 1]) for i in range(total)])
+
+
+def masks_of(group, near, stage):
     if len(group) == 1:
         return [1 << group[0]]
     high, low = 1 << group[0], 1 << group[1]
-    return [high | low, high, low] if closing else [high, high | low, low]
+    three = [high | low, high, low]
+    return [three[k] for k in ORDERS[near][stage > 0]]
 
 
 def stages(devices):
@@ -224,40 +234,50 @@
     core_bit = devices[1].bit_length() - 1
     line = [b for b in range(bits) if b != core_bit][::-1]
     groups = [line[i : i + 2] for i in range(0, len(line), 2)]
-    spots = [0] * bits
-    size = 1
-    for group in groups:
-        for place, mask in enumerate(masks_of(group, group is groups[-1])):
-            if mask & (mask - 1) == 0:
-                spots[mask.bit_length() - 1] = size * (place + 1)
-        size <<= len(group)
-    spots[core_bit] = size
-    return groups, core_bit, spots
+    both = []
+    for core in range(2):
+        order = list(groups)
+        if core == SWAP and len(groups[0]) == len(groups[-1]):
+            order[0], order[-1] = order[-1], order[0]
+        spots = [0] * bits
+        size = 1
+        masks = []
+        for stage, group in enumerate(order):
+            masks.append(masks_of(group, group is groups[-1], stage))
+            for place, mask in enumerate(masks[-1]):
+                if mask & (mask - 1) == 0:
+                    spots[mask.bit_length() - 1] = size * (place + 1)
+            size <<= len(group)
+        spots[core_bit] = size
+        both.append((spots, masks))
+    return [list(zip(*pair)) for pair in zip(both[0][1], both[1][1])], core_bit, [spots for spots, _ in both]
 
 
 def solution(mesh):
     devices = (mesh.shape["blk"], mesh.shape["col"])
     total = devices[0] * devices[1]
-    groups, core_bit, spots = stages(devices)
+    groups, core_bit, both = stages(devices)
+    plan = (core_bit, both)
+    swap = [1 << core_bit] * 2
 
     def shards(features, tile_vals, tile_cols, tile_count, norm_gain):
         current = features
         for hop in range(norm_gain.shape[0]):
             held = current[None]
             if hop == 0:
-                current, accs = begin(tile_vals[0], tile_cols, tile_count, features, devices, spots)
+                current, accs = begin(tile_vals[0], tile_cols, tile_count, features, devices, plan)
             for group in groups:
-                received = [exchange(held, mask, total) for mask in masks_of(group, group is groups[-1])]
+                received = [exchange(held, masks, core_bit, total) for masks in group]
                 if hop == 0 and group is groups[0]:
                     received, accs = lax.optimization_barrier((received, accs))
-                    adj = finish(tile_vals[0], tile_cols, tile_count, accs, devices, spots)
+                    adj = finish(tile_vals[0], tile_cols, tile_count, accs, devices, plan)
                 parts = [current[None] if group is groups[0] else held, *received]
                 if group is not groups[-1]:
                     held = jnp.concatenate(parts, axis=0)
             if hop == 0:
                 *received, adj = lax.optimization_barrier((*parts[1:], adj))
                 parts = [parts[0], *received]
-            others = [exchange(part, 1 << core_bit, total) for part in parts]
+            others = [exchange(part, swap, core_bit, total) for part in parts]
             size = parts[0].shape[0]
             near = [j * size for j in range(len(parts))]
             far = [total // 2 + spot for spot in near]

time: 54.6 us -> 53.9 us (0.987)
  transfers between devices with their start and end apart: 30 -> 30, of which waited for: 21 -> 22; matrix products, arithmetic and copies ran while one was open for 0% -> 0% of each run, Pallas kernels for 10% -> 10%
where the time goes in v4:
time: 53.9 us; the launch traced here: 53.8 us
  starting transfers between devices  23.9 us (44%)
  waiting for transfers between devices  21.6 us (40%)
  Pallas kernels  7.36 us (14%)
  between operations  0.77 us (1%)
    ppermute x30, starting transfers between devices, exchange(): lax.ppermute(value, AXES, [(i, i ^ masks[i >> core_bit & 1]) for i in ran...  23.9 us
    ppermute x30, waiting for transfers between devices, exchange(): lax.ppermute(value, AXES, [(i, i ^ masks[i >> core_bit & 1]) for i in ran...  21.6 us
    pallas_call x1, Pallas kernels, finish(): pl.pallas_call(functools.partial(finish_kernel, ways=ways, window=(split(...  2.12 us
    pallas_call x3, Pallas kernels, last(): pl.pallas_call(functools.partial(last_kernel, spots=spots, hop=hop), out_...  1.95 us
    pallas_call x1, Pallas kernels, begin(): pl.pallas_call(functools.partial(begin_kernel, ways=ways, window=(0, leng...  1.8 us
    pallas_call x3, Pallas kernels, partial_sum(): pl.pallas_call(functools.partial(partial_kernel, spots=spots), out_shape=...  1.49 us
  transfers between devices with their start and end apart: 30, of which 22 were waited for; matrix products, arithmetic and copies ran while one was open for 0% of the time, Pallas kernels for 10%

profile of v4, /device:TPU:0, one launch (start us, length us, event | category | flops | bytes accessed | tf_op | source)
XLA Modules:
  0.0 53.8 jit_solution(4491911170140252393)
XLA Ops:
  0.0 4.1 %collective-permute-start = (bf16[1,128,128]{2,1,0:T(8,128)(2,1)}, bf16[1,128,128]{2,1,0:T(8,128)(2,1)S(1)}, u32[]{:S(2)}, u32[]{:S(2)}) collective-permute-start(bf16[1,128,128]{2,1,0:T(8,128)(2,1)} %bitcast.16), channel_id=1, source_target_pairs={{0,16},{1,17},{2,7},{3,6},{4,20},{5,21},{6,3},{7,2},{8,24},{9,25},... | collective-permute-start | bytes 98312 | tf_op jit(solution)/shard_map/ppermute | solution.py:221
  4.1 1.3 %collective-permute-start.1 = (bf16[1,128,128]{2,1,0:T(8,128)(2,1)}, bf16[1,128,128]{2,1,0:T(8,128)(2,1)S(1)}, u32[]{:S(2)}, u32[]{:S(2)}) collective-permute-start(bf16[1,128,128]{2,1,0:T(8,128)(2,1)} %bitcast.17), channel_id=1, source_target_pairs={{0,24},{1,25},{2,6},{3,7},{4,28},{5,29},{6,2},{7,3},{8,16},{9,17},... | collective-permute-start | bytes 98312 | tf_op jit(solution)/shard_map/ppermute | solution.py:221
  6.3 1.8 %begin.1 = (bf16[128,128]{1,0:T(8,128)(2,1)S(1)}, f32[34,128,128]{2,1,0:T(8,128)S(1)}, f32[34,128,128]{2,1,0:T(8,128)S(1)}) custom-call(s32[1]{0:T(128)S(6)} %copy.10.count_ref, s32[1,128]{1,0:T(1,128)} %cols_hbm.3, bf16[128,128,256]{2,1,0:T(8,128)(2,1)} %bitcast.14, bf16[128,128]{1,0:T(8,128)(2,1)} %own_hbm.1), custom_call_target="tpu_custom_call" | custom-call | flops 8388608 | bytes 2097152 | tf_op jit(solution)/shard_map/begin/pallas_call | solution.py:143
  8.1 1.9 %collective-permute-done.1 = bf16[1,128,128]{2,1,0:T(8,128)(2,1)S(1)} collective-permute-done((bf16[1,128,128]{2,1,0:T(8,128)(2,1)}, bf16[1,128,128]{2,1,0:T(8,128)(2,1)S(1)}, u32[]{:S(2)}, u32[]{:S(2)}) %collective-permute-start.1) | collective-permute-done | bytes 32800 | tf_op jit(solution)/shard_map/ppermute | solution.py:221
  10.0 2.5 %collective-permute-start.3 = (bf16[4,128,128]{2,1,0:T(8,128)(2,1)S(1)}, bf16[4,128,128]{2,1,0:T(8,128)(2,1)S(1)}, u32[]{:S(2)}, u32[]{:S(2)}) collective-permute-start(bf16[4,128,128]{2,1,0:T(8,128)(2,1)S(1)} %pad_maximum_fusion.refs_0_), channel_id=1, source_target_pairs={{0,5},{1,4},{2,26},{3,27},{4,1},{5,0},{6,30},{7,31},{8,13},{9,12},... | collective-permute-start | bytes 393224 | tf_op jit(solution)/shard_map/ppermute | solution.py:221
  12.5 0.5 collective-permute-start.4
  13.6 2.1 %finish.1 = (bf16[32,256,128]{2,1,0:T(8,128)(2,1)S(1)}, f32[34,128,128]{2,1,0:T(8,128)S(1)}, f32[34,128,128]{2,1,0:T(8,128)S(1)}) custom-call(s32[1]{0:T(128)S(6)} %copy.10.count_ref, s32[1,128]{1,0:T(1,128)} %cols_hbm.3, bf16[128,128,256]{2,1,0:T(8,128)(2,1)} %bitcast.15, ...), custom_call_target="tpu_custom_call", output_to_operand_aliasing={{1}: (3, {}), {2}: (4, {})} | custom-call | flops 25165824 | bytes 6291456 | tf_op jit(solution)/shard_map/finish/pallas_call | solution.py:162
  15.9 1.5 %collective-permute-done.4.refs_2_ = bf16[4,128,128]{2,1,0:T(8,128)(2,1)S(1)} collective-permute-done((bf16[4,128,128]{2,1,0:T(8,128)(2,1)S(1)}, bf16[4,128,128]{2,1,0:T(8,128)(2,1)S(1)}, u32[]{:S(2)}, u32[]{:S(2)}) %collective-permute-start.4) | collective-permute-done | bytes 131104 | tf_op jit(solution)/shard_map/ppermute | solution.py:221
  20.3 1.3 %collective-permute-start.10 = (bf16[1,128,128]{2,1,0:T(8,128)(2,1)S(1)}, bf16[1,128,128]{2,1,0:T(8,128)(2,1)S(1)}, u32[]{:S(2)}, u32[]{:S(2)}) collective-permute-start(bf16[1,128,128]{2,1,0:T(8,128)(2,1)S(1)} %bitcast.9), channel_id=1, source_target_pairs={{0,16},{1,17},{2,7},{3,6},{4,20},{5,21},{6,3},{7,2},{8,24},{9,25},... | collective-permute-start | bytes 98312 | tf_op jit(solution)/shard_map/ppermute | solution.py:221
  21.6 1.1 %collective-permute-start.11 = (bf16[1,128,128]{2,1,0:T(8,128)(2,1)S(1)}, bf16[1,128,128]{2,1,0:T(8,128)(2,1)S(1)}, u32[]{:S(2)}, u32[]{:S(2)}) collective-permute-start(bf16[1,128,128]{2,1,0:T(8,128)(2,1)S(1)} %bitcast.10), channel_id=1, source_target_pairs={{0,24},{1,25},{2,6},{3,7},{4,28},{5,29},{6,2},{7,3},{8,16},{9,17},... | collective-permute-start | bytes 98312 | tf_op jit(solution)/shard_map/ppermute | solution.py:221
  22.7 1.2 %collective-permute-start.12 = (bf16[1,128,128]{2,1,0:T(8,128)(2,1)S(1)}, bf16[1,128,128]{2,1,0:T(8,128)(2,1)S(1)}, u32[]{:S(2)}, u32[]{:S(2)}) collective-permute-start(bf16[1,128,128]{2,1,0:T(8,128)(2,1)S(1)} %bitcast.11), channel_id=1, source_target_pairs={{0,8},{1,9},{2,3},{3,2},{4,12},{5,13},{6,7},{7,6},{8,0},{9,1},{10,... | collective-permute-start | bytes 98312 | tf_op jit(solution)/shard_map/ppermute | solution.py:221
  23.9 1.3 %collective-permute-done.10 = bf16[1,128,128]{2,1,0:T(8,128)(2,1)S(1)} collective-permute-done((bf16[1,128,128]{2,1,0:T(8,128)(2,1)S(1)}, bf16[1,128,128]{2,1,0:T(8,128)(2,1)S(1)}, u32[]{:S(2)}, u32[]{:S(2)}) %collective-permute-start.10) | collective-permute-done | bytes 32800 | tf_op jit(solution)/shard_map/ppermute | solution.py:221
  25.2 2.1 %collective-permute-done.11 = bf16[1,128,128]{2,1,0:T(8,128)(2,1)S(1)} collective-permute-done((bf16[1,128,128]{2,1,0:T(8,128)(2,1)S(1)}, bf16[1,128,128]{2,1,0:T(8,128)(2,1)S(1)}, u32[]{:S(2)}, u32[]{:S(2)}) %collective-permute-start.11) | collective-permute-done | bytes 32800 | tf_op jit(solution)/shard_map/ppermute | solution.py:221
  27.4 2.0 %collective-permute-start.13 = (bf16[4,128,128]{2,1,0:T(8,128)(2,1)S(1)}, bf16[4,128,128]{2,1,0:T(8,128)(2,1)S(1)}, u32[]{:S(2)}, u32[]{:S(2)}) collective-permute-start(bf16[4,128,128]{2,1,0:T(8,128)(2,1)S(1)} %pad_maximum_fusion.1.refs_0_), channel_id=1, source_target_pairs={{0,5},{1,4},{2,26},{3,27},{4,1},{5,0},{6,30},{7,31},{8,13},{9,12},... | collective-permute-start | bytes 393224 | tf_op jit(solution)/shard_map/ppermute | solution.py:221
  29.3 0.7 %collective-permute-start.14 = (bf16[4,128,128]{2,1,0:T(8,128)(2,1)S(1)}, bf16[4,128,128]{2,1,0:T(8,128)(2,1)S(1)}, u32[]{:S(2)}, u32[]{:S(2)}) collective-permute-start(bf16[4,128,128]{2,1,0:T(8,128)(2,1)S(1)} %pad_maximum_fusion.1.refs_0_), channel_id=1, source_target_pairs={{0,4},{1,5},{2,18},{3,19},{4,0},{5,1},{6,22},{7,23},{8,12},{9,13},... | collective-permute-start | bytes 393224 | tf_op jit(solution)/shard_map/ppermute | solution.py:221
  30.1 0.9 %collective-permute-start.15 = (bf16[4,128,128]{2,1,0:T(8,128)(2,1)S(1)}, bf16[4,128,128]{2,1,0:T(8,128)(2,1)S(1)}, u32[]{:S(2)}, u32[]{:S(2)}) collective-permute-start(bf16[4,128,128]{2,1,0:T(8,128)(2,1)S(1)} %pad_maximum_fusion.1.refs_0_), channel_id=1, source_target_pairs={{0,1},{1,0},{2,10},{3,11},{4,5},{5,4},{6,14},{7,15},{8,9},{9,8},{1... | collective-permute-start | bytes 393224 | tf_op jit(solution)/shard_map/ppermute | solution.py:221
  30.9 2.4 %collective-permute-done.13.refs_1_ = bf16[4,128,128]{2,1,0:T(8,128)(2,1)S(1)} collective-permute-done((bf16[4,128,128]{2,1,0:T(8,128)(2,1)S(1)}, bf16[4,128,128]{2,1,0:T(8,128)(2,1)S(1)}, u32[]{:S(2)}, u32[]{:S(2)}) %collective-permute-start.13) | collective-permute-done | bytes 131104 | tf_op jit(solution)/shard_map/ppermute | solution.py:221
  33.3 1.1 %collective-permute-done.14.refs_2_ = bf16[4,128,128]{2,1,0:T(8,128)(2,1)S(1)} collective-permute-done((bf16[4,128,128]{2,1,0:T(8,128)(2,1)S(1)}, bf16[4,128,128]{2,1,0:T(8,128)(2,1)S(1)}, u32[]{:S(2)}, u32[]{:S(2)}) %collective-permute-start.14) | collective-permute-done | bytes 131104 | tf_op jit(solution)/shard_map/ppermute | solution.py:221
  34.4 0.6 %collective-permute-done.15.refs_3_ = bf16[4,128,128]{2,1,0:T(8,128)(2,1)S(1)} collective-permute-done((bf16[4,128,128]{2,1,0:T(8,128)(2,1)S(1)}, bf16[4,128,128]{2,1,0:T(8,128)(2,1)S(1)}, u32[]{:S(2)}, u32[]{:S(2)}) %collective-permute-start.15) | collective-permute-done | bytes 131104 | tf_op jit(solution)/shard_map/ppermute | solution.py:221
  35.7 0.6 %collective-permute-done.19.refs_2_ = bf16[4,128,128]{2,1,0:T(8,128)(2,1)S(1)} collective-permute-done((bf16[4,128,128]{2,1,0:T(8,128)(2,1)S(1)}, bf16[4,128,128]{2,1,0:T(8,128)(2,1)S(1)}, u32[]{:S(2)}, u32[]{:S(2)}) %collective-permute-start.19) | collective-permute-done | bytes 131104 | tf_op jit(solution)/shard_map/ppermute | solution.py:221
  36.8 1.0 %collective-permute-start.20 = (bf16[1,128,128]{2,1,0:T(8,128)(2,1)S(1)}, bf16[1,128,128]{2,1,0:T(8,128)(2,1)S(1)}, u32[]{:S(2)}, u32[]{:S(2)}) collective-permute-start(bf16[1,128,128]{2,1,0:T(8,128)(2,1)S(1)} %bitcast.5), channel_id=1, source_target_pairs={{0,16},{1,17},{2,7},{3,6},{4,20},{5,21},{6,3},{7,2},{8,24},{9,25},... | collective-permute-start | bytes 98312 | tf_op jit(solution)/shard_map/ppermute | solution.py:221
  37.8 1.9 %collective-permute-start.21 = (bf16[1,128,128]{2,1,0:T(8,128)(2,1)S(1)}, bf16[1,128,128]{2,1,0:T(8,128)(2,1)S(1)}, u32[]{:S(2)}, u32[]{:S(2)}) collective-permute-start(bf16[1,128,128]{2,1,0:T(8,128)(2,1)S(1)} %bitcast.6), channel_id=1, source_target_pairs={{0,24},{1,25},{2,6},{3,7},{4,28},{5,29},{6,2},{7,3},{8,16},{9,17},... | collective-permute-start | bytes 98312 | tf_op jit(solution)/shard_map/ppermute | solution.py:221
  39.7 0.7 %collective-permute-start.22 = (bf16[1,128,128]{2,1,0:T(8,128)(2,1)S(1)}, bf16[1,128,128]{2,1,0:T(8,128)(2,1)S(1)}, u32[]{:S(2)}, u32[]{:S(2)}) collective-permute-start(bf16[1,128,128]{2,1,0:T(8,128)(2,1)S(1)} %bitcast.7), channel_id=1, source_target_pairs={{0,8},{1,9},{2,3},{3,2},{4,12},{5,13},{6,7},{7,6},{8,0},{9,1},{10,... | collective-permute-start | bytes 98312 | tf_op jit(solution)/shard_map/ppermute | solution.py:221
  40.4 1.6 %collective-permute-done.20 = bf16[1,128,128]{2,1,0:T(8,128)(2,1)S(1)} collective-permute-done((bf16[1,128,128]{2,1,0:T(8,128)(2,1)S(1)}, bf16[1,128,128]{2,1,0:T(8,128)(2,1)S(1)}, u32[]{:S(2)}, u32[]{:S(2)}) %collective-permute-start.20) | collective-permute-done | bytes 32800 | tf_op jit(solution)/shard_map/ppermute | solution.py:221
  41.9 1.6 %collective-permute-done.21 = bf16[1,128,128]{2,1,0:T(8,128)(2,1)S(1)} collective-permute-done((bf16[1,128,128]{2,1,0:T(8,128)(2,1)S(1)}, bf16[1,128,128]{2,1,0:T(8,128)(2,1)S(1)}, u32[]{:S(2)}, u32[]{:S(2)}) %collective-permute-start.21) | collective-permute-done | bytes 32800 | tf_op jit(solution)/shard_map/ppermute | solution.py:221
  43.9 2.0 %collective-permute-start.23 = (bf16[4,128,128]{2,1,0:T(8,128)(2,1)S(1)}, bf16[4,128,128]{2,1,0:T(8,128)(2,1)S(1)}, u32[]{:S(2)}, u32[]{:S(2)}) collective-permute-start(bf16[4,128,128]{2,1,0:T(8,128)(2,1)S(1)} %pad_maximum_fusion.2.refs_0_), channel_id=1, source_target_pairs={{0,5},{1,4},{2,26},{3,27},{4,1},{5,0},{6,30},{7,31},{8,13},{9,12},... | collective-permute-start | bytes 393224 | tf_op jit(solution)/shard_map/ppermute | solution.py:221
  45.9 0.5 collective-permute-start.24
  46.4 1.0 %collective-permute-start.25 = (bf16[4,128,128]{2,1,0:T(8,128)(2,1)S(1)}, bf16[4,128,128]{2,1,0:T(8,128)(2,1)S(1)}, u32[]{:S(2)}, u32[]{:S(2)}) collective-permute-start(bf16[4,128,128]{2,1,0:T(8,128)(2,1)S(1)} %pad_maximum_fusion.2.refs_0_), channel_id=1, source_target_pairs={{0,1},{1,0},{2,10},{3,11},{4,5},{5,4},{6,14},{7,15},{8,9},{9,8},{1... | collective-permute-start | bytes 393224 | tf_op jit(solution)/shard_map/ppermute | solution.py:221
  47.4 2.4 %collective-permute-done.23.refs_1_ = bf16[4,128,128]{2,1,0:T(8,128)(2,1)S(1)} collective-permute-done((bf16[4,128,128]{2,1,0:T(8,128)(2,1)S(1)}, bf16[4,128,128]{2,1,0:T(8,128)(2,1)S(1)}, u32[]{:S(2)}, u32[]{:S(2)}) %collective-permute-start.23) | collective-permute-done | bytes 131104 | tf_op jit(solution)/shard_map/ppermute | solution.py:221
  49.8 1.0 %collective-permute-done.24.refs_2_ = bf16[4,128,128]{2,1,0:T(8,128)(2,1)S(1)} collective-permute-done((bf16[4,128,128]{2,1,0:T(8,128)(2,1)S(1)}, bf16[4,128,128]{2,1,0:T(8,128)(2,1)S(1)}, u32[]{:S(2)}, u32[]{:S(2)}) %collective-permute-start.24) | collective-permute-done | bytes 131104 | tf_op jit(solution)/shard_map/ppermute | solution.py:221
  52.2 0.5 collective-permute-done.29.refs_2_
  52.7 1.1 %last.5 = bf16[128,128]{1,0:T(8,128)(2,1)} custom-call(bf16[32,256,128]{2,1,0:T(8,128)(2,1)S(1)} %get-tuple-element.27.adj_ref, f32[128,128]{1,0:T(8,128)S(1)} %partial.5.partial_ref, bf16[128,128]{1,0:T(8,128)(2,1)S(1)} %last.4.own_ref, f32[3,128]{1,0:T(4,128)S(1)} %copy-done, bf16[4,128,128]{2,1,0:T(8,128)(2,1)S(1)} %collective-permute-done.27.refs_0_, ...), custom_call_target="tpu_custom_call" | custom-call | tf_op jit(solution)/shard_map/last/pallas_call | solution.py:212
  (41 shorter events, 6.7 us)
Async XLA Ops:
  0.0 8.1 %collective-permute-start = (bf16[1,128,128]{2,1,0:T(8,128)(2,1)}, bf16[1,128,128]{2,1,0:T(8,128)(2,1)S(1)}, u32[]{:S(2)}, u32[]{:S(2)}) collective-permute-start(bf16[1,128,128]{2,1,0:T(8,128)(2,1)} %bitcast.16), channel_id=1, source_target_pairs={{0,16},{1,17},{2,7},{3,6},{4,20},{5,21},{6,3},{7,2},{8,24},{9,25},... | collective-permute-start | bytes 98312 | tf_op jit(solution)/shard_map/ppermute | solution.py:221
  4.1 5.9 %collective-permute-start.1 = (bf16[1,128,128]{2,1,0:T(8,128)(2,1)}, bf16[1,128,128]{2,1,0:T(8,128)(2,1)S(1)}, u32[]{:S(2)}, u32[]{:S(2)}) collective-permute-start(bf16[1,128,128]{2,1,0:T(8,128)(2,1)} %bitcast.17), channel_id=1, source_target_pairs={{0,24},{1,25},{2,6},{3,7},{4,28},{5,29},{6,2},{7,3},{8,16},{9,17},... | collective-permute-start | bytes 98312 | tf_op jit(solution)/shard_map/ppermute | solution.py:221
  5.4 4.6 %collective-permute-start.2 = (bf16[1,128,128]{2,1,0:T(8,128)(2,1)}, bf16[1,128,128]{2,1,0:T(8,128)(2,1)S(1)}, u32[]{:S(2)}, u32[]{:S(2)}) collective-permute-start(bf16[1,128,128]{2,1,0:T(8,128)(2,1)} %bitcast.18), channel_id=1, source_target_pairs={{0,8},{1,9},{2,3},{3,2},{4,12},{5,13},{6,7},{7,6},{8,0},{9,1},{10,... | collective-permute-start | bytes 98312 | tf_op jit(solution)/shard_map/ppermute | solution.py:221
  10.0 5.9 %collective-permute-start.3 = (bf16[4,128,128]{2,1,0:T(8,128)(2,1)S(1)}, bf16[4,128,128]{2,1,0:T(8,128)(2,1)S(1)}, u32[]{:S(2)}, u32[]{:S(2)}) collective-permute-start(bf16[4,128,128]{2,1,0:T(8,128)(2,1)S(1)} %pad_maximum_fusion.refs_0_), channel_id=1, source_target_pairs={{0,5},{1,4},{2,26},{3,27},{4,1},{5,0},{6,30},{7,31},{8,13},{9,12},... | collective-permute-start | bytes 393224 | tf_op jit(solution)/shard_map/ppermute | solution.py:221
  12.5 5.0 %collective-permute-start.4 = (bf16[4,128,128]{2,1,0:T(8,128)(2,1)S(1)}, bf16[4,128,128]{2,1,0:T(8,128)(2,1)S(1)}, u32[]{:S(2)}, u32[]{:S(2)}) collective-permute-start(bf16[4,128,128]{2,1,0:T(8,128)(2,1)S(1)} %pad_maximum_fusion.refs_0_), channel_id=1, source_target_pairs={{0,4},{1,5},{2,18},{3,19},{4,0},{5,1},{6,22},{7,23},{8,12},{9,13},... | collective-permute-start | bytes 393224 | tf_op jit(solution)/shard_map/ppermute | solution.py:221
  13.1 5.0 %collective-permute-start.5 = (bf16[4,128,128]{2,1,0:T(8,128)(2,1)S(1)}, bf16[4,128,128]{2,1,0:T(8,128)(2,1)S(1)}, u32[]{:S(2)}, u32[]{:S(2)}) collective-permute-start(bf16[4,128,128]{2,1,0:T(8,128)(2,1)S(1)} %pad_maximum_fusion.refs_0_), channel_id=1, source_target_pairs={{0,1},{1,0},{2,10},{3,11},{4,5},{5,4},{6,14},{7,15},{8,9},{9,8},{1... | collective-permute-start | bytes 393224 | tf_op jit(solution)/shard_map/ppermute | solution.py:221
  13.6 5.0 %collective-permute-start.6 = (bf16[4,128,128]{2,1,0:T(8,128)(2,1)S(1)}, bf16[4,128,128]{2,1,0:T(8,128)(2,1)S(1)}, u32[]{:S(2)}, u32[]{:S(2)}) collective-permute-start(bf16[4,128,128]{2,1,0:T(8,128)(2,1)S(1)} %pad_maximum_fusion.refs_0_), channel_id=1, source_target_pairs={{0,2},{1,3},{2,0},{3,1},{4,6},{5,7},{6,4},{7,5},{8,10},{9,11},{10,... | collective-permute-start | bytes 393224 | tf_op jit(solution)/shard_map/ppermute | solution.py:221
  15.7 4.2 %copy-start = (f32[3,128]{1,0:T(4,128)S(1)}, f32[3,128]{1,0:T(4,128)}, u32[]{:S(2)}) copy-start(f32[3,128]{1,0:T(4,128)} %gain_ref.5) | copy-start | bytes 4612
  18.0 1.3 %collective-permute-start.7 = (bf16[4,128,128]{2,1,0:T(8,128)(2,1)S(1)}, bf16[4,128,128]{2,1,0:T(8,128)(2,1)S(1)}, u32[]{:S(2)}, u32[]{:S(2)}) collective-permute-start(bf16[4,128,128]{2,1,0:T(8,128)(2,1)S(1)} %collective-permute-done.3.refs_1_), channel_id=1, source_target_pairs={{0,2},{1,3},{2,0},{3,1},{4,6},{5,7},{6,4},{7,5},{8,10},{9,11},{10,... | collective-permute-start | bytes 393224 | tf_op jit(solution)/shard_map/ppermute | solution.py:221
  18.0 1.5 %collective-permute-start.8 = (bf16[4,128,128]{2,1,0:T(8,128)(2,1)S(1)}, bf16[4,128,128]{2,1,0:T(8,128)(2,1)S(1)}, u32[]{:S(2)}, u32[]{:S(2)}) collective-permute-start(bf16[4,128,128]{2,1,0:T(8,128)(2,1)S(1)} %collective-permute-done.4.refs_2_), channel_id=1, source_target_pairs={{0,2},{1,3},{2,0},{3,1},{4,6},{5,7},{6,4},{7,5},{8,10},{9,11},{10,... | collective-permute-start | bytes 393224 | tf_op jit(solution)/shard_map/ppermute | solution.py:221
  18.5 1.3 %collective-permute-start.9 = (bf16[4,128,128]{2,1,0:T(8,128)(2,1)S(1)}, bf16[4,128,128]{2,1,0:T(8,128)(2,1)S(1)}, u32[]{:S(2)}, u32[]{:S(2)}) collective-permute-start(bf16[4,128,128]{2,1,0:T(8,128)(2,1)S(1)} %collective-permute-done.5.refs_3_), channel_id=1, source_target_pairs={{0,2},{1,3},{2,0},{3,1},{4,6},{5,7},{6,4},{7,5},{8,10},{9,11},{10,... | collective-permute-start | bytes 393224 | tf_op jit(solution)/shard_map/ppermute | solution.py:221
  20.3 4.9 %collective-permute-start.10 = (bf16[1,128,128]{2,1,0:T(8,128)(2,1)S(1)}, bf16[1,128,128]{2,1,0:T(8,128)(2,1)S(1)}, u32[]{:S(2)}, u32[]{:S(2)}) collective-permute-start(bf16[1,128,128]{2,1,0:T(8,128)(2,1)S(1)} %bitcast.9), channel_id=1, source_target_pairs={{0,16},{1,17},{2,7},{3,6},{4,20},{5,21},{6,3},{7,2},{8,24},{9,25},... | collective-permute-start | bytes 98312 | tf_op jit(solution)/shard_map/ppermute | solution.py:221
  21.6 5.7 %collective-permute-start.11 = (bf16[1,128,128]{2,1,0:T(8,128)(2,1)S(1)}, bf16[1,128,128]{2,1,0:T(8,128)(2,1)S(1)}, u32[]{:S(2)}, u32[]{:S(2)}) collective-permute-start(bf16[1,128,128]{2,1,0:T(8,128)(2,1)S(1)} %bitcast.10), channel_id=1, source_target_pairs={{0,24},{1,25},{2,6},{3,7},{4,28},{5,29},{6,2},{7,3},{8,16},{9,17},... | collective-permute-start | bytes 98312 | tf_op jit(solution)/shard_map/ppermute | solution.py:221
  22.7 4.6 %collective-permute-start.12 = (bf16[1,128,128]{2,1,0:T(8,128)(2,1)S(1)}, bf16[1,128,128]{2,1,0:T(8,128)(2,1)S(1)}, u32[]{:S(2)}, u32[]{:S(2)}) collective-permute-start(bf16[1,128,128]{2,1,0:T(8,128)(2,1)S(1)} %bitcast.11), channel_id=1, source_target_pairs={{0,8},{1,9},{2,3},{3,2},{4,12},{5,13},{6,7},{7,6},{8,0},{9,1},{10,... | collective-permute-start | bytes 98312 | tf_op jit(solution)/shard_map/ppermute | solution.py:221
  27.4 5.9 %collective-permute-start.13 = (bf16[4,128,128]{2,1,0:T(8,128)(2,1)S(1)}, bf16[4,128,128]{2,1,0:T(8,128)(2,1)S(1)}, u32[]{:S(2)}, u32[]{:S(2)}) collective-permute-start(bf16[4,128,128]{2,1,0:T(8,128)(2,1)S(1)} %pad_maximum_fusion.1.refs_0_), channel_id=1, source_target_pairs={{0,5},{1,4},{2,26},{3,27},{4,1},{5,0},{6,30},{7,31},{8,13},{9,12},... | collective-permute-start | bytes 393224 | tf_op jit(solution)/shard_map/ppermute | solution.py:221
  29.3 5.1 %collective-permute-start.14 = (bf16[4,128,128]{2,1,0:T(8,128)(2,1)S(1)}, bf16[4,128,128]{2,1,0:T(8,128)(2,1)S(1)}, u32[]{:S(2)}, u32[]{:S(2)}) collective-permute-start(bf16[4,128,128]{2,1,0:T(8,128)(2,1)S(1)} %pad_maximum_fusion.1.refs_0_), channel_id=1, source_target_pairs={{0,4},{1,5},{2,18},{3,19},{4,0},{5,1},{6,22},{7,23},{8,12},{9,13},... | collective-permute-start | bytes 393224 | tf_op jit(solution)/shard_map/ppermute | solution.py:221
  30.1 5.0 %collective-permute-start.15 = (bf16[4,128,128]{2,1,0:T(8,128)(2,1)S(1)}, bf16[4,128,128]{2,1,0:T(8,128)(2,1)S(1)}, u32[]{:S(2)}, u32[]{:S(2)}) collective-permute-start(bf16[4,128,128]{2,1,0:T(8,128)(2,1)S(1)} %pad_maximum_fusion.1.refs_0_), channel_id=1, source_target_pairs={{0,1},{1,0},{2,10},{3,11},{4,5},{5,4},{6,14},{7,15},{8,9},{9,8},{1... | collective-permute-start | bytes 393224 | tf_op jit(solution)/shard_map/ppermute | solution.py:221
  30.9 4.1 %collective-permute-start.16 = (bf16[4,128,128]{2,1,0:T(8,128)(2,1)S(1)}, bf16[4,128,128]{2,1,0:T(8,128)(2,1)S(1)}, u32[]{:S(2)}, u32[]{:S(2)}) collective-permute-start(bf16[4,128,128]{2,1,0:T(8,128)(2,1)S(1)} %pad_maximum_fusion.1.refs_0_), channel_id=1, source_target_pairs={{0,2},{1,3},{2,0},{3,1},{4,6},{5,7},{6,4},{7,5},{8,10},{9,11},{10,... | collective-permute-start | bytes 393224 | tf_op jit(solution)/shard_map/ppermute | solution.py:221
  33.3 2.2 %collective-permute-start.17 = (bf16[4,128,128]{2,1,0:T(8,128)(2,1)S(1)}, bf16[4,128,128]{2,1,0:T(8,128)(2,1)S(1)}, u32[]{:S(2)}, u32[]{:S(2)}) collective-permute-start(bf16[4,128,128]{2,1,0:T(8,128)(2,1)S(1)} %collective-permute-done.13.refs_1_), channel_id=1, source_target_pairs={{0,2},{1,3},{2,0},{3,1},{4,6},{5,7},{6,4},{7,5},{8,10},{9,11},{10,... | collective-permute-start | bytes 393224 | tf_op jit(solution)/shard_map/ppermute | solution.py:221
  34.4 1.3 %collective-permute-start.18 = (bf16[4,128,128]{2,1,0:T(8,128)(2,1)S(1)}, bf16[4,128,128]{2,1,0:T(8,128)(2,1)S(1)}, u32[]{:S(2)}, u32[]{:S(2)}) collective-permute-start(bf16[4,128,128]{2,1,0:T(8,128)(2,1)S(1)} %collective-permute-done.14.refs_2_), channel_id=1, source_target_pairs={{0,2},{1,3},{2,0},{3,1},{4,6},{5,7},{6,4},{7,5},{8,10},{9,11},{10,... | collective-permute-start | bytes 393224 | tf_op jit(solution)/shard_map/ppermute | solution.py:221
  35.0 1.3 %collective-permute-start.19 = (bf16[4,128,128]{2,1,0:T(8,128)(2,1)S(1)}, bf16[4,128,128]{2,1,0:T(8,128)(2,1)S(1)}, u32[]{:S(2)}, u32[]{:S(2)}) collective-permute-start(bf16[4,128,128]{2,1,0:T(8,128)(2,1)S(1)} %collective-permute-done.15.refs_3_), channel_id=1, source_target_pairs={{0,2},{1,3},{2,0},{3,1},{4,6},{5,7},{6,4},{7,5},{8,10},{9,11},{10,... | collective-permute-start | bytes 393224 | tf_op jit(solution)/shard_map/ppermute | solution.py:221
  36.8 5.1 %collective-permute-start.20 = (bf16[1,128,128]{2,1,0:T(8,128)(2,1)S(1)}, bf16[1,128,128]{2,1,0:T(8,128)(2,1)S(1)}, u32[]{:S(2)}, u32[]{:S(2)}) collective-permute-start(bf16[1,128,128]{2,1,0:T(8,128)(2,1)S(1)} %bitcast.5), channel_id=1, source_target_pairs={{0,16},{1,17},{2,7},{3,6},{4,20},{5,21},{6,3},{7,2},{8,24},{9,25},... | collective-permute-start | bytes 98312 | tf_op jit(solution)/shard_map/ppermute | solution.py:221
  37.8 5.7 %collective-permute-start.21 = (bf16[1,128,128]{2,1,0:T(8,128)(2,1)S(1)}, bf16[1,128,128]{2,1,0:T(8,128)(2,1)S(1)}, u32[]{:S(2)}, u32[]{:S(2)}) collective-permute-start(bf16[1,128,128]{2,1,0:T(8,128)(2,1)S(1)} %bitcast.6), channel_id=1, source_target_pairs={{0,24},{1,25},{2,6},{3,7},{4,28},{5,29},{6,2},{7,3},{8,16},{9,17},... | collective-permute-start | bytes 98312 | tf_op jit(solution)/shard_map/ppermute | solution.py:221
  39.7 4.2 %collective-permute-start.22 = (bf16[1,128,128]{2,1,0:T(8,128)(2,1)S(1)}, bf16[1,128,128]{2,1,0:T(8,128)(2,1)S(1)}, u32[]{:S(2)}, u32[]{:S(2)}) collective-permute-start(bf16[1,128,128]{2,1,0:T(8,128)(2,1)S(1)} %bitcast.7), channel_id=1, source_target_pairs={{0,8},{1,9},{2,3},{3,2},{4,12},{5,13},{6,7},{7,6},{8,0},{9,1},{10,... | collective-permute-start | bytes 98312 | tf_op jit(solution)/shard_map/ppermute | solution.py:221
  43.9 5.9 %collective-permute-start.23 = (bf16[4,128,128]{2,1,0:T(8,128)(2,1)S(1)}, bf16[4,128,128]{2,1,0:T(8,128)(2,1)S(1)}, u32[]{:S(2)}, u32[]{:S(2)}) collective-permute-start(bf16[4,128,128]{2,1,0:T(8,128)(2,1)S(1)} %pad_maximum_fusion.2.refs_0_), channel_id=1, source_target_pairs={{0,5},{1,4},{2,26},{3,27},{4,1},{5,0},{6,30},{7,31},{8,13},{9,12},... | collective-permute-start | bytes 393224 | tf_op jit(solution)/shard_map/ppermute | solution.py:221
  45.9 5.0 %collective-permute-start.24 = (bf16[4,128,128]{2,1,0:T(8,128)(2,1)S(1)}, bf16[4,128,128]{2,1,0:T(8,128)(2,1)S(1)}, u32[]{:S(2)}, u32[]{:S(2)}) collective-permute-start(bf16[4,128,128]{2,1,0:T(8,128)(2,1)S(1)} %pad_maximum_fusion.2.refs_0_), channel_id=1, source_target_pairs={{0,4},{1,5},{2,18},{3,19},{4,0},{5,1},{6,22},{7,23},{8,12},{9,13},... | collective-permute-start | bytes 393224 | tf_op jit(solution)/shard_map/ppermute | solution.py:221
  46.4 5.0 %collective-permute-start.25 = (bf16[4,128,128]{2,1,0:T(8,128)(2,1)S(1)}, bf16[4,128,128]{2,1,0:T(8,128)(2,1)S(1)}, u32[]{:S(2)}, u32[]{:S(2)}) collective-permute-start(bf16[4,128,128]{2,1,0:T(8,128)(2,1)S(1)} %pad_maximum_fusion.2.refs_0_), channel_id=1, source_target_pairs={{0,1},{1,0},{2,10},{3,11},{4,5},{5,4},{6,14},{7,15},{8,9},{9,8},{1... | collective-permute-start | bytes 393224 | tf_op jit(solution)/shard_map/ppermute | solution.py:221
  47.4 3.9 %collective-permute-start.26 = (bf16[4,128,128]{2,1,0:T(8,128)(2,1)S(1)}, bf16[4,128,128]{2,1,0:T(8,128)(2,1)S(1)}, u32[]{:S(2)}, u32[]{:S(2)}) collective-permute-start(bf16[4,128,128]{2,1,0:T(8,128)(2,1)S(1)} %pad_maximum_fusion.2.refs_0_), channel_id=1, source_target_pairs={{0,2},{1,3},{2,0},{3,1},{4,6},{5,7},{6,4},{7,5},{8,10},{9,11},{10,... | collective-permute-start | bytes 393224 | tf_op jit(solution)/shard_map/ppermute | solution.py:221
  49.8 2.1 %collective-permute-start.27 = (bf16[4,128,128]{2,1,0:T(8,128)(2,1)S(1)}, bf16[4,128,128]{2,1,0:T(8,128)(2,1)S(1)}, u32[]{:S(2)}, u32[]{:S(2)}) collective-permute-start(bf16[4,128,128]{2,1,0:T(8,128)(2,1)S(1)} %collective-permute-done.23.refs_1_), channel_id=1, source_target_pairs={{0,2},{1,3},{2,0},{3,1},{4,6},{5,7},{6,4},{7,5},{8,10},{9,11},{10,... | collective-permute-start | bytes 393224 | tf_op jit(solution)/shard_map/ppermute | solution.py:221
  50.8 1.3 %collective-permute-start.28 = (bf16[4,128,128]{2,1,0:T(8,128)(2,1)S(1)}, bf16[4,128,128]{2,1,0:T(8,128)(2,1)S(1)}, u32[]{:S(2)}, u32[]{:S(2)}) collective-permute-start(bf16[4,128,128]{2,1,0:T(8,128)(2,1)S(1)} %collective-permute-done.24.refs_2_), channel_id=1, source_target_pairs={{0,2},{1,3},{2,0},{3,1},{4,6},{5,7},{6,4},{7,5},{8,10},{9,11},{10,... | collective-permute-start | bytes 393224 | tf_op jit(solution)/shard_map/ppermute | solution.py:221
  51.4 1.3 %collective-permute-start.29 = (bf16[4,128,128]{2,1,0:T(8,128)(2,1)S(1)}, bf16[4,128,128]{2,1,0:T(8,128)(2,1)S(1)}, u32[]{:S(2)}, u32[]{:S(2)}) collective-permute-start(bf16[4,128,128]{2,1,0:T(8,128)(2,1)S(1)} %collective-permute-done.25.refs_3_), channel_id=1, source_target_pairs={{0,2},{1,3},{2,0},{3,1},{4,6},{5,7},{6,4},{7,5},{8,10},{9,11},{10,... | collective-permute-start | bytes 393224 | tf_op jit(solution)/shard_map/ppermute | solution.py:221
